TPU v7x, 32 devices: a whole 2x2x4 slice. The times are simulated.
32 devices in a mesh: frames: 8 (over z, x), rows: 4 (over y, core).
Axes of the slice: x: 2, y: 2, z: 4, core: 2. Of those that a mesh axis runs over, the one named last changes fastest.
Arguments:
- video: bfloat16 [8, 32, 160, 512], P('frames', 'rows'), may hold values from -6 to 6
- norm1_gain: float32 [512], replicated, may hold values from 0.25 to 1.75
- norm1_shift: float32 [512], replicated, may hold values from -1.75 to 1.75
- conv1_weight: bfloat16 [3, 3, 512, 512], replicated, may hold values from -0.09375 to 0.09375
- conv1_bias: float32 [512], replicated, may hold values from -1.75 to 1.75
- norm2_gain: float32 [512], replicated, may hold values from 0.25 to 1.75
- norm2_shift: float32 [512], replicated, may hold values from -1.75 to 1.75
- conv2_weight: bfloat16 [3, 3, 512, 512], replicated, may hold values from -0.09375 to 0.09375
- conv2_bias: float32 [512], replicated, may hold values from -1.75 to 1.75
- out_gain: float32 [512], replicated, may hold values from 0.25 to 1.75
- out_shift: float32 [512], replicated, may hold values from -1.75 to 1.75
- out_weight: bfloat16 [3, 3, 512, 8], replicated, may hold values from -0.09375 to 0.09375
- out_bias: float32 [8], replicated, may hold values from -1.75 to 1.75
- quant_weight: float32 [8, 4], replicated, may hold values from -2 to 2
- quant_bias: float32 [4], replicated, may hold values from -1.75 to 1.75
- time_in_weight: bfloat16 [3, 3, 3, 4, 128], replicated, may hold values from -0.625 to 0.625
- time_in_bias: float32 [128], replicated, may hold values from -1.75 to 1.75
- tnorm1_gain: float32 [128], replicated, may hold values from 0.25 to 1.75
- tnorm1_shift: float32 [128], replicated, may hold values from -1.75 to 1.75
- time1_weight: bfloat16 [3, 3, 3, 128, 128], replicated, may hold values from -0.109375 to 0.109375
- tnorm2_gain: float32 [128], replicated, may hold values from 0.25 to 1.75
- tnorm2_shift: float32 [128], replicated, may hold values from -1.75 to 1.75
- time2_weight: bfloat16 [3, 3, 3, 128, 128], replicated, may hold values from -0.109375 to 0.109375
- time2_bias: float32 [128], replicated, may hold values from -1.75 to 1.75
Outputs:
- features: bfloat16 [8, 32, 160, 128], P('frames', 'rows')
All inputs are finite; a program needn't handle non-finite values.
Results may differ from a plain program's by a relative error of at most 0.01.
Values may be sent and summed in bfloat16 or wider, within the bound.
No kernel may reach another device: no remote copies, remote signals or barrier semaphores. Data moves between devices by JAX's collectives and lax.ppermute only.
A program may use at most 64 MiB of HBM per device.

v0:
```python
import functools

import jax
import jax.numpy as jnp
from jax import lax
from jax.experimental import pallas as pl
from jax.experimental.pallas import tpu as pltpu
from jax.sharding import PartitionSpec as P

GROUPS = 32
EPS = 1e-06
LATENT_SCALE = 0.13025
LANES = 128
F32 = jnp.float32
BF16 = jnp.bfloat16

ANY = pl.BlockSpec(memory_space=pl.ANY)
VMEM = pl.BlockSpec(memory_space=pltpu.VMEM)
SMEM = pl.BlockSpec(memory_space=pltpu.SMEM)


def params(mib=48):
    return pltpu.CompilerParams(vmem_limit_bytes=mib * 1024 * 1024)


def lane_groups(values, size):
    lane = lax.broadcasted_iota(jnp.int32, values.shape, 1)
    step = 1
    while step < size:
        up = pltpu.roll(values, step, 1)
        down = pltpu.roll(values, LANES - step, 1)
        values = values + jnp.where((lane & step) != 0, up, down)
        step *= 2
    return values


def half_affine(parts, rows, gain, shift, count, per_group):
    total = parts[0][...]
    for part in parts[1:]:
        total = total + part[...]
    total = lane_groups(total, per_group) / count
    mean = total[0:rows]
    variance = total[rows : 2 * rows] - mean * mean
    scale = lax.rsqrt(variance + EPS) * gain
    return 0.5 * scale, 0.5 * (shift - mean * scale)


def as_row(block):
    return jnp.concatenate([block[k : k + 1, :] for k in range(block.shape[0])], axis=1)


def half_silu(values, scale, shift):
    t = values * scale + shift
    return t * jnp.tanh(t) + t


def put_sums(out_ref, first, second, rows):
    for k in range(rows):
        lanes = slice(k * LANES, (k + 1) * LANES)
        out_ref[k : k + 1, :] = first[:, lanes]
        out_ref[rows + k : rows + k + 1, :] = second[:, lanes]


def spread_columns(slots, row, at, even, odd, channels):
    half, width = even.shape
    index = lax.broadcasted_iota(jnp.int32, (half, width), 0)
    before = jnp.where(index == 0, 0.0, pltpu.roll(odd, 1, 0))
    after = jnp.where(index == half - 1, 0.0, pltpu.roll(even, half - 1, 0))
    for slot, piece in enumerate((before, even, odd, after)):
        slots[row, :, slot * channels + at : slot * channels + at + width] = piece.astype(BF16)


def input_sums_kernel(x_hbm, out_ref, xs, sems):
    lines = xs.shape[0]
    copies = [pltpu.make_async_copy(x_hbm.at[r], xs.at[r], sems.at[r]) for r in range(lines)]
    for copy in copies:
        copy.start()
    width, channels = xs.shape[1], xs.shape[2]
    first = [jnp.zeros((8, LANES), F32) for _ in range(channels // LANES)]
    second = list(first)
    for r in range(lines):
        copies[r].wait()

        def step(m, carry, r=r):
            first, second = carry
            first, second = list(first), list(second)
            at = pl.multiple_of(m * 32, 32)
            for k in range(channels // LANES):
                v = xs[r, pl.ds(at, 32), k * LANES : (k + 1) * LANES].astype(F32)
                v = v.reshape(4, 8, LANES)
                first[k] = first[k] + v.sum(0)
                second[k] = second[k] + (v * v).sum(0)
            return tuple(first), tuple(second)

        first, second = lax.fori_loop(0, width // 32, step, (tuple(first), tuple(second)))
    rows = channels // LANES
    for k in range(rows):
        out_ref[k : k + 1, :] = first[k].sum(0, keepdims=True)
        out_ref[rows + k : rows + k + 1, :] = second[k].sum(0, keepdims=True)


def input_sums(x):
    lines, width, channels = x.shape
    return pl.pallas_call(
        input_sums_kernel,
        out_shape=jax.ShapeDtypeStruct((2 * channels // LANES, LANES), F32),
        in_specs=[ANY],
        out_specs=VMEM,
        scratch_shapes=[pltpu.VMEM(x.shape, BF16), pltpu.SemaphoreType.DMA((lines,))],
        compiler_params=params(16),
        name="input_sums",
    )(x)


def conv_rows(slots, weights, bias_ref, out, sums, out_lines, own_at, own_lines, half, channels, residual):
    tile = 256
    n_tiles = channels // tile
    sums[...] = jnp.zeros_like(sums)

    def step(index, _):
        parity = index // n_tiles
        at = pl.multiple_of((index % n_tiles) * tile, tile)
        left = pl.multiple_of(parity * channels, channels)
        acc = None
        for i in range(3):
            lhs = slots[i : i + out_lines, :, pl.ds(left, 3 * channels)].reshape(out_lines * half, 3 * channels)
            part = jnp.dot(lhs, weights[i, :, pl.ds(at, tile)], preferred_element_type=F32)
            acc = part if acc is None else acc + part
        acc = acc.reshape(out_lines, half, tile) + bias_ref[:, pl.ds(at, tile)].reshape(1, 1, tile)
        if residual is not None:
            acc = acc + residual[:, parity, :, pl.ds(at, tile)].astype(F32)
        out[:, parity, :, pl.ds(at, tile)] = acc
        own = acc[own_at : own_at + own_lines].reshape(own_lines * half, tile)
        sums[0:1, pl.ds(at, tile)] += own.sum(0, keepdims=True)
        sums[1:2, pl.ds(at, tile)] += (own * own).sum(0, keepdims=True)
        return 0

    lax.fori_loop(0, 2 * n_tiles, step, 0)


def conv1_kernel(
    meta, s0, s1, s2, s3, gain, shift, bias, x_hbm, up_hbm, low_hbm, w_hbm,
    h_hbm, xp_ref, stats_ref,
    xs, rowf, slots, wv, hv, sums, sems, wsem, hsem,
    *, count, per_group, n_blocks,
):
    own = x_hbm.shape[0]
    halo = up_hbm.shape[0]
    lines, width, channels = xs.shape
    half = width // 2
    loads = [
        pltpu.make_async_copy(up_hbm, xs.at[pl.ds(0, halo)], sems.at[0]),
        pltpu.make_async_copy(x_hbm, xs.at[pl.ds(halo, own)], sems.at[1]),
        pltpu.make_async_copy(low_hbm, xs.at[pl.ds(halo + own, halo)], sems.at[2]),
    ]
    for copy in loads:
        copy.start()
    weight_load = pltpu.make_async_copy(w_hbm, wv, wsem)
    weight_load.start()
    scale, move = half_affine((s0, s1, s2, s3), channels // LANES, gain[...], shift[...], count, per_group)
    scale, move = as_row(scale), as_row(move)
    for copy in loads:
        copy.wait()
    first_line = meta[0] * own - halo

    def norm(r, _):
        line = first_line + r
        inside = (line >= 0) & (line < n_blocks * own)
        for at in range(0, channels, LANES):
            cols = slice(at, at + LANES)
            chunk = at // LANES
            rowf[chunk] = xs[r, :, cols].astype(F32)
            even = rowf[chunk, pl.ds(0, half, stride=2), :]
            odd = rowf[chunk, pl.ds(1, half, stride=2), :]
            xp_ref[r, 0, :, cols] = even.astype(BF16)
            xp_ref[r, 1, :, cols] = odd.astype(BF16)
            even = jnp.where(inside, half_silu(even, scale[:, cols], move[:, cols]), 0.0)
            odd = jnp.where(inside, half_silu(odd, scale[:, cols], move[:, cols]), 0.0)
            spread_columns(slots, r, at, even, odd, channels)
        return 0

    lax.fori_loop(0, lines, norm, 0)
    weight_load.wait()
    conv_rows(slots, wv, bias, hv, sums, lines - 2, halo - 1, own, half, channels, None)
    store = pltpu.make_async_copy(hv, h_hbm, hsem)
    store.start()
    put_sums(stats_ref, sums[0:1, :], sums[1:2, :], channels // LANES)
    store.wait()


def conv1(meta, stats, gain, shift, bias, x, up, low, weight, n_blocks):
    own, width, channels = x.shape
    halo = up.shape[0]
    lines = own + 2 * halo
    half = width // 2
    rows = channels // LANES
    count = float(n_blocks * own * width * (channels // GROUPS))
    return pl.pallas_call(
        functools.partial(conv1_kernel, count=count, per_group=channels // GROUPS, n_blocks=n_blocks),
        out_shape=(
            jax.ShapeDtypeStruct((lines - 2, 2, half, channels), F32),
            jax.ShapeDtypeStruct((lines, 2, half, channels), BF16),
            jax.ShapeDtypeStruct((2 * rows, LANES), F32),
        ),
        in_specs=[SMEM] + [VMEM] * 7 + [ANY] * 4,
        out_specs=(ANY, VMEM, VMEM),
        scratch_shapes=[
            pltpu.VMEM((lines, width, channels), BF16),
            pltpu.VMEM((channels // LANES, width, LANES), F32),
            pltpu.VMEM((lines, half, 4 * channels), BF16),
            pltpu.VMEM((3, 3 * channels, channels), BF16),
            pltpu.VMEM((lines - 2, 2, half, channels), F32),
            pltpu.VMEM((2, channels), F32),
            pltpu.SemaphoreType.DMA((3,)),
            pltpu.SemaphoreType.DMA,
            pltpu.SemaphoreType.DMA,
        ],
        compiler_params=params(48),
        name="conv1",
    )(meta, *stats, gain.reshape(rows, LANES), shift.reshape(rows, LANES), bias.reshape(1, channels), x, up, low,
      weight.reshape(3, 3 * channels, channels))


def conv2_kernel(
    meta, s0, s1, s2, s3, gain, shift, bias, h_hbm, xp_hbm, w_hbm,
    y_hbm, stats_ref,
    hs, xs, slots, wv, yv, sums, sems, xsem, wsem, ysem,
    *, count, per_group, n_blocks,
):
    lines, _, half, channels = hs.shape
    own = lines - 2
    loads = [pltpu.make_async_copy(h_hbm.at[r], hs.at[r], sems.at[r]) for r in range(lines)]
    for copy in loads:
        copy.start()
    weight_load = pltpu.make_async_copy(w_hbm, wv, wsem)
    weight_load.start()
    edge = (xp_hbm.shape[0] - own) // 2
    x_load = pltpu.make_async_copy(xp_hbm.at[pl.ds(edge, own)], xs, xsem)
    x_load.start()
    scale, move = half_affine((s0, s1, s2, s3), channels // LANES, gain[...], shift[...], count, per_group)
    scale, move = as_row(scale), as_row(move)
    for copy in loads:
        copy.wait()
    first_line = meta[0] * own - 1

    def norm(r, _):
        line = first_line + r
        inside = (line >= 0) & (line < n_blocks * own)
        for at in range(0, channels, LANES):
            cols = slice(at, at + LANES)
            even = jnp.where(inside, half_silu(hs[r, 0, :, cols], scale[:, cols], move[:, cols]), 0.0)
            odd = jnp.where(inside, half_silu(hs[r, 1, :, cols], scale[:, cols], move[:, cols]), 0.0)
            spread_columns(slots, r, at, even, odd, channels)
        return 0

    lax.fori_loop(0, lines, norm, 0)
    x_load.wait()
    weight_load.wait()
    conv_rows(slots, wv, bias, yv, sums, own, 0, own, half, channels, xs)
    store = pltpu.make_async_copy(yv, y_hbm, ysem)
    store.start()
    put_sums(stats_ref, sums[0:1, :], sums[1:2, :], channels // LANES)
    store.wait()


def conv2(meta, stats, gain, shift, bias, h, xp, weight, n_blocks):
    lines, _, half, channels = h.shape
    own = lines - 2
    rows = channels // LANES
    count = float(n_blocks * own * 2 * half * (channels // GROUPS))
    return pl.pallas_call(
        functools.partial(conv2_kernel, count=count, per_group=channels // GROUPS, n_blocks=n_blocks),
        out_shape=(
            jax.ShapeDtypeStruct((own, 2, half, channels), F32),
            jax.ShapeDtypeStruct((2 * rows, LANES), F32),
        ),
        in_specs=[SMEM] + [VMEM] * 7 + [ANY] * 3,
        out_specs=(ANY, VMEM),
        scratch_shapes=[
            pltpu.VMEM((lines, 2, half, channels), F32),
            pltpu.VMEM((own, 2, half, channels), BF16),
            pltpu.VMEM((lines, half, 4 * channels), BF16),
            pltpu.VMEM((3, 3 * channels, channels), BF16),
            pltpu.VMEM((own, 2, half, channels), F32),
            pltpu.VMEM((2, channels), F32),
            pltpu.SemaphoreType.DMA((lines,)),
            pltpu.SemaphoreType.DMA,
            pltpu.SemaphoreType.DMA,
            pltpu.SemaphoreType.DMA,
        ],
        compiler_params=params(48),
        name="conv2",
    )(meta, *stats, gain.reshape(rows, LANES), shift.reshape(rows, LANES), bias.reshape(1, channels), h, xp,
      weight.reshape(3, 3 * channels, channels))


def column_shift(values, tap, half):
    size = values.shape[1]
    lane = lax.broadcasted_iota(jnp.int32, values.shape, 1) % (2 * half)
    even = lane < half
    if tap == 0:
        moved = jnp.where(even, pltpu.roll(values, size - (half - 1), 1), pltpu.roll(values, half, 1))
        return jnp.where(lane == 0, 0.0, moved)
    moved = jnp.where(even, pltpu.roll(values, size - half, 1), pltpu.roll(values, half - 1, 1))
    return jnp.where(lane == 2 * half - 1, 0.0, moved)


def head_kernel(
    meta, s0, s1, s2, s3, gain, shift, w_ref, q_ref, b_ref, y_hbm, part_ref, up_ref, low_ref, ys, act, sems,
    *, count, per_group, n_blocks, n_send,
):
    own, _, half, channels = ys.shape
    width = 2 * half
    loads = [pltpu.make_async_copy(y_hbm.at[r], ys.at[r], sems.at[r]) for r in range(own)]
    for copy in loads:
        copy.start()
    scale, move = half_affine((s0, s1, s2, s3), channels // LANES, gain[...], shift[...], count, per_group)
    scale, move = as_row(scale), as_row(move)
    for copy in loads:
        copy.wait()

    def norm(r, _):
        for parity in range(2):
            for at in range(0, channels, LANES):
                cols = slice(at, at + LANES)
                act[r, parity, :, cols] = half_silu(ys[r, parity, :, cols], scale[:, cols], move[:, cols]).astype(BF16)
        return 0

    lax.fori_loop(0, own, norm, 0)
    flat = act[...].reshape(own * width, channels)
    taps = lax.dot_general(w_ref[...], flat, (((1,), (1,)), ((), ())), preferred_element_type=F32)
    size = part_ref.shape[1]
    moments_n = taps.shape[0] // 9
    spare = jnp.zeros((moments_n, size - own * width), F32)
    total = None
    for i in range(3):
        piece = None
        for j in range(3):
            at = (3 * i + j) * moments_n
            one = taps[at : at + moments_n]
            one = one if j == 1 else column_shift(one, j, half)
            piece = one if piece is None else piece + one
        piece = jnp.concatenate([piece, spare], axis=1)
        if i < 2:
            piece = pltpu.roll(piece, (2 - i) * width, 1)
        total = piece if total is None else total + piece
    lane = lax.broadcasted_iota(jnp.int32, (1, size), 1)
    own_lane = (lane >= width) & (lane < (own + 1) * width)
    latents = []
    for c in range(q_ref.shape[1]):
        value = LATENT_SCALE * jnp.sum(total * q_ref[:, c : c + 1], axis=0, keepdims=True)
        latents.append(value + jnp.where(own_lane, b_ref[c : c + 1, 0:1], 0.0))
    latent = jnp.concatenate(latents, axis=0)
    keep = ((lane >= width) | (meta[0] > 0)) & ((lane < (own + 1) * width) | (meta[0] < n_blocks - 1))
    part_ref[...] = jnp.where(keep, latent, 0.0)
    up_ref[...] = latent[:, : n_send * width]
    low_ref[...] = pltpu.roll(latent, size - (own + 2 - n_send) * width, 1)[:, : n_send * width]


def head(meta, stats, gain, shift, y, weight, bias, quant_weight, quant_bias, n_blocks, n_send):
    own, _, half, channels = y.shape
    width = 2 * half
    rows = channels // LANES
    moments, latents = quant_weight.shape
    count = float(n_blocks * own * width * (channels // GROUPS))
    size = -(-((own + 2) * width) // LANES) * LANES
    taps = weight.transpose(0, 1, 3, 2).reshape(9 * moments, channels)
    offset = LATENT_SCALE * (jnp.sum(bias[:, None] * quant_weight, axis=0) + quant_bias)
    offset = jnp.broadcast_to(offset[:, None], (latents, LANES))
    return pl.pallas_call(
        functools.partial(head_kernel, count=count, per_group=channels // GROUPS, n_blocks=n_blocks, n_send=n_send),
        out_shape=(
            jax.ShapeDtypeStruct((latents, size), F32),
            jax.ShapeDtypeStruct((latents, n_send * width), F32),
            jax.ShapeDtypeStruct((latents, n_send * width), F32),
        ),
        in_specs=[SMEM] + [VMEM] * 9 + [ANY],
        out_specs=(VMEM, VMEM, VMEM),
        scratch_shapes=[
            pltpu.VMEM((own, 2, half, channels), F32),
            pltpu.VMEM((own, 2, half, channels), BF16),
            pltpu.SemaphoreType.DMA((own,)),
        ],
        compiler_params=params(32),
        name="head",
    )(meta, *stats, gain.reshape(rows, LANES), shift.reshape(rows, LANES), taps, quant_weight, offset, y)


def lift_kernel(meta, w_ref, bias_ref, *refs, own, half, n_frames, n_out):
    latents = refs[:n_frames]
    t0_hbm, stats_ref, stack, patches, t0v, sem = refs[n_frames:]
    width = 2 * half
    out_lines = own + 4
    pixels = out_lines * width
    depth, size = stack.shape
    each = latents[0].shape[0]
    for k in range(n_frames):
        value = latents[k][...].astype(F32)
        stack[k * each : (k + 1) * each, :] = jnp.where(meta[1] >= k, value, 0.0)
    frames = stack[...]
    patches[...] = jnp.zeros_like(patches)
    for j in range(3):
        moved = frames if j == 1 else column_shift(frames, j, half)
        for i in range(3):
            piece = moved if i == 0 else pltpu.roll(moved, size - i * width, 1)
            at = (3 * i + j) * depth
            patches[at : at + depth, :] = piece[:, :pixels]
    lhs = jnp.transpose(patches[...], (1, 0)).astype(BF16)
    channels = bias_ref.shape[1]
    for g in range(n_out):
        cols = slice(g * channels, (g + 1) * channels)
        value = jnp.dot(lhs, w_ref[:, cols], preferred_element_type=F32) + bias_ref[...]
        t0v[:, cols] = value
        mine = value[2 * width : (2 + own) * width]
        stats_ref[g : g + 1, :] = mine.sum(0, keepdims=True)
        stats_ref[n_out + g : n_out + g + 1, :] = (mine * mine).sum(0, keepdims=True)
    store = pltpu.make_async_copy(t0v, t0_hbm, sem)
    store.start()
    store.wait()


def lift_weights(weight, n_frames, n_out):
    _, _, _, latents, channels = weight.shape
    back = weight[::-1].transpose(1, 2, 0, 3, 4).reshape(9, 3 * latents, channels)
    blocks = []
    for g in range(n_out):
        blocks.append(jnp.pad(back, ((0, 0), (g * latents, (n_frames - 3 - g) * latents), (0, 0))))
    whole = jnp.concatenate(blocks, axis=2).reshape(9 * n_frames * latents, n_out * channels)
    extra = -whole.shape[0] % 256
    return jnp.pad(whole, ((0, extra), (0, 0)))


def lift(meta, packed, bias, latents, own, half, n_out):
    n_frames = len(latents)
    each, size = latents[0].shape
    channels = bias.shape[0]
    pixels = (own + 4) * 2 * half
    stat_rows = -(-2 * n_out // 8) * 8
    return pl.pallas_call(
        functools.partial(lift_kernel, own=own, half=half, n_frames=n_frames, n_out=n_out),
        out_shape=(
            jax.ShapeDtypeStruct((pixels, n_out * channels), F32),
            jax.ShapeDtypeStruct((stat_rows, channels), F32),
        ),
        in_specs=[SMEM] + [VMEM] * (2 + n_frames),
        out_specs=(ANY, VMEM),
        scratch_shapes=[
            pltpu.VMEM((n_frames * each, size), F32),
            pltpu.VMEM((packed.shape[0], pixels), F32),
            pltpu.VMEM((pixels, n_out * channels), F32),
            pltpu.SemaphoreType.DMA,
        ],
        compiler_params=params(32),
        name="lift",
    )(meta, packed, bias.reshape(1, channels), *latents)


def pair_weight_copies(w_hbm, wv, sems, channels):
    copies = []
    for c in range(2):
        for j in range(3):
            target = wv.at[:, pl.ds((j + c) * channels, channels), pl.ds(c * channels, channels)]
            copies.append(pltpu.make_async_copy(w_hbm.at[:, j], target, sems.at[3 * c + j]))
    return copies


def clear_pair_weights(wv, channels):
    zero = jnp.zeros((wv.shape[0], channels, channels), BF16)
    wv[:, 3 * channels : 4 * channels, 0:channels] = zero
    wv[:, 0:channels, channels : 2 * channels] = zero


def time1_kernel(
    meta, s0, s1, s2, s3, gain, shift, t0_hbm, w_hbm, t1_hbm, stats_ref,
    ts, slots, wv, t1v, sem, wsems, osem,
    *, count, per_group, n_blocks, own, n_out,
):
    frames, lines, half, _ = slots.shape
    channels = gain.shape[1]
    width = 2 * half
    load = pltpu.make_async_copy(t0_hbm, ts, sem)
    load.start()
    weight_loads = pair_weight_copies(w_hbm, wv, wsems, channels)
    for copy in weight_loads:
        copy.start()
    clear_pair_weights(wv, channels)
    scale, move = half_affine((s0, s1, s2, s3), frames, gain[...], shift[...], count, per_group)
    load.wait()
    first_line = meta[0] * own - 2
    for k in range(frames):
        cols = slice(k * channels, (k + 1) * channels)

        def norm(r, _, k=k, cols=cols):
            line = first_line + r
            inside = (line >= 0) & (line < n_blocks * own) & (meta[1] >= k)
            at = pl.multiple_of(r * width, width)
            even = half_silu(ts[pl.ds(at, half), cols], scale[k : k + 1], move[k : k + 1])
            odd = half_silu(ts[pl.ds(at + half, half), cols], scale[k : k + 1], move[k : k + 1])
            even = jnp.where(inside, even, 0.0)
            odd = jnp.where(inside, odd, 0.0)
            spread_columns(slots.at[k], r, 0, even, odd, channels)
            return 0

        lax.fori_loop(0, lines, norm, 0)
    for copy in weight_loads:
        copy.wait()
    out_lines = lines - 2
    for k in range(n_out):
        acc = None
        for t in range(3):
            for i in range(3):
                lhs = slots[k + 2 - t, i : i + out_lines].reshape(out_lines * half, 4 * channels)
                part = jnp.dot(lhs, wv[3 * t + i], preferred_element_type=F32)
                acc = part if acc is None else acc + part
        t1v[k] = acc.reshape(out_lines, half, 2 * channels)
        mine = acc[half : (1 + own) * half]
        first = mine.sum(0, keepdims=True)
        second = (mine * mine).sum(0, keepdims=True)
        stats_ref[k : k + 1, :] = first[:, :channels] + first[:, channels:]
        stats_ref[n_out + k : n_out + k + 1, :] = second[:, :channels] + second[:, channels:]
    store = pltpu.make_async_copy(t1v, t1_hbm, osem)
    store.start()
    store.wait()


def time1(meta, stats, gain, shift, t0, weight, n_blocks, own, half, n_frames, n_out):
    channels = gain.shape[0]
    count = float(n_blocks * own * 2 * half * (channels // GROUPS))
    lines = own + 4
    return pl.pallas_call(
        functools.partial(
            time1_kernel, count=count, per_group=channels // GROUPS, n_blocks=n_blocks, own=own, n_out=n_out
        ),
        out_shape=(
            jax.ShapeDtypeStruct((n_out, lines - 2, half, 2 * channels), F32),
            jax.ShapeDtypeStruct((-(-2 * n_out // 8) * 8, channels), F32),
        ),
        in_specs=[SMEM] + [VMEM] * 6 + [ANY] * 2,
        out_specs=(ANY, VMEM),
        scratch_shapes=[
            pltpu.VMEM(t0.shape, F32),
            pltpu.VMEM((n_frames, lines, half, 4 * channels), BF16),
            pltpu.VMEM((9, 4 * channels, 2 * channels), BF16),
            pltpu.VMEM((n_out, lines - 2, half, 2 * channels), F32),
            pltpu.SemaphoreType.DMA,
            pltpu.SemaphoreType.DMA((6,)),
            pltpu.SemaphoreType.DMA,
        ],
        compiler_params=params(48),
        name="time1",
    )(meta, *stats, gain.reshape(1, channels), shift.reshape(1, channels), t0,
      weight.reshape(9, 3, channels, channels))


def time2_kernel(
    meta, s0, s1, s2, s3, gain, shift, bias, t1_hbm, t0_hbm, w_hbm, out_hbm,
    ts, t0s, slots, wv, rowf, outv, sem, t0sem, wsems, osem,
    *, count, per_group, n_blocks,
):
    frames, lines, half, _ = slots.shape
    own = lines - 2
    channels = gain.shape[1]
    width = 2 * half
    load = pltpu.make_async_copy(t1_hbm, ts, sem)
    load.start()
    weight_loads = pair_weight_copies(w_hbm, wv, wsems, channels)
    for copy in weight_loads:
        copy.start()
    t0_load = pltpu.make_async_copy(t0_hbm.at[pl.ds(2 * width, own * width), pl.ds(0, channels)], t0s, t0sem)
    t0_load.start()
    clear_pair_weights(wv, channels)
    scale, move = half_affine((s0, s1, s2, s3), frames, gain[...], shift[...], count, per_group)
    load.wait()
    first_line = meta[0] * own - 1
    for k in range(frames):

        def norm(r, _, k=k):
            line = first_line + r
            inside = (line >= 0) & (line < n_blocks * own) & (meta[1] >= k)
            even = half_silu(ts[k, r, :, 0:channels], scale[k : k + 1], move[k : k + 1])
            odd = half_silu(ts[k, r, :, channels : 2 * channels], scale[k : k + 1], move[k : k + 1])
            even = jnp.where(inside, even, 0.0)
            odd = jnp.where(inside, odd, 0.0)
            spread_columns(slots.at[k], r, 0, even, odd, channels)
            return 0

        lax.fori_loop(0, lines, norm, 0)
    for copy in weight_loads:
        copy.wait()
    acc = None
    for t in range(3):
        for i in range(3):
            lhs = slots[2 - t, i : i + own].reshape(own * half, 4 * channels)
            part = jnp.dot(lhs, wv[3 * t + i], preferred_element_type=F32)
            acc = part if acc is None else acc + part
    acc = acc.reshape(own, half, 2 * channels)
    t0_load.wait()
    for r in range(own):
        for parity in range(2):
            at = r * width + parity * half
            value = acc[r, :, parity * channels : (parity + 1) * channels] + bias[...] + t0s[at : at + half, :]
            rowf[r, pl.ds(parity, half, stride=2), :] = value
        outv[r] = rowf[r].astype(BF16)
    store = pltpu.make_async_copy(outv, out_hbm.at[0], osem)
    store.start()
    store.wait()


def time2(meta, stats, gain, shift, bias, t1, t0, weight, n_blocks):
    frames, lines, half, _ = t1.shape
    own = lines - 2
    channels = gain.shape[0]
    count = float(n_blocks * own * 2 * half * (channels // GROUPS))
    return pl.pallas_call(
        functools.partial(time2_kernel, count=count, per_group=channels // GROUPS, n_blocks=n_blocks),
        out_shape=jax.ShapeDtypeStruct((1, own, 2 * half, channels), BF16),
        in_specs=[SMEM] + [VMEM] * 7 + [ANY] * 3,
        out_specs=ANY,
        scratch_shapes=[
            pltpu.VMEM(t1.shape, F32),
            pltpu.VMEM((own * 2 * half, channels), F32),
            pltpu.VMEM((frames, lines, half, 4 * channels), BF16),
            pltpu.VMEM((9, 4 * channels, 2 * channels), BF16),
            pltpu.VMEM((own, 2 * half, channels), F32),
            pltpu.VMEM((own, 2 * half, channels), BF16),
            pltpu.SemaphoreType.DMA,
            pltpu.SemaphoreType.DMA,
            pltpu.SemaphoreType.DMA((6,)),
            pltpu.SemaphoreType.DMA,
        ],
        compiler_params=params(48),
        name="time2",
    )(meta, *stats, gain.reshape(1, channels), shift.reshape(1, channels), bias.reshape(1, channels), t1, t0,
      weight.reshape(9, 3, channels, channels))


def turned(block, axis, distance):
    count = lax.axis_size(axis)
    return lax.ppermute(block, axis, [(i, (i + distance) % count) for i in range(count)])


def from_all(block):
    return [block] + [turned(block, "rows", d) for d in range(1, lax.axis_size("rows"))]


def body(
    video, norm1_gain, norm1_shift, conv1_weight, conv1_bias, norm2_gain, norm2_shift, conv2_weight, conv2_bias,
    out_gain, out_shift, out_weight, out_bias, quant_weight, quant_bias, time_in_weight, time_in_bias,
    tnorm1_gain, tnorm1_shift, time1_weight, tnorm2_gain, tnorm2_shift, time2_weight, time2_bias,
):
    x = video[0]
    own, width, _ = x.shape
    half = width // 2
    n_blocks = lax.axis_size("rows")
    meta = jnp.stack([lax.axis_index("rows"), lax.axis_index("frames")]).astype(jnp.int32)
    up = turned(x[own - 2 :], "rows", 1)
    low = turned(x[:2], "rows", -1)
    stats = from_all(input_sums(x))
    h, xp, sums = conv1(meta, stats, norm1_gain, norm1_shift, conv1_bias, x, up, low, conv1_weight, n_blocks)
    y, sums = conv2(meta, from_all(sums), norm2_gain, norm2_shift, conv2_bias, h, xp, conv2_weight, n_blocks)
    part, to_up, to_low = head(
        meta, from_all(sums), out_gain, out_shift, y, out_weight, out_bias, quant_weight, quant_bias, n_blocks, 4
    )
    above = turned(to_low, "rows", 1)
    below = turned(to_up, "rows", -1)
    size = -(-((own + 6) * width) // LANES) * LANES
    row = lax.axis_index("rows")
    above = jnp.where(row > 0, above, 0.0)
    below = jnp.where(row < n_blocks - 1, below, 0.0)
    latent = (
        jnp.pad(part, ((0, 0), (2 * width, size))) [:, :size]
        + jnp.pad(above, ((0, 0), (0, size - 4 * width)))
        + jnp.pad(below, ((0, 0), ((own + 2) * width, size - (own + 6) * width)))
    ).astype(BF16)
    near = jnp.concatenate([latent, turned(latent, "frames", 1), turned(latent, "frames", 2)], axis=0)
    far = turned(near, "frames", 3)
    farther = turned(near, "frames", 4)
    each = latent.shape[0]
    latents = [near[k * each : (k + 1) * each] for k in range(3)] + [far[k * each : (k + 1) * each] for k in range(3)]
    latents.append(farther[2 * each : 3 * each])
    t0, sums = lift(meta, lift_weights(time_in_weight, 7, 5), time_in_bias, latents, own, half, 5)
    t1, sums = time1(meta, from_all(sums), tnorm1_gain, tnorm1_shift, t0, time1_weight, n_blocks, own, half, 5, 3)
    return time2(meta, from_all(sums), tnorm2_gain, tnorm2_shift, time2_bias, t1, t0, time2_weight, n_blocks)


def solution(mesh):
    return jax.shard_map(
        body,
        mesh=mesh,
        in_specs=(P("frames", "rows", None, None),) + (P(),) * 23,
        out_specs=P("frames", "rows", None, None),
        check_vma=False,
    )
```

profile of v0, /device:TPU:0, one launch (start us, length us, event | category | flops | bytes accessed | tf_op | source)
XLA Modules:
  0.0 113.0 jit_solution(3401389760499015637)
XLA Ops:
  0.0 1.3 %copy-done.1 = bf16[1,8,160,512]{3,2,1,0:T(8,128)(2,1)S(1)} copy-done((bf16[1,8,160,512]{3,2,1,0:T(8,128)(2,1)S(1)}, bf16[1,8,160,512]{3,2,1,0:T(8,128)(2,1)}, u32[]{:S(2)}) %copy-start.1) | copy-done | bytes 1310744
  1.4 2.4 %input_sums.1.s0 = f32[8,128]{1,0:T(8,128)S(1)} custom-call(bf16[8,160,512]{2,1,0:T(8,128)(2,1)S(1)} %bitcast.30), custom_call_target="tpu_custom_call" | custom-call | tf_op jit(solution)/shard_map/input_sums/pallas_call | solution.py:104
  3.8 0.5 collective-permute-start
  4.3 2.6 %collective-permute-start.1 = (f32[8,128]{1,0:T(8,128)S(1)}, f32[8,128]{1,0:T(8,128)S(1)}, u32[]{:S(2)}, u32[]{:S(2)}) collective-permute-start(f32[8,128]{1,0:T(8,128)S(1)} %input_sums.1.s0), channel_id=1, source_target_pairs={{0,2},{1,3},{2,0},{3,1},{4,6},{5,7},{6,4},{7,5},{8,10},{9,11},{10,... | collective-permute-start | bytes 12296 | tf_op jit(solution)/shard_map/ppermute | solution.py:639
  6.9 1.4 %collective-permute-start.2 = (f32[8,128]{1,0:T(8,128)S(1)}, f32[8,128]{1,0:T(8,128)S(1)}, u32[]{:S(2)}, u32[]{:S(2)}) collective-permute-start(f32[8,128]{1,0:T(8,128)S(1)} %input_sums.1.s0), channel_id=1, source_target_pairs={{0,3},{1,0},{2,1},{3,2},{4,7},{5,4},{6,5},{7,6},{8,11},{9,8},{10,9... | collective-permute-start | bytes 12296 | tf_op jit(solution)/shard_map/ppermute | solution.py:639
  8.4 1.7 %collective-permute-start.4 = (bf16[2,160,512]{2,1,0:T(8,128)(2,1)S(1)}, bf16[2,160,512]{2,1,0:T(8,128)(2,1)S(1)}, u32[]{:S(2)}, u32[]{:S(2)}) collective-permute-start(bf16[2,160,512]{2,1,0:T(8,128)(2,1)S(1)} %get-tuple-element.29), channel_id=1, source_target_pairs={{0,3},{1,0},{2,1},{3,2},{4,7},{5,4},{6,5},{7,6},{8,11},{9,8},{10,9... | collective-permute-start | bytes 983048 | tf_op jit(solution)/shard_map/ppermute | solution.py:639
  10.2 0.1 multiply_reduce_fusion
  10.5 7.3 %collective-permute-done.3.up_hbm = bf16[2,160,512]{2,1,0:T(8,128)(2,1)S(1)} collective-permute-done((bf16[2,160,512]{2,1,0:T(8,128)(2,1)S(1)}, bf16[2,160,512]{2,1,0:T(8,128)(2,1)S(1)}, u32[]{:S(2)}, u32[]{:S(2)}) %collective-permute-start.3) | collective-permute-done | bytes 327712 | tf_op jit(solution)/shard_map/ppermute | solution.py:639
  17.9 13.2 %conv1.1 = (f32[10,2,80,512]{3,2,1,0:T(8,128)}, bf16[12,2,80,512]{3,2,1,0:T(8,128)(2,1)S(1)}, f32[8,128]{1,0:T(8,128)S(1)}) custom-call(s32[2]{0:T(128)S(1)} %pad_add_fusion.meta, f32[8,128]{1,0:T(8,128)S(1)} %input_sums.1.s0, f32[8,128]{1,0:T(8,128)S(1)} %collective-permute-done.s1, f32[8,128]{1,0:T(8,128)S(1)} %collective-permute-done.1.s2, ...), custom_call_target="tpu_custom_call" | custom-call | tf_op jit(solution)/shard_map/conv1/pallas_call | solution.py:198
  31.1 0.4 collective-permute-start.5
  31.5 0.3 collective-permute-start.6
  31.9 1.1 collective-permute-start.7
  33.0 0.6 pad_dynamic-update-slice_fusion.4
  33.6 0.6 collective-permute-done.5.s1
  34.2 1.0 collective-permute-done.6.s2
  35.2 11.0 %conv2.1 = (f32[8,2,80,512]{3,2,1,0:T(8,128)S(1)}, f32[8,128]{1,0:T(8,128)S(1)}) custom-call(s32[2]{0:T(128)S(1)} %pad_add_fusion.meta, f32[8,128]{1,0:T(8,128)S(1)} %get-tuple-element.17.s0, f32[8,128]{1,0:T(8,128)S(1)} %collective-permute-done.5.s1, f32[8,128]{1,0:T(8,128)S(1)} %collective-permute-done.6.s2, f32[8,128]{1,0:T(8,128)S(1)} %collective-permute-done.7.s3, ...), custom_call_target="tpu_custom_call" | custom-call | tf_op jit(solution)/shard_map/conv2/pallas_call | solution.py:271
  46.2 0.9 collective-permute-start.10
  47.1 0.1 collective-permute-start.8
  47.2 1.6 %collective-permute-start.9 = (f32[8,128]{1,0:T(8,128)S(1)}, f32[8,128]{1,0:T(8,128)S(1)}, u32[]{:S(2)}, u32[]{:S(2)}) collective-permute-start(f32[8,128]{1,0:T(8,128)S(1)} %get-tuple-element.20.s0), channel_id=1, source_target_pairs={{0,2},{1,3},{2,0},{3,1},{4,6},{5,7},{6,4},{7,5},{8,10},{9,11},{10,... | collective-permute-start | bytes 12296 | tf_op jit(solution)/shard_map/ppermute | solution.py:639
  48.8 0.7 pad_dynamic-update-slice_fusion.3
  49.5 0.1 copy.27.q_ref
  49.5 0.6 collective-permute-done.8.s1
  50.2 0.7 collective-permute-done.9.s2
  50.9 0.5 copy-done.6
  51.4 0.9 copy-done.5
  52.3 0.7 copy-done.7
  53.0 0.7 copy-done.11
  53.7 0.7 copy-done.12
  54.3 3.7 %head.1 = (f32[4,1664]{1,0:T(4,128)S(1)}, f32[4,640]{1,0:T(4,128)S(1)}, f32[4,640]{1,0:T(4,128)}) custom-call(s32[2]{0:T(128)S(1)} %pad_add_fusion.meta, f32[8,128]{1,0:T(8,128)S(1)} %get-tuple-element.20.s0, f32[8,128]{1,0:T(8,128)S(1)} %collective-permute-done.8.s1, f32[8,128]{1,0:T(8,128)S(1)} %copy-done.7, f32[8,128]{1,0:T(8,128)S(1)} %collective-permute-done.10.s3, ...), custom_call_target="tpu_custom_call" | custom-call | tf_op jit(solution)/shard_map/head/pallas_call | solution.py:370
  58.1 0.6 copy-done.22
  58.7 0.5 collective-permute-start.11
  59.2 0.6 pad_dynamic-update-slice_fusion.2
  59.8 1.2 %collective-permute-start.12 = (f32[4,640]{1,0:T(4,128)}, f32[4,640]{1,0:T(4,128)S(1)}, u32[]{:S(2)}, u32[]{:S(2)}) collective-permute-start(f32[4,640]{1,0:T(4,128)} %copy-done.22), channel_id=1, source_target_pairs={{0,3},{1,0},{2,1},{3,2},{4,7},{5,4},{6,5},{7,6},{8,11},{9,8},{10,9... | collective-permute-start | bytes 30728 | tf_op jit(solution)/shard_map/ppermute | solution.py:639
  61.0 0.9 collective-permute-done.11
  62.0 0.7 collective-permute-done.12
  62.6 0.1 fusion.2.refs_0_
  62.7 1.4 %collective-permute-start.13 = (bf16[4,2304]{1,0:T(4,128)(2,1)S(1)}, bf16[4,2304]{1,0:T(4,128)(2,1)S(1)}, u32[]{:S(2)}, u32[]{:S(2)}) collective-permute-start(bf16[4,2304]{1,0:T(4,128)(2,1)S(1)} %fusion.2.refs_0_), channel_id=1, source_target_pairs={{0,4},{4,8},{8,12},{12,16},{16,20},{20,24},{24,28},{28,0},{1,5},{5... | collective-permute-start | bytes 55304 | tf_op jit(solution)/shard_map/ppermute | solution.py:639
  64.2 1.6 %collective-permute-start.14 = (bf16[4,2304]{1,0:T(4,128)(2,1)S(1)}, bf16[4,2304]{1,0:T(4,128)(2,1)S(1)}, u32[]{:S(2)}, u32[]{:S(2)}) collective-permute-start(bf16[4,2304]{1,0:T(4,128)(2,1)S(1)} %fusion.2.refs_0_), channel_id=1, source_target_pairs={{0,8},{4,12},{8,16},{12,20},{16,24},{20,28},{24,0},{28,4},{1,9},{5... | collective-permute-start | bytes 55304 | tf_op jit(solution)/shard_map/ppermute | solution.py:639
  65.8 1.4 %pad_dynamic-update-slice_fusion.1 = bf16[9,28,640]{2,1,0:T(8,128)(2,1)} fusion(bf16[9,28,640]{2,1,0:T(8,128)(2,1)} %pad_dynamic-update-slice_fusion.2, bf16[9,12,128]{2,1,0:T(8,128)(2,1)} %copy-done.23), kind=kLoop, calls=%fused_computation.4 | loop fusion | bytes 110592
  67.2 2.1 %collective-permute-done.13.refs_1_ = bf16[4,2304]{1,0:T(4,128)(2,1)S(1)} collective-permute-done((bf16[4,2304]{1,0:T(4,128)(2,1)S(1)}, bf16[4,2304]{1,0:T(4,128)(2,1)S(1)}, u32[]{:S(2)}, u32[]{:S(2)}) %collective-permute-start.13) | collective-permute-done | bytes 18464 | tf_op jit(solution)/shard_map/ppermute | solution.py:639
  69.2 0.5 collective-permute-done.14.refs_2_
  69.8 0.8 collective-permute-start.15
  70.6 1.4 %pad_dynamic-update-slice_fusion = bf16[9,28,640]{2,1,0:T(8,128)(2,1)} fusion(bf16[9,28,640]{2,1,0:T(8,128)(2,1)} %pad_dynamic-update-slice_fusion.1, bf16[9,12,128]{2,1,0:T(8,128)(2,1)} %copy-done.23), kind=kLoop, calls=%fused_computation.3 | loop fusion | bytes 110592 | tf_op jit(solution)/shard_map/concatenate | solution.py:428
  72.0 1.0 reshape.68
  73.1 1.4 %collective-permute-start.16 = (bf16[12,2304]{1,0:T(8,128)(2,1)S(1)}, bf16[12,2304]{1,0:T(8,128)(2,1)S(1)}, u32[]{:S(2)}, u32[]{:S(2)}) collective-permute-start(bf16[12,2304]{1,0:T(8,128)(2,1)S(1)} %pad_maximum_fusion), channel_id=1, source_target_pairs={{0,16},{4,20},{8,24},{12,28},{16,0},{20,4},{24,8},{28,12},{1,17},{... | collective-permute-start | bytes 165896 | tf_op jit(solution)/shard_map/ppermute | solution.py:639
  74.5 2.3 %collective-permute-done.15 = bf16[12,2304]{1,0:T(8,128)(2,1)S(1)} collective-permute-done((bf16[12,2304]{1,0:T(8,128)(2,1)S(1)}, bf16[12,2304]{1,0:T(8,128)(2,1)S(1)}, u32[]{:S(2)}, u32[]{:S(2)}) %collective-permute-start.15) | collective-permute-done | bytes 55328 | tf_op jit(solution)/shard_map/ppermute | solution.py:639
  76.8 3.3 %collective-permute-done.16 = bf16[12,2304]{1,0:T(8,128)(2,1)S(1)} collective-permute-done((bf16[12,2304]{1,0:T(8,128)(2,1)S(1)}, bf16[12,2304]{1,0:T(8,128)(2,1)S(1)}, u32[]{:S(2)}, u32[]{:S(2)}) %collective-permute-start.16) | collective-permute-done | bytes 55328 | tf_op jit(solution)/shard_map/ppermute | solution.py:639
  80.2 0.6 copy-done.16
  80.8 3.3 %lift.1 = (f32[1920,640]{1,0:T(8,128)S(1)}, f32[16,128]{1,0:T(8,128)S(1)}) custom-call(s32[2]{0:T(128)S(1)} %pad_add_fusion.meta, bf16[256,640]{1,0:T(8,128)(2,1)S(1)} %pad.41.w_ref, f32[1,128]{1,0:T(1,128)S(1)} %bitcast.43, bf16[4,2304]{1,0:T(4,128)(2,1)S(1)} %fusion.2.refs_0_, bf16[4,2304]{1,0:T(4,128)(2,1)S(1)} %collective-permute-done.13.refs_1_, ...), custom_call_target="tpu_custom_call" | custom-call | tf_op jit(solution)/shard_map/lift/pallas_call | solution.py:439
  84.1 2.2 %copy-done = f32[1920,640]{1,0:T(8,128)} copy-done((f32[1920,640]{1,0:T(8,128)}, f32[1920,640]{1,0:T(8,128)S(1)}, u32[]{:S(2)}) %copy-start) | copy-done | bytes 4915224
  86.3 1.0 collective-permute-start.18
  87.4 1.5 %collective-permute-start.19 = (f32[16,128]{1,0:T(8,128)S(1)}, f32[16,128]{1,0:T(8,128)S(1)}, u32[]{:S(2)}, u32[]{:S(2)}) collective-permute-start(f32[16,128]{1,0:T(8,128)S(1)} %get-tuple-element.25.s0), channel_id=1, source_target_pairs={{0,3},{1,0},{2,1},{3,2},{4,7},{5,4},{6,5},{7,6},{8,11},{9,8},{10,9... | collective-permute-start | bytes 24584 | tf_op jit(solution)/shard_map/ppermute | solution.py:639
  88.8 0.6 collective-permute-done.17.s1
  89.4 0.6 collective-permute-done.18.s2
  90.0 0.2 collective-permute-done.19.s3
  90.2 0.7 copy-done.17
  90.8 0.7 copy-done.18
  91.5 11.5 %time1.1 = (f32[3,10,80,256]{3,2,1,0:T(8,128)S(1)}, f32[8,128]{1,0:T(8,128)S(1)}) custom-call(s32[2]{0:T(128)S(1)} %pad_add_fusion.meta, f32[16,128]{1,0:T(8,128)S(1)} %get-tuple-element.25.s0, f32[16,128]{1,0:T(8,128)S(1)} %collective-permute-done.17.s1, f32[16,128]{1,0:T(8,128)S(1)} %collective-permute-done.18.s2, ...), custom_call_target="tpu_custom_call" | custom-call | tf_op jit(solution)/shard_map/time1/pallas_call | solution.py:530
  103.0 1.1 %collective-permute-start.20 = (f32[8,128]{1,0:T(8,128)S(1)}, f32[8,128]{1,0:T(8,128)S(1)}, u32[]{:S(2)}, u32[]{:S(2)}) collective-permute-start(f32[8,128]{1,0:T(8,128)S(1)} %get-tuple-element.27.s0), channel_id=1, source_target_pairs={{0,1},{1,2},{2,3},{3,0},{4,5},{5,6},{6,7},{7,4},{8,9},{9,10},{10,1... | collective-permute-start | bytes 12296 | tf_op jit(solution)/shard_map/ppermute | solution.py:639
  104.2 1.0 collective-permute-start.21
  105.2 0.4 collective-permute-start.22
  105.6 0.5 collective-permute-done.20.s1
  106.1 1.7 %collective-permute-done.21.s2 = f32[8,128]{1,0:T(8,128)S(1)} collective-permute-done((f32[8,128]{1,0:T(8,128)S(1)}, f32[8,128]{1,0:T(8,128)S(1)}, u32[]{:S(2)}, u32[]{:S(2)}) %collective-permute-start.21) | collective-permute-done | bytes 4128 | tf_op jit(solution)/shard_map/ppermute | solution.py:639
  107.8 5.0 %time2.1 = bf16[1,8,160,128]{3,2,1,0:T(8,128)(2,1)} custom-call(s32[2]{0:T(128)S(1)} %pad_add_fusion.meta, f32[8,128]{1,0:T(8,128)S(1)} %get-tuple-element.27.s0, f32[8,128]{1,0:T(8,128)S(1)} %collective-permute-done.20.s1, f32[8,128]{1,0:T(8,128)S(1)} %collective-permute-done.21.s2, f32[8,128]{1,0:T(8,128)S(1)} %collective-permute-done.22.s3, ...), custom_call_target="tpu_custom_call" | custom-call | tf_op jit(solution)/shard_map/time2/pallas_call | solution.py:614
  (69 shorter events, 0.5 us)
Async XLA Ops:
  0.0 10.1 %copy-start.27 = (f32[8]{0:T(128)S(1)}, f32[8]{0:T(128)}, u32[]{:S(2)}) copy-start(f32[8]{0:T(128)} %param.36) | copy-start | bytes 100
  0.0 10.3 %copy-start.28 = (f32[4]{0:T(128)S(1)}, f32[4]{0:T(128)}, u32[]{:S(2)}) copy-start(f32[4]{0:T(128)} %param.38) | copy-start | bytes 52
  0.0 1.3 %copy-start.1 = (bf16[1,8,160,512]{3,2,1,0:T(8,128)(2,1)S(1)}, bf16[1,8,160,512]{3,2,1,0:T(8,128)(2,1)}, u32[]{:S(2)}) copy-start(bf16[1,8,160,512]{3,2,1,0:T(8,128)(2,1)} %param.24) | copy-start | bytes 3932164
  1.3 8.8 %copy-start.25 = (bf16[3,3,3,4,128]{4,3,2,1,0:T(4,128)(2,1)S(1)}, bf16[3,3,3,4,128]{4,3,2,1,0:T(4,128)(2,1)}, u32[]{:S(2)}) copy-start(bf16[3,3,3,4,128]{4,3,2,1,0:T(4,128)(2,1)} %param.39) | copy-start | bytes 82948
  1.4 8.8 %copy-start.26 = (f32[8,4]{0,1:T(4,128)S(1)}, f32[8,4]{0,1:T(4,128)}, u32[]{:S(2)}) copy-start(f32[8,4]{0,1:T(4,128)} %param.37) | copy-start | bytes 388
  1.4 16.4 %copy-start.2 = (bf16[1,8,160,512]{3,2,1,0:T(8,128)(2,1)S(1)}, bf16[1,8,160,512]{3,2,1,0:T(8,128)(2,1)}, u32[]{:S(2)}) copy-start(bf16[1,8,160,512]{3,2,1,0:T(8,128)(2,1)} %param.24) | copy-start | bytes 3932164
  1.4 16.4 %copy-start.8 = (f32[512]{0:T(512)S(1)}, f32[512]{0:T(512)}, u32[]{:S(2)}) copy-start(f32[512]{0:T(512)} %param.25) | copy-start | bytes 6148
  1.4 16.4 %copy-start.9 = (f32[512]{0:T(512)S(1)}, f32[512]{0:T(512)}, u32[]{:S(2)}) copy-start(f32[512]{0:T(512)} %param.26) | copy-start | bytes 6148
  1.4 16.4 %copy-start.10 = (f32[512]{0:T(512)S(1)}, f32[512]{0:T(512)}, u32[]{:S(2)}) copy-start(f32[512]{0:T(512)} %param.28) | copy-start | bytes 6148
  3.8 6.7 %collective-permute-start = (f32[8,128]{1,0:T(8,128)S(1)}, f32[8,128]{1,0:T(8,128)S(1)}, u32[]{:S(2)}, u32[]{:S(2)}) collective-permute-start(f32[8,128]{1,0:T(8,128)S(1)} %input_sums.1.s0), channel_id=1, source_target_pairs={{0,1},{1,2},{2,3},{3,0},{4,5},{5,6},{6,7},{7,4},{8,9},{9,10},{10,1... | collective-permute-start | bytes 12296 | tf_op jit(solution)/shard_map/ppermute | solution.py:639
  4.3 6.1 %collective-permute-start.1 = (f32[8,128]{1,0:T(8,128)S(1)}, f32[8,128]{1,0:T(8,128)S(1)}, u32[]{:S(2)}, u32[]{:S(2)}) collective-permute-start(f32[8,128]{1,0:T(8,128)S(1)} %input_sums.1.s0), channel_id=1, source_target_pairs={{0,2},{1,3},{2,0},{3,1},{4,6},{5,7},{6,4},{7,5},{8,10},{9,11},{10,... | collective-permute-start | bytes 12296 | tf_op jit(solution)/shard_map/ppermute | solution.py:639
  6.9 3.6 %collective-permute-start.2 = (f32[8,128]{1,0:T(8,128)S(1)}, f32[8,128]{1,0:T(8,128)S(1)}, u32[]{:S(2)}, u32[]{:S(2)}) collective-permute-start(f32[8,128]{1,0:T(8,128)S(1)} %input_sums.1.s0), channel_id=1, source_target_pairs={{0,3},{1,0},{2,1},{3,2},{4,7},{5,4},{6,5},{7,6},{8,11},{9,8},{10,9... | collective-permute-start | bytes 12296 | tf_op jit(solution)/shard_map/ppermute | solution.py:639
  8.3 9.5 %collective-permute-start.3 = (bf16[2,160,512]{2,1,0:T(8,128)(2,1)S(1)}, bf16[2,160,512]{2,1,0:T(8,128)(2,1)S(1)}, u32[]{:S(2)}, u32[]{:S(2)}) collective-permute-start(bf16[2,160,512]{2,1,0:T(8,128)(2,1)S(1)} %get-tuple-element.30), channel_id=1, source_target_pairs={{0,1},{1,2},{2,3},{3,0},{4,5},{5,6},{6,7},{7,4},{8,9},{9,10},{10,1... | collective-permute-start | bytes 983048 | tf_op jit(solution)/shard_map/ppermute | solution.py:639
  8.4 9.4 %collective-permute-start.4 = (bf16[2,160,512]{2,1,0:T(8,128)(2,1)S(1)}, bf16[2,160,512]{2,1,0:T(8,128)(2,1)S(1)}, u32[]{:S(2)}, u32[]{:S(2)}) collective-permute-start(bf16[2,160,512]{2,1,0:T(8,128)(2,1)S(1)} %get-tuple-element.29), channel_id=1, source_target_pairs={{0,3},{1,0},{2,1},{3,2},{4,7},{5,4},{6,5},{7,6},{8,11},{9,8},{10,9... | collective-permute-start | bytes 983048 | tf_op jit(solution)/shard_map/ppermute | solution.py:639
  10.4 38.4 %copy-start.23 = (bf16[9,12,128]{2,1,0:T(8,128)(2,1)}, bf16[9,12,128]{2,1,0:T(8,128)(2,1)S(1)}, u32[]{:S(2)}) copy-start(bf16[9,12,128]{2,1,0:T(8,128)(2,1)S(1)} %reshape.67) | copy-start | bytes 82948
  17.8 17.3 %copy-start.13 = (f32[512]{0:T(512)S(1)}, f32[512]{0:T(512)}, u32[]{:S(2)}) copy-start(f32[512]{0:T(512)} %param.29) | copy-start | bytes 6148
  17.8 17.3 %copy-start.14 = (f32[512]{0:T(512)S(1)}, f32[512]{0:T(512)}, u32[]{:S(2)}) copy-start(f32[512]{0:T(512)} %param.30) | copy-start | bytes 6148
  17.9 17.3 %copy-start.15 = (f32[512]{0:T(512)S(1)}, f32[512]{0:T(512)}, u32[]{:S(2)}) copy-start(f32[512]{0:T(512)} %param.32) | copy-start | bytes 6148
  31.1 3.1 %collective-permute-start.5 = (f32[8,128]{1,0:T(8,128)S(1)}, f32[8,128]{1,0:T(8,128)S(1)}, u32[]{:S(2)}, u32[]{:S(2)}) collective-permute-start(f32[8,128]{1,0:T(8,128)S(1)} %get-tuple-element.17.s0), channel_id=1, source_target_pairs={{0,1},{1,2},{2,3},{3,0},{4,5},{5,6},{6,7},{7,4},{8,9},{9,10},{10,1... | collective-permute-start | bytes 12296 | tf_op jit(solution)/shard_map/ppermute | solution.py:639
  31.5 3.6 %collective-permute-start.6 = (f32[8,128]{1,0:T(8,128)S(1)}, f32[8,128]{1,0:T(8,128)S(1)}, u32[]{:S(2)}, u32[]{:S(2)}) collective-permute-start(f32[8,128]{1,0:T(8,128)S(1)} %get-tuple-element.17.s0), channel_id=1, source_target_pairs={{0,2},{1,3},{2,0},{3,1},{4,6},{5,7},{6,4},{7,5},{8,10},{9,11},{10,... | collective-permute-start | bytes 12296 | tf_op jit(solution)/shard_map/ppermute | solution.py:639
  31.9 3.3 %collective-permute-start.7 = (f32[8,128]{1,0:T(8,128)S(1)}, f32[8,128]{1,0:T(8,128)S(1)}, u32[]{:S(2)}, u32[]{:S(2)}) collective-permute-start(f32[8,128]{1,0:T(8,128)S(1)} %get-tuple-element.17.s0), channel_id=1, source_target_pairs={{0,3},{1,0},{2,1},{3,2},{4,7},{5,4},{6,5},{7,6},{8,11},{9,8},{10,9... | collective-permute-start | bytes 12296 | tf_op jit(solution)/shard_map/ppermute | solution.py:639
  46.2 3.3 %collective-permute-start.10 = (f32[8,128]{1,0:T(8,128)S(1)}, f32[8,128]{1,0:T(8,128)S(1)}, u32[]{:S(2)}, u32[]{:S(2)}) collective-permute-start(f32[8,128]{1,0:T(8,128)S(1)} %get-tuple-element.20.s0), channel_id=1, source_target_pairs={{0,3},{1,0},{2,1},{3,2},{4,7},{5,4},{6,5},{7,6},{8,11},{9,8},{10,9... | collective-permute-start | bytes 12296 | tf_op jit(solution)/shard_map/ppermute | solution.py:639
  47.1 3.0 %collective-permute-start.8 = (f32[8,128]{1,0:T(8,128)S(1)}, f32[8,128]{1,0:T(8,128)S(1)}, u32[]{:S(2)}, u32[]{:S(2)}) collective-permute-start(f32[8,128]{1,0:T(8,128)S(1)} %get-tuple-element.20.s0), channel_id=1, source_target_pairs={{0,1},{1,2},{2,3},{3,0},{4,5},{5,6},{6,7},{7,4},{8,9},{9,10},{10,1... | collective-permute-start | bytes 12296 | tf_op jit(solution)/shard_map/ppermute | solution.py:639
  47.2 3.6 %collective-permute-start.9 = (f32[8,128]{1,0:T(8,128)S(1)}, f32[8,128]{1,0:T(8,128)S(1)}, u32[]{:S(2)}, u32[]{:S(2)}) collective-permute-start(f32[8,128]{1,0:T(8,128)S(1)} %get-tuple-element.20.s0), channel_id=1, source_target_pairs={{0,2},{1,3},{2,0},{3,1},{4,6},{5,7},{6,4},{7,5},{8,10},{9,11},{10,... | collective-permute-start | bytes 12296 | tf_op jit(solution)/shard_map/ppermute | solution.py:639
  50.8 0.6 copy-start.6
  51.4 0.9 copy-start.5
  52.3 0.7 copy-start.7
  53.0 0.7 copy-start.11
  53.7 0.7 copy-start.12
  54.3 4.8 %copy-start.24 = (bf16[9,12,128]{2,1,0:T(8,128)(2,1)S(1)}, bf16[9,12,128]{2,1,0:T(8,128)(2,1)}, u32[]{:S(2)}) copy-start(bf16[9,12,128]{2,1,0:T(8,128)(2,1)} %copy-done.23) | copy-start | bytes 82948
  54.3 35.8 %copy-start.4 = (bf16[3,3,3,128,128]{4,3,2,1,0:T(8,128)(2,1)S(1)}, bf16[3,3,3,128,128]{4,3,2,1,0:T(8,128)(2,1)}, u32[]{:S(2)}) copy-start(bf16[3,3,3,128,128]{4,3,2,1,0:T(8,128)(2,1)} %param.43) | copy-start | bytes 2654212
  58.1 0.6 copy-start.22
  58.7 3.3 %collective-permute-start.11 = (f32[4,640]{1,0:T(4,128)}, f32[4,640]{1,0:T(4,128)S(1)}, u32[]{:S(2)}, u32[]{:S(2)}) collective-permute-start(f32[4,640]{1,0:T(4,128)} %get-tuple-element.23), channel_id=1, source_target_pairs={{0,1},{1,2},{2,3},{3,0},{4,5},{5,6},{6,7},{7,4},{8,9},{9,10},{10,1... | collective-permute-start | bytes 30728 | tf_op jit(solution)/shard_map/ppermute | solution.py:639
  59.8 2.8 %collective-permute-start.12 = (f32[4,640]{1,0:T(4,128)}, f32[4,640]{1,0:T(4,128)S(1)}, u32[]{:S(2)}, u32[]{:S(2)}) collective-permute-start(f32[4,640]{1,0:T(4,128)} %copy-done.22), channel_id=1, source_target_pairs={{0,3},{1,0},{2,1},{3,2},{4,7},{5,4},{6,5},{7,6},{8,11},{9,8},{10,9... | collective-permute-start | bytes 30728 | tf_op jit(solution)/shard_map/ppermute | solution.py:639
  62.7 6.5 %collective-permute-start.13 = (bf16[4,2304]{1,0:T(4,128)(2,1)S(1)}, bf16[4,2304]{1,0:T(4,128)(2,1)S(1)}, u32[]{:S(2)}, u32[]{:S(2)}) collective-permute-start(bf16[4,2304]{1,0:T(4,128)(2,1)S(1)} %fusion.2.refs_0_), channel_id=1, source_target_pairs={{0,4},{4,8},{8,12},{12,16},{16,20},{20,24},{24,28},{28,0},{1,5},{5... | collective-permute-start | bytes 55304 | tf_op jit(solution)/shard_map/ppermute | solution.py:639
  64.2 5.6 %collective-permute-start.14 = (bf16[4,2304]{1,0:T(4,128)(2,1)S(1)}, bf16[4,2304]{1,0:T(4,128)(2,1)S(1)}, u32[]{:S(2)}, u32[]{:S(2)}) collective-permute-start(bf16[4,2304]{1,0:T(4,128)(2,1)S(1)} %fusion.2.refs_0_), channel_id=1, source_target_pairs={{0,8},{4,12},{8,16},{12,20},{16,24},{20,28},{24,0},{28,4},{1,9},{5... | collective-permute-start | bytes 55304 | tf_op jit(solution)/shard_map/ppermute | solution.py:639
  69.8 7.0 %collective-permute-start.15 = (bf16[12,2304]{1,0:T(8,128)(2,1)S(1)}, bf16[12,2304]{1,0:T(8,128)(2,1)S(1)}, u32[]{:S(2)}, u32[]{:S(2)}) collective-permute-start(bf16[12,2304]{1,0:T(8,128)(2,1)S(1)} %pad_maximum_fusion), channel_id=1, source_target_pairs={{0,12},{4,16},{8,20},{12,24},{16,28},{20,0},{24,4},{28,8},{1,13},{... | collective-permute-start | bytes 165896 | tf_op jit(solution)/shard_map/ppermute | solution.py:639
  73.1 7.0 %collective-permute-start.16 = (bf16[12,2304]{1,0:T(8,128)(2,1)S(1)}, bf16[12,2304]{1,0:T(8,128)(2,1)S(1)}, u32[]{:S(2)}, u32[]{:S(2)}) collective-permute-start(bf16[12,2304]{1,0:T(8,128)(2,1)S(1)} %pad_maximum_fusion), channel_id=1, source_target_pairs={{0,16},{4,20},{8,24},{12,28},{16,0},{20,4},{24,8},{28,12},{1,17},{... | collective-permute-start | bytes 165896 | tf_op jit(solution)/shard_map/ppermute | solution.py:639
  80.1 0.7 copy-start.16
  84.1 2.2 %copy-start = (f32[1920,640]{1,0:T(8,128)}, f32[1920,640]{1,0:T(8,128)S(1)}, u32[]{:S(2)}) copy-start(f32[1920,640]{1,0:T(8,128)S(1)} %get-tuple-element.26.t0_hbm) | copy-start | bytes 14745604
  86.3 3.1 %collective-permute-start.17 = (f32[16,128]{1,0:T(8,128)S(1)}, f32[16,128]{1,0:T(8,128)S(1)}, u32[]{:S(2)}, u32[]{:S(2)}) collective-permute-start(f32[16,128]{1,0:T(8,128)S(1)} %get-tuple-element.25.s0), channel_id=1, source_target_pairs={{0,1},{1,2},{2,3},{3,0},{4,5},{5,6},{6,7},{7,4},{8,9},{9,10},{10,1... | collective-permute-start | bytes 24584 | tf_op jit(solution)/shard_map/ppermute | solution.py:639
  86.3 3.7 %collective-permute-start.18 = (f32[16,128]{1,0:T(8,128)S(1)}, f32[16,128]{1,0:T(8,128)S(1)}, u32[]{:S(2)}, u32[]{:S(2)}) collective-permute-start(f32[16,128]{1,0:T(8,128)S(1)} %get-tuple-element.25.s0), channel_id=1, source_target_pairs={{0,2},{1,3},{2,0},{3,1},{4,6},{5,7},{6,4},{7,5},{8,10},{9,11},{10,... | collective-permute-start | bytes 24584 | tf_op jit(solution)/shard_map/ppermute | solution.py:639
  87.4 2.8 %collective-permute-start.19 = (f32[16,128]{1,0:T(8,128)S(1)}, f32[16,128]{1,0:T(8,128)S(1)}, u32[]{:S(2)}, u32[]{:S(2)}) collective-permute-start(f32[16,128]{1,0:T(8,128)S(1)} %get-tuple-element.25.s0), channel_id=1, source_target_pairs={{0,3},{1,0},{2,1},{3,2},{4,7},{5,4},{6,5},{7,6},{8,11},{9,8},{10,9... | collective-permute-start | bytes 24584 | tf_op jit(solution)/shard_map/ppermute | solution.py:639
  90.2 0.7 copy-start.17
  90.8 0.7 copy-start.18
  91.5 16.3 %copy-start.3 = (bf16[3,3,3,128,128]{4,3,2,1,0:T(8,128)(2,1)S(1)}, bf16[3,3,3,128,128]{4,3,2,1,0:T(8,128)(2,1)}, u32[]{:S(2)}) copy-start(bf16[3,3,3,128,128]{4,3,2,1,0:T(8,128)(2,1)} %param.46) | copy-start | bytes 2654212
  91.5 16.3 %copy-start.19 = (f32[128]{0:T(128)S(1)}, f32[128]{0:T(128)}, u32[]{:S(2)}) copy-start(f32[128]{0:T(128)} %param.44) | copy-start | bytes 1540
  91.5 16.3 %copy-start.20 = (f32[128]{0:T(128)S(1)}, f32[128]{0:T(128)}, u32[]{:S(2)}) copy-start(f32[128]{0:T(128)} %param.45) | copy-start | bytes 1540
  91.5 16.3 %copy-start.21 = (f32[128]{0:T(128)S(1)}, f32[128]{0:T(128)}, u32[]{:S(2)}) copy-start(f32[128]{0:T(128)} %param.47) | copy-start | bytes 1540
  103.0 3.1 %collective-permute-start.20 = (f32[8,128]{1,0:T(8,128)S(1)}, f32[8,128]{1,0:T(8,128)S(1)}, u32[]{:S(2)}, u32[]{:S(2)}) collective-permute-start(f32[8,128]{1,0:T(8,128)S(1)} %get-tuple-element.27.s0), channel_id=1, source_target_pairs={{0,1},{1,2},{2,3},{3,0},{4,5},{5,6},{6,7},{7,4},{8,9},{9,10},{10,1... | collective-permute-start | bytes 12296 | tf_op jit(solution)/shard_map/ppermute | solution.py:639
  104.2 3.6 %collective-permute-start.21 = (f32[8,128]{1,0:T(8,128)S(1)}, f32[8,128]{1,0:T(8,128)S(1)}, u32[]{:S(2)}, u32[]{:S(2)}) collective-permute-start(f32[8,128]{1,0:T(8,128)S(1)} %get-tuple-element.27.s0), channel_id=1, source_target_pairs={{0,2},{1,3},{2,0},{3,1},{4,6},{5,7},{6,4},{7,5},{8,10},{9,11},{10,... | collective-permute-start | bytes 12296 | tf_op jit(solution)/shard_map/ppermute | solution.py:639
  105.2 2.6 %collective-permute-start.22 = (f32[8,128]{1,0:T(8,128)S(1)}, f32[8,128]{1,0:T(8,128)S(1)}, u32[]{:S(2)}, u32[]{:S(2)}) collective-permute-start(f32[8,128]{1,0:T(8,128)S(1)} %get-tuple-element.27.s0), channel_id=1, source_target_pairs={{0,3},{1,0},{2,1},{3,2},{4,7},{5,4},{6,5},{7,6},{8,11},{9,8},{10,9... | collective-permute-start | bytes 12296 | tf_op jit(solution)/shard_map/ppermute | solution.py:639
where the time goes:
time: 113 us
  Pallas kernels  50.1 us (44%)
  waiting for transfers between devices  23.5 us (21%)
  starting transfers between devices  22.8 us (20%)
  local copies, waits for them, and re-layouts  15.8 us (14%)
    ppermute x23, waiting for transfers between devices, turned(): lax.ppermute(block, axis, [(i, (i + distance) % count) for i in range(cou...  23.5 us
    ppermute x23, starting transfers between devices, turned(): lax.ppermute(block, axis, [(i, (i + distance) % count) for i in range(cou...  22.8 us
    pallas_call x1, Pallas kernels, conv1(): pl.pallas_call(functools.partial(conv1_kernel, count=count, per_group=cha...  13.2 us
    unnamed x63, local copies, waits for them, and re-layouts  13.1 us
    pallas_call x1, Pallas kernels, time1(): pl.pallas_call(functools.partial(time1_kernel, count=count, per_group=cha...  11.5 us
    pallas_call x1, Pallas kernels, conv2(): pl.pallas_call(functools.partial(conv2_kernel, count=count, per_group=cha...  11 us
    pallas_call x1, Pallas kernels, time2(): pl.pallas_call(functools.partial(time2_kernel, count=count, per_group=cha...  4.99 us
    pallas_call x1, Pallas kernels, head(): pl.pallas_call(functools.partial(head_kernel, count=count, per_group=chan...  3.7 us
  transfers between devices with their start and end apart: 23, of which 16 were waited for; matrix products, arithmetic and copies ran while one was open for 6% of the time, Pallas kernels for 0%

commit v1 on v0

--- a/solution.py
+++ b/solution.py
@@ -14,13 +14,21 @@
 F32 = jnp.float32
 BF16 = jnp.bfloat16
 
-ANY = pl.BlockSpec(memory_space=pl.ANY)
+HBM = pl.BlockSpec(memory_space=pltpu.HBM)
 VMEM = pl.BlockSpec(memory_space=pltpu.VMEM)
 SMEM = pl.BlockSpec(memory_space=pltpu.SMEM)
 
 
+def in_hbm(array):
+    return pltpu.with_memory_space_constraint(array, pltpu.HBM)
+
+
 def params(mib=48):
     return pltpu.CompilerParams(vmem_limit_bytes=mib * 1024 * 1024)
+
+
+def cost(flops):
+    return pl.CostEstimate(flops=int(flops), transcendentals=0, bytes_accessed=0)
 
 
 def lane_groups(values, size):
@@ -70,44 +78,34 @@
         slots[row, :, slot * channels + at : slot * channels + at + width] = piece.astype(BF16)
 
 
-def input_sums_kernel(x_hbm, out_ref, xs, sems):
-    lines = xs.shape[0]
-    copies = [pltpu.make_async_copy(x_hbm.at[r], xs.at[r], sems.at[r]) for r in range(lines)]
-    for copy in copies:
-        copy.start()
-    width, channels = xs.shape[1], xs.shape[2]
-    first = [jnp.zeros((8, LANES), F32) for _ in range(channels // LANES)]
-    second = list(first)
-    for r in range(lines):
-        copies[r].wait()
-
-        def step(m, carry, r=r):
-            first, second = carry
-            first, second = list(first), list(second)
-            at = pl.multiple_of(m * 32, 32)
-            for k in range(channels // LANES):
-                v = xs[r, pl.ds(at, 32), k * LANES : (k + 1) * LANES].astype(F32)
-                v = v.reshape(4, 8, LANES)
-                first[k] = first[k] + v.sum(0)
-                second[k] = second[k] + (v * v).sum(0)
-            return tuple(first), tuple(second)
-
-        first, second = lax.fori_loop(0, width // 32, step, (tuple(first), tuple(second)))
+def input_sums_kernel(x_ref, out_ref):
+    lines, width, channels = x_ref.shape
     rows = channels // LANES
+
+    def step(r, carry):
+        first, second = list(carry[0]), list(carry[1])
+        for k in range(rows):
+            v = x_ref[r, :, k * LANES : (k + 1) * LANES].astype(F32).reshape(width // 8, 8, LANES)
+            first[k] = first[k] + v.sum(0)
+            second[k] = second[k] + (v * v).sum(0)
+        return tuple(first), tuple(second)
+
+    zero = tuple(jnp.zeros((8, LANES), F32) for _ in range(rows))
+    first, second = lax.fori_loop(0, lines, step, (zero, zero))
     for k in range(rows):
         out_ref[k : k + 1, :] = first[k].sum(0, keepdims=True)
         out_ref[rows + k : rows + k + 1, :] = second[k].sum(0, keepdims=True)
 
 
 def input_sums(x):
-    lines, width, channels = x.shape
+    channels = x.shape[2]
     return pl.pallas_call(
         input_sums_kernel,
         out_shape=jax.ShapeDtypeStruct((2 * channels // LANES, LANES), F32),
-        in_specs=[ANY],
+        in_specs=[VMEM],
         out_specs=VMEM,
-        scratch_shapes=[pltpu.VMEM(x.shape, BF16), pltpu.SemaphoreType.DMA((lines,))],
-        compiler_params=params(16),
+        compiler_params=params(6),
+        cost_estimate=cost(6e9),
         name="input_sums",
     )(x)
 
@@ -139,53 +137,43 @@
 
 
 def conv1_kernel(
-    meta, s0, s1, s2, s3, gain, shift, bias, x_hbm, up_hbm, low_hbm, w_hbm,
-    h_hbm, xp_ref, stats_ref,
-    xs, rowf, slots, wv, hv, sums, sems, wsem, hsem,
+    meta, s0, s1, s2, s3, gain, shift, bias, x_ref, up_ref, low_ref, w_hbm,
+    h_ref, xp_ref, stats_ref,
+    rowf, slots, wv, sums, wsem,
     *, count, per_group, n_blocks,
 ):
-    own = x_hbm.shape[0]
-    halo = up_hbm.shape[0]
-    lines, width, channels = xs.shape
+    own, width, channels = x_ref.shape
+    halo = up_ref.shape[0]
+    lines = own + 2 * halo
     half = width // 2
-    loads = [
-        pltpu.make_async_copy(up_hbm, xs.at[pl.ds(0, halo)], sems.at[0]),
-        pltpu.make_async_copy(x_hbm, xs.at[pl.ds(halo, own)], sems.at[1]),
-        pltpu.make_async_copy(low_hbm, xs.at[pl.ds(halo + own, halo)], sems.at[2]),
-    ]
-    for copy in loads:
-        copy.start()
     weight_load = pltpu.make_async_copy(w_hbm, wv, wsem)
     weight_load.start()
     scale, move = half_affine((s0, s1, s2, s3), channels // LANES, gain[...], shift[...], count, per_group)
     scale, move = as_row(scale), as_row(move)
-    for copy in loads:
-        copy.wait()
     first_line = meta[0] * own - halo
 
-    def norm(r, _):
-        line = first_line + r
+    def norm(source, at_line, r, keep):
+        line = first_line + at_line + r
         inside = (line >= 0) & (line < n_blocks * own)
         for at in range(0, channels, LANES):
             cols = slice(at, at + LANES)
             chunk = at // LANES
-            rowf[chunk] = xs[r, :, cols].astype(F32)
+            rowf[chunk] = source[r, :, cols].astype(F32)
             even = rowf[chunk, pl.ds(0, half, stride=2), :]
             odd = rowf[chunk, pl.ds(1, half, stride=2), :]
-            xp_ref[r, 0, :, cols] = even.astype(BF16)
-            xp_ref[r, 1, :, cols] = odd.astype(BF16)
+            if keep:
+                xp_ref[r, 0, :, cols] = even.astype(BF16)
+                xp_ref[r, 1, :, cols] = odd.astype(BF16)
             even = jnp.where(inside, half_silu(even, scale[:, cols], move[:, cols]), 0.0)
             odd = jnp.where(inside, half_silu(odd, scale[:, cols], move[:, cols]), 0.0)
-            spread_columns(slots, r, at, even, odd, channels)
-        return 0
-
-    lax.fori_loop(0, lines, norm, 0)
+            spread_columns(slots, at_line + r, at, even, odd, channels)
+
+    pl.loop(0, halo)(lambda r: norm(up_ref, 0, r, False))
+    pl.loop(0, own)(lambda r: norm(x_ref, halo, r, True))
+    pl.loop(0, halo)(lambda r: norm(low_ref, halo + own, r, False))
     weight_load.wait()
-    conv_rows(slots, wv, bias, hv, sums, lines - 2, halo - 1, own, half, channels, None)
-    store = pltpu.make_async_copy(hv, h_hbm, hsem)
-    store.start()
+    conv_rows(slots, wv, bias, h_ref, sums, lines - 2, halo - 1, own, half, channels, None)
     put_sums(stats_ref, sums[0:1, :], sums[1:2, :], channels // LANES)
-    store.wait()
 
 
 def conv1(meta, stats, gain, shift, bias, x, up, low, weight, n_blocks):
@@ -198,49 +186,38 @@
     return pl.pallas_call(
         functools.partial(conv1_kernel, count=count, per_group=channels // GROUPS, n_blocks=n_blocks),
         out_shape=(
-            jax.ShapeDtypeStruct((lines - 2, 2, half, channels), F32),
-            jax.ShapeDtypeStruct((lines, 2, half, channels), BF16),
+            pltpu.VMEM((lines - 2, 2, half, channels), F32),
+            pltpu.VMEM((own, 2, half, channels), BF16),
             jax.ShapeDtypeStruct((2 * rows, LANES), F32),
         ),
-        in_specs=[SMEM] + [VMEM] * 7 + [ANY] * 4,
-        out_specs=(ANY, VMEM, VMEM),
+        in_specs=[SMEM] + [VMEM] * 10 + [HBM],
+        out_specs=(VMEM, VMEM, VMEM),
         scratch_shapes=[
-            pltpu.VMEM((lines, width, channels), BF16),
             pltpu.VMEM((channels // LANES, width, LANES), F32),
             pltpu.VMEM((lines, half, 4 * channels), BF16),
             pltpu.VMEM((3, 3 * channels, channels), BF16),
-            pltpu.VMEM((lines - 2, 2, half, channels), F32),
             pltpu.VMEM((2, channels), F32),
-            pltpu.SemaphoreType.DMA((3,)),
-            pltpu.SemaphoreType.DMA,
             pltpu.SemaphoreType.DMA,
         ],
-        compiler_params=params(48),
+        compiler_params=params(26),
+        cost_estimate=cost(40e9),
         name="conv1",
     )(meta, *stats, gain.reshape(rows, LANES), shift.reshape(rows, LANES), bias.reshape(1, channels), x, up, low,
-      weight.reshape(3, 3 * channels, channels))
+      in_hbm(weight.reshape(3, 3 * channels, channels)))
 
 
 def conv2_kernel(
-    meta, s0, s1, s2, s3, gain, shift, bias, h_hbm, xp_hbm, w_hbm,
-    y_hbm, stats_ref,
-    hs, xs, slots, wv, yv, sums, sems, xsem, wsem, ysem,
+    meta, s0, s1, s2, s3, gain, shift, bias, hs, xs, w_hbm,
+    y_ref, stats_ref,
+    slots, wv, sums, wsem,
     *, count, per_group, n_blocks,
 ):
     lines, _, half, channels = hs.shape
     own = lines - 2
-    loads = [pltpu.make_async_copy(h_hbm.at[r], hs.at[r], sems.at[r]) for r in range(lines)]
-    for copy in loads:
-        copy.start()
     weight_load = pltpu.make_async_copy(w_hbm, wv, wsem)
     weight_load.start()
-    edge = (xp_hbm.shape[0] - own) // 2
-    x_load = pltpu.make_async_copy(xp_hbm.at[pl.ds(edge, own)], xs, xsem)
-    x_load.start()
     scale, move = half_affine((s0, s1, s2, s3), channels // LANES, gain[...], shift[...], count, per_group)
     scale, move = as_row(scale), as_row(move)
-    for copy in loads:
-        copy.wait()
     first_line = meta[0] * own - 1
 
     def norm(r, _):
@@ -254,13 +231,9 @@
         return 0
 
     lax.fori_loop(0, lines, norm, 0)
-    x_load.wait()
     weight_load.wait()
-    conv_rows(slots, wv, bias, yv, sums, own, 0, own, half, channels, xs)
-    store = pltpu.make_async_copy(yv, y_hbm, ysem)
-    store.start()
+    conv_rows(slots, wv, bias, y_ref, sums, own, 0, own, half, channels, xs)
     put_sums(stats_ref, sums[0:1, :], sums[1:2, :], channels // LANES)
-    store.wait()
 
 
 def conv2(meta, stats, gain, shift, bias, h, xp, weight, n_blocks):
@@ -271,27 +244,22 @@
     return pl.pallas_call(
         functools.partial(conv2_kernel, count=count, per_group=channels // GROUPS, n_blocks=n_blocks),
         out_shape=(
-            jax.ShapeDtypeStruct((own, 2, half, channels), F32),
+            pltpu.VMEM((own, 2, half, channels), F32),
             jax.ShapeDtypeStruct((2 * rows, LANES), F32),
         ),
-        in_specs=[SMEM] + [VMEM] * 7 + [ANY] * 3,
-        out_specs=(ANY, VMEM),
+        in_specs=[SMEM] + [VMEM] * 9 + [HBM],
+        out_specs=(VMEM, VMEM),
         scratch_shapes=[
-            pltpu.VMEM((lines, 2, half, channels), F32),
-            pltpu.VMEM((own, 2, half, channels), BF16),
             pltpu.VMEM((lines, half, 4 * channels), BF16),
             pltpu.VMEM((3, 3 * channels, channels), BF16),
-            pltpu.VMEM((own, 2, half, channels), F32),
             pltpu.VMEM((2, channels), F32),
-            pltpu.SemaphoreType.DMA((lines,)),
-            pltpu.SemaphoreType.DMA,
-            pltpu.SemaphoreType.DMA,
             pltpu.SemaphoreType.DMA,
         ],
-        compiler_params=params(48),
+        compiler_params=params(26),
+        cost_estimate=cost(30e9),
         name="conv2",
     )(meta, *stats, gain.reshape(rows, LANES), shift.reshape(rows, LANES), bias.reshape(1, channels), h, xp,
-      weight.reshape(3, 3 * channels, channels))
+      in_hbm(weight.reshape(3, 3 * channels, channels)))
 
 
 def column_shift(values, tap, half):
@@ -306,18 +274,13 @@
 
 
 def head_kernel(
-    meta, s0, s1, s2, s3, gain, shift, w_ref, q_ref, b_ref, y_hbm, part_ref, up_ref, low_ref, ys, act, sems,
+    meta, s0, s1, s2, s3, gain, shift, w_ref, b_ref, q_ref, qb_ref, ys, part_ref, up_ref, low_ref, act,
     *, count, per_group, n_blocks, n_send,
 ):
     own, _, half, channels = ys.shape
     width = 2 * half
-    loads = [pltpu.make_async_copy(y_hbm.at[r], ys.at[r], sems.at[r]) for r in range(own)]
-    for copy in loads:
-        copy.start()
     scale, move = half_affine((s0, s1, s2, s3), channels // LANES, gain[...], shift[...], count, per_group)
     scale, move = as_row(scale), as_row(move)
-    for copy in loads:
-        copy.wait()
 
     def norm(r, _):
         for parity in range(2):
@@ -347,9 +310,13 @@
     lane = lax.broadcasted_iota(jnp.int32, (1, size), 1)
     own_lane = (lane >= width) & (lane < (own + 1) * width)
     latents = []
-    for c in range(q_ref.shape[1]):
-        value = LATENT_SCALE * jnp.sum(total * q_ref[:, c : c + 1], axis=0, keepdims=True)
-        latents.append(value + jnp.where(own_lane, b_ref[c : c + 1, 0:1], 0.0))
+    for c in range(q_ref.shape[0]):
+        value, offset = None, qb_ref[c]
+        for o in range(moments_n):
+            term = total[o : o + 1, :] * q_ref[c, o]
+            value = term if value is None else value + term
+            offset = offset + b_ref[o] * q_ref[c, o]
+        latents.append(LATENT_SCALE * (value + jnp.where(own_lane, offset, 0.0)))
     latent = jnp.concatenate(latents, axis=0)
     keep = ((lane >= width) | (meta[0] > 0)) & ((lane < (own + 1) * width) | (meta[0] < n_blocks - 1))
     part_ref[...] = jnp.where(keep, latent, 0.0)
@@ -365,8 +332,6 @@
     count = float(n_blocks * own * width * (channels // GROUPS))
     size = -(-((own + 2) * width) // LANES) * LANES
     taps = weight.transpose(0, 1, 3, 2).reshape(9 * moments, channels)
-    offset = LATENT_SCALE * (jnp.sum(bias[:, None] * quant_weight, axis=0) + quant_bias)
-    offset = jnp.broadcast_to(offset[:, None], (latents, LANES))
     return pl.pallas_call(
         functools.partial(head_kernel, count=count, per_group=channels // GROUPS, n_blocks=n_blocks, n_send=n_send),
         out_shape=(
@@ -374,85 +339,73 @@
             jax.ShapeDtypeStruct((latents, n_send * width), F32),
             jax.ShapeDtypeStruct((latents, n_send * width), F32),
         ),
-        in_specs=[SMEM] + [VMEM] * 9 + [ANY],
+        in_specs=[SMEM] + [VMEM] * 7 + [SMEM] * 3 + [VMEM],
         out_specs=(VMEM, VMEM, VMEM),
-        scratch_shapes=[
-            pltpu.VMEM((own, 2, half, channels), F32),
-            pltpu.VMEM((own, 2, half, channels), BF16),
-            pltpu.SemaphoreType.DMA((own,)),
-        ],
-        compiler_params=params(32),
+        scratch_shapes=[pltpu.VMEM((own, 2, half, channels), BF16)],
+        compiler_params=params(12),
+        cost_estimate=cost(10e9),
         name="head",
-    )(meta, *stats, gain.reshape(rows, LANES), shift.reshape(rows, LANES), taps, quant_weight, offset, y)
-
-
-def lift_kernel(meta, w_ref, bias_ref, *refs, own, half, n_frames, n_out):
-    latents = refs[:n_frames]
-    t0_hbm, stats_ref, stack, patches, t0v, sem = refs[n_frames:]
+    )(meta, *stats, gain.reshape(rows, LANES), shift.reshape(rows, LANES), taps, bias, quant_weight.T, quant_bias, y)
+
+
+def lift_kernel(meta, w_ref, bias_ref, latents, t0_ref, stats_ref, stack, patches, weights, *, own, half, n_frames, n_out):
     width = 2 * half
     out_lines = own + 4
     pixels = out_lines * width
     depth, size = stack.shape
-    each = latents[0].shape[0]
-    for k in range(n_frames):
-        value = latents[k][...].astype(F32)
-        stack[k * each : (k + 1) * each, :] = jnp.where(meta[1] >= k, value, 0.0)
+    each = latents.shape[1]
+    channels = bias_ref.shape[1]
+    for s in range(n_frames):
+        frame = meta[1] - (n_frames - 1 - s)
+        value = latents[jnp.maximum(frame, 0)].astype(F32)
+        stack[s * each : (s + 1) * each, :] = jnp.where(frame >= 0, value, 0.0)
     frames = stack[...]
-    patches[...] = jnp.zeros_like(patches)
+    patches[9 * depth :, :] = jnp.zeros_like(patches[9 * depth :, :])
+    weights[...] = jnp.zeros_like(weights)
     for j in range(3):
         moved = frames if j == 1 else column_shift(frames, j, half)
         for i in range(3):
             piece = moved if i == 0 else pltpu.roll(moved, size - i * width, 1)
             at = (3 * i + j) * depth
             patches[at : at + depth, :] = piece[:, :pixels]
+            for t in range(3):
+                tap = w_ref[9 * t + 3 * i + j].astype(F32)
+                for g in range(n_out):
+                    row = at + (n_frames - 3 - g + t) * each
+                    weights[row : row + each, g * channels : (g + 1) * channels] = tap
     lhs = jnp.transpose(patches[...], (1, 0)).astype(BF16)
-    channels = bias_ref.shape[1]
     for g in range(n_out):
         cols = slice(g * channels, (g + 1) * channels)
-        value = jnp.dot(lhs, w_ref[:, cols], preferred_element_type=F32) + bias_ref[...]
-        t0v[:, cols] = value
+        value = jnp.dot(lhs, weights[:, cols].astype(BF16), preferred_element_type=F32) + bias_ref[...]
+        t0_ref[:, cols] = value
         mine = value[2 * width : (2 + own) * width]
         stats_ref[g : g + 1, :] = mine.sum(0, keepdims=True)
         stats_ref[n_out + g : n_out + g + 1, :] = (mine * mine).sum(0, keepdims=True)
-    store = pltpu.make_async_copy(t0v, t0_hbm, sem)
-    store.start()
-    store.wait()
-
-
-def lift_weights(weight, n_frames, n_out):
-    _, _, _, latents, channels = weight.shape
-    back = weight[::-1].transpose(1, 2, 0, 3, 4).reshape(9, 3 * latents, channels)
-    blocks = []
-    for g in range(n_out):
-        blocks.append(jnp.pad(back, ((0, 0), (g * latents, (n_frames - 3 - g) * latents), (0, 0))))
-    whole = jnp.concatenate(blocks, axis=2).reshape(9 * n_frames * latents, n_out * channels)
-    extra = -whole.shape[0] % 256
-    return jnp.pad(whole, ((0, extra), (0, 0)))
-
-
-def lift(meta, packed, bias, latents, own, half, n_out):
-    n_frames = len(latents)
-    each, size = latents[0].shape
+
+
+def lift(meta, weight, bias, latents, own, half, n_frames, n_out):
+    _, each, size = latents.shape
     channels = bias.shape[0]
     pixels = (own + 4) * 2 * half
     stat_rows = -(-2 * n_out // 8) * 8
+    depth = -(-9 * n_frames * each // 256) * 256
     return pl.pallas_call(
         functools.partial(lift_kernel, own=own, half=half, n_frames=n_frames, n_out=n_out),
         out_shape=(
-            jax.ShapeDtypeStruct((pixels, n_out * channels), F32),
+            pltpu.VMEM((pixels, n_out * channels), F32),
             jax.ShapeDtypeStruct((stat_rows, channels), F32),
         ),
-        in_specs=[SMEM] + [VMEM] * (2 + n_frames),
-        out_specs=(ANY, VMEM),
+        in_specs=[SMEM] + [VMEM] * 3,
+        out_specs=(VMEM, VMEM),
         scratch_shapes=[
             pltpu.VMEM((n_frames * each, size), F32),
-            pltpu.VMEM((packed.shape[0], pixels), F32),
-            pltpu.VMEM((pixels, n_out * channels), F32),
-            pltpu.SemaphoreType.DMA,
+            pltpu.VMEM((depth, pixels), F32),
+            pltpu.VMEM((depth, n_out * channels), F32),
         ],
-        compiler_params=params(32),
+        compiler_params=params(20),
+        cost_estimate=cost(8e9),
         name="lift",
-    )(meta, packed, bias.reshape(1, channels), *latents)
+    )(meta, weight.reshape(27, each, channels), bias.reshape(1, channels), latents)
 
 
 def pair_weight_copies(w_hbm, wv, sems, channels):
@@ -471,21 +424,17 @@
 
 
 def time1_kernel(
-    meta, s0, s1, s2, s3, gain, shift, t0_hbm, w_hbm, t1_hbm, stats_ref,
-    ts, slots, wv, t1v, sem, wsems, osem,
+    meta, s0, s1, s2, s3, gain, shift, ts, w_hbm, t1v, stats_ref, slots, wv, wsems,
     *, count, per_group, n_blocks, own, n_out,
 ):
     frames, lines, half, _ = slots.shape
     channels = gain.shape[1]
     width = 2 * half
-    load = pltpu.make_async_copy(t0_hbm, ts, sem)
-    load.start()
     weight_loads = pair_weight_copies(w_hbm, wv, wsems, channels)
     for copy in weight_loads:
         copy.start()
     clear_pair_weights(wv, channels)
     scale, move = half_affine((s0, s1, s2, s3), frames, gain[...], shift[...], count, per_group)
-    load.wait()
     first_line = meta[0] * own - 2
     for k in range(frames):
         cols = slice(k * channels, (k + 1) * channels)
@@ -518,9 +467,6 @@
         second = (mine * mine).sum(0, keepdims=True)
         stats_ref[k : k + 1, :] = first[:, :channels] + first[:, channels:]
         stats_ref[n_out + k : n_out + k + 1, :] = second[:, :channels] + second[:, channels:]
-    store = pltpu.make_async_copy(t1v, t1_hbm, osem)
-    store.start()
-    store.wait()
 
 
 def time1(meta, stats, gain, shift, t0, weight, n_blocks, own, half, n_frames, n_out):
@@ -532,45 +478,36 @@
             time1_kernel, count=count, per_group=channels // GROUPS, n_blocks=n_blocks, own=own, n_out=n_out
         ),
         out_shape=(
-            jax.ShapeDtypeStruct((n_out, lines - 2, half, 2 * channels), F32),
+            pltpu.VMEM((n_out, lines - 2, half, 2 * channels), F32),
             jax.ShapeDtypeStruct((-(-2 * n_out // 8) * 8, channels), F32),
         ),
-        in_specs=[SMEM] + [VMEM] * 6 + [ANY] * 2,
-        out_specs=(ANY, VMEM),
+        in_specs=[SMEM] + [VMEM] * 7 + [HBM],
+        out_specs=(VMEM, VMEM),
         scratch_shapes=[
-            pltpu.VMEM(t0.shape, F32),
             pltpu.VMEM((n_frames, lines, half, 4 * channels), BF16),
             pltpu.VMEM((9, 4 * channels, 2 * channels), BF16),
-            pltpu.VMEM((n_out, lines - 2, half, 2 * channels), F32),
-            pltpu.SemaphoreType.DMA,
             pltpu.SemaphoreType.DMA((6,)),
-            pltpu.SemaphoreType.DMA,
         ],
-        compiler_params=params(48),
+        compiler_params=params(26),
+        cost_estimate=cost(30e9),
         name="time1",
     )(meta, *stats, gain.reshape(1, channels), shift.reshape(1, channels), t0,
-      weight.reshape(9, 3, channels, channels))
+      in_hbm(weight.reshape(9, 3, channels, channels)))
 
 
 def time2_kernel(
-    meta, s0, s1, s2, s3, gain, shift, bias, t1_hbm, t0_hbm, w_hbm, out_hbm,
-    ts, t0s, slots, wv, rowf, outv, sem, t0sem, wsems, osem,
+    meta, s0, s1, s2, s3, gain, shift, bias, ts, t0s, w_hbm, outv, slots, wv, rowf, wsems,
     *, count, per_group, n_blocks,
 ):
     frames, lines, half, _ = slots.shape
     own = lines - 2
     channels = gain.shape[1]
     width = 2 * half
-    load = pltpu.make_async_copy(t1_hbm, ts, sem)
-    load.start()
     weight_loads = pair_weight_copies(w_hbm, wv, wsems, channels)
     for copy in weight_loads:
         copy.start()
-    t0_load = pltpu.make_async_copy(t0_hbm.at[pl.ds(2 * width, own * width), pl.ds(0, channels)], t0s, t0sem)
-    t0_load.start()
     clear_pair_weights(wv, channels)
     scale, move = half_affine((s0, s1, s2, s3), frames, gain[...], shift[...], count, per_group)
-    load.wait()
     first_line = meta[0] * own - 1
     for k in range(frames):
 
@@ -594,16 +531,12 @@
             part = jnp.dot(lhs, wv[3 * t + i], preferred_element_type=F32)
             acc = part if acc is None else acc + part
     acc = acc.reshape(own, half, 2 * channels)
-    t0_load.wait()
     for r in range(own):
         for parity in range(2):
-            at = r * width + parity * half
-            value = acc[r, :, parity * channels : (parity + 1) * channels] + bias[...] + t0s[at : at + half, :]
-            rowf[r, pl.ds(parity, half, stride=2), :] = value
-        outv[r] = rowf[r].astype(BF16)
-    store = pltpu.make_async_copy(outv, out_hbm.at[0], osem)
-    store.start()
-    store.wait()
+            at = (2 + r) * width + parity * half
+            value = acc[r, :, parity * channels : (parity + 1) * channels] + bias[...]
+            rowf[r, pl.ds(parity, half, stride=2), :] = value + t0s[at : at + half, 0:channels]
+        outv[0, r] = rowf[r].astype(BF16)
 
 
 def time2(meta, stats, gain, shift, bias, t1, t0, weight, n_blocks):
@@ -614,24 +547,19 @@
     return pl.pallas_call(
         functools.partial(time2_kernel, count=count, per_group=channels // GROUPS, n_blocks=n_blocks),
         out_shape=jax.ShapeDtypeStruct((1, own, 2 * half, channels), BF16),
-        in_specs=[SMEM] + [VMEM] * 7 + [ANY] * 3,
-        out_specs=ANY,
+        in_specs=[SMEM] + [VMEM] * 9 + [HBM],
+        out_specs=VMEM,
         scratch_shapes=[
-            pltpu.VMEM(t1.shape, F32),
-            pltpu.VMEM((own * 2 * half, channels), F32),
             pltpu.VMEM((frames, lines, half, 4 * channels), BF16),
             pltpu.VMEM((9, 4 * channels, 2 * channels), BF16),
             pltpu.VMEM((own, 2 * half, channels), F32),
-            pltpu.VMEM((own, 2 * half, channels), BF16),
-            pltpu.SemaphoreType.DMA,
-            pltpu.SemaphoreType.DMA,
             pltpu.SemaphoreType.DMA((6,)),
-            pltpu.SemaphoreType.DMA,
         ],
-        compiler_params=params(48),
+        compiler_params=params(24),
+        cost_estimate=cost(12e9),
         name="time2",
     )(meta, *stats, gain.reshape(1, channels), shift.reshape(1, channels), bias.reshape(1, channels), t1, t0,
-      weight.reshape(9, 3, channels, channels))
+      in_hbm(weight.reshape(9, 3, channels, channels)))
 
 
 def turned(block, axis, distance):
@@ -672,13 +600,9 @@
         + jnp.pad(above, ((0, 0), (0, size - 4 * width)))
         + jnp.pad(below, ((0, 0), ((own + 2) * width, size - (own + 6) * width)))
     ).astype(BF16)
-    near = jnp.concatenate([latent, turned(latent, "frames", 1), turned(latent, "frames", 2)], axis=0)
-    far = turned(near, "frames", 3)
-    farther = turned(near, "frames", 4)
-    each = latent.shape[0]
-    latents = [near[k * each : (k + 1) * each] for k in range(3)] + [far[k * each : (k + 1) * each] for k in range(3)]
-    latents.append(farther[2 * each : 3 * each])
-    t0, sums = lift(meta, lift_weights(time_in_weight, 7, 5), time_in_bias, latents, own, half, 5)
+    n_frames = lax.axis_size("frames")
+    latents = lax.all_to_all(jnp.broadcast_to(latent[None], (n_frames,) + latent.shape), "frames", 0, 0)
+    t0, sums = lift(meta, time_in_weight, time_in_bias, latents, own, half, 7, 5)
     t1, sums = time1(meta, from_all(sums), tnorm1_gain, tnorm1_shift, t0, time1_weight, n_blocks, own, half, 5, 3)
     return time2(meta, from_all(sums), tnorm2_gain, tnorm2_shift, time2_bias, t1, t0, time2_weight, n_blocks)
 

time: 113 us -> 88.3 us (0.78)
  blocking collectives: 0 us -> 13.7 us
  local copies, waits for them, and re-layouts: 15.8 us -> 2.58 us
  Pallas kernels: 50.1 us -> 39.9 us
  starting transfers between devices: 22.8 us -> 12.9 us
  waiting for transfers between devices: 23.5 us -> 18.5 us
    all_to_all x0 -> x1, blocking collectives: none -> 13.7 us  [body(): lax.all_to_all(jnp.broadcast_to(latent[None], (n_frames,) + latent.shape)...]
    unnamed x63 -> x42, local copies, waits for them, and re-layouts: 13.1 us -> 1.43 us
    ppermute x23 -> x19, starting transfers between devices: 22.8 us -> 12.9 us  [turned(): lax.ppermute(block, axis, [(i, (i + distance) % count) for i in range(cou...]
    ppermute x23 -> x19, waiting for transfers between devices: 23.5 us -> 18.5 us  [turned(): lax.ppermute(block, axis, [(i, (i + distance) % count) for i in range(cou...]
    pallas_call x1, Pallas kernels: 11.5 us -> 8.98 us  [time1(): pl.pallas_call(functools.partial(time1_kernel, count=count, per_group=cha...]
    pallas_call x1, Pallas kernels: 13.2 us -> 11.2 us  [conv1(): pl.pallas_call(functools.partial(conv1_kernel, count=count, per_group=cha...]
    pallas_call x1, Pallas kernels: 2.37 us -> 0.47 us  [input_sums(): pl.pallas_call(input_sums_kernel, out_shape=jax.ShapeDtypeStruct((2 * cha...]
    concatenate x1 -> x0, local copies, waits for them, and re-layouts: 1.42 us -> none  [lift_weights(): jnp.concatenate(blocks, axis=2)]
  transfers between devices with their start and end apart: 23 -> 19, of which waited for: 16 -> 12; matrix products, arithmetic and copies ran while one was open for 6% -> 0% of each run, Pallas kernels for 0% -> 1%
where the time goes in v1:
time: 88.3 us; the launch traced here: 88 us
  Pallas kernels  39.9 us (45%)
  waiting for transfers between devices  18.5 us (21%)
  blocking collectives  13.7 us (16%)
  starting transfers between devices  12.9 us (15%)
  local copies, waits for them, and re-layouts  2.58 us (3%)
    ppermute x19, waiting for transfers between devices, turned(): lax.ppermute(block, axis, [(i, (i + distance) % count) for i in range(cou...  18.5 us
    all_to_all x1, blocking collectives, body(): lax.all_to_all(jnp.broadcast_to(latent[None], (n_frames,) + latent.shape)...  13.7 us
    ppermute x19, starting transfers between devices, turned(): lax.ppermute(block, axis, [(i, (i + distance) % count) for i in range(cou...  12.9 us
    pallas_call x1, Pallas kernels, conv1(): pl.pallas_call(functools.partial(conv1_kernel, count=count, per_group=cha...  11.2 us
    pallas_call x1, Pallas kernels, conv2(): pl.pallas_call(functools.partial(conv2_kernel, count=count, per_group=cha...  9.75 us
    pallas_call x1, Pallas kernels, time1(): pl.pallas_call(functools.partial(time1_kernel, count=count, per_group=cha...  8.98 us
    pallas_call x1, Pallas kernels, time2(): pl.pallas_call(functools.partial(time2_kernel, count=count, per_group=cha...  4.5 us
    pallas_call x1, Pallas kernels, lift(): pl.pallas_call(functools.partial(lift_kernel, own=own, half=half, n_frame...  2.7 us
  transfers between devices with their start and end apart: 19, of which 12 were waited for; matrix products, arithmetic and copies ran while one was open for 0% of the time, Pallas kernels for 1%

profile of v1, /device:TPU:0, one launch (start us, length us, event | category | flops | bytes accessed | tf_op | source)
XLA Modules:
  0.0 88.0 jit_solution(5529137961542373256)
XLA Ops:
  0.0 1.1 %slice_bitcast_fusion = (bf16[2,160,512]{2,1,0:T(8,128)(2,1)S(1)}, bf16[2,160,512]{2,1,0:T(8,128)(2,1)S(1)}) fusion(bf16[1,8,160,512]{3,2,1,0:T(8,128)(2,1)} %param.24), kind=kLoop, calls=%fused_computation | loop fusion | bytes 1310720 | tf_op jit(solution)/shard_map/slice | solution.py:585
  1.1 2.5 %collective-permute-start.4 = (bf16[2,160,512]{2,1,0:T(8,128)(2,1)S(1)}, bf16[2,160,512]{2,1,0:T(8,128)(2,1)S(1)}, u32[]{:S(2)}, u32[]{:S(2)}) collective-permute-start(bf16[2,160,512]{2,1,0:T(8,128)(2,1)S(1)} %get-tuple-element.29), channel_id=1, source_target_pairs={{0,3},{1,0},{2,1},{3,2},{4,7},{5,4},{6,5},{7,6},{8,11},{9,8},{10,9... | collective-permute-start | bytes 983048 | tf_op jit(solution)/shard_map/ppermute | solution.py:567
  3.6 0.0 collective-permute-start.3
  3.6 1.3 %copy-done = bf16[1,8,160,512]{3,2,1,0:T(8,128)(2,1)S(1)} copy-done((bf16[1,8,160,512]{3,2,1,0:T(8,128)(2,1)S(1)}, bf16[1,8,160,512]{3,2,1,0:T(8,128)(2,1)}, u32[]{:S(2)}) %copy-start) | copy-done | bytes 1310744
  4.9 0.5 input_sums.1.s0
  5.4 1.8 %collective-permute-start.2 = (f32[8,128]{1,0:T(8,128)S(1)}, f32[8,128]{1,0:T(8,128)S(1)}, u32[]{:S(2)}, u32[]{:S(2)}) collective-permute-start(f32[8,128]{1,0:T(8,128)S(1)} %input_sums.1.s0), channel_id=1, source_target_pairs={{0,3},{1,0},{2,1},{3,2},{4,7},{5,4},{6,5},{7,6},{8,11},{9,8},{10,9... | collective-permute-start | bytes 12296 | tf_op jit(solution)/shard_map/ppermute | solution.py:567
  7.2 0.6 collective-permute-start.1
  7.8 0.0 collective-permute-start
  7.8 0.1 pad_add_fusion.meta
  7.9 3.8 %collective-permute-done.2.s3 = f32[8,128]{1,0:T(8,128)S(1)} collective-permute-done((f32[8,128]{1,0:T(8,128)S(1)}, f32[8,128]{1,0:T(8,128)S(1)}, u32[]{:S(2)}, u32[]{:S(2)}) %collective-permute-start.2) | collective-permute-done | bytes 4128 | tf_op jit(solution)/shard_map/ppermute | solution.py:567
  11.7 0.3 collective-permute-done.1.s2
  12.0 0.9 %collective-permute-done.s1 = f32[8,128]{1,0:T(8,128)S(1)} collective-permute-done((f32[8,128]{1,0:T(8,128)S(1)}, f32[8,128]{1,0:T(8,128)S(1)}, u32[]{:S(2)}, u32[]{:S(2)}) %collective-permute-start) | collective-permute-done | bytes 4128 | tf_op jit(solution)/shard_map/ppermute | solution.py:567
  12.9 0.0 collective-permute-done.4.low_ref
  12.9 0.0 collective-permute-done.3.up_ref
  12.9 0.0 copy-start.7
  13.0 0.0 copy-start.8
  13.0 0.0 copy-start.9
  13.0 11.2 %conv1.1 = (f32[10,2,80,512]{3,2,1,0:T(8,128)S(1)}, bf16[8,2,80,512]{3,2,1,0:T(8,128)(2,1)S(1)}, f32[8,128]{1,0:T(8,128)S(1)}) custom-call(s32[2]{0:T(128)S(1)} %pad_add_fusion.meta, f32[8,128]{1,0:T(8,128)S(1)} %input_sums.1.s0, f32[8,128]{1,0:T(8,128)S(1)} %collective-permute-done.s1, f32[8,128]{1,0:T(8,128)S(1)} %collective-permute-done.1.s2, ...), custom_call_target="tpu_custom_call" | custom-call | flops 40000000000 | tf_op jit(solution)/shard_map/conv1/pallas_call | solution.py:186
  24.2 1.2 %collective-permute-start.7 = (f32[8,128]{1,0:T(8,128)S(1)}, f32[8,128]{1,0:T(8,128)S(1)}, u32[]{:S(2)}, u32[]{:S(2)}) collective-permute-start(f32[8,128]{1,0:T(8,128)S(1)} %get-tuple-element.17.s0), channel_id=1, source_target_pairs={{0,3},{1,0},{2,1},{3,2},{4,7},{5,4},{6,5},{7,6},{8,11},{9,8},{10,9... | collective-permute-start | bytes 12296 | tf_op jit(solution)/shard_map/ppermute | solution.py:567
  25.4 0.5 collective-permute-start.6
  25.9 0.0 collective-permute-start.5
  25.9 0.8 collective-permute-done.7.s3
  26.7 2.3 %collective-permute-done.6.s2 = f32[8,128]{1,0:T(8,128)S(1)} collective-permute-done((f32[8,128]{1,0:T(8,128)S(1)}, f32[8,128]{1,0:T(8,128)S(1)}, u32[]{:S(2)}, u32[]{:S(2)}) %collective-permute-start.6) | collective-permute-done | bytes 4128 | tf_op jit(solution)/shard_map/ppermute | solution.py:567
  29.0 0.0 collective-permute-done.5.s1
  29.0 0.0 copy-start.2
  29.0 0.0 copy-start.10
  29.0 0.0 copy-start.11
  29.1 0.0 copy-start.12
  29.1 0.0 copy-start.13
  29.1 0.0 copy-start.14
  29.1 9.7 %conv2.1 = (f32[8,2,80,512]{3,2,1,0:T(8,128)S(1)}, f32[8,128]{1,0:T(8,128)S(1)}) custom-call(s32[2]{0:T(128)S(1)} %pad_add_fusion.meta, f32[8,128]{1,0:T(8,128)S(1)} %get-tuple-element.17.s0, f32[8,128]{1,0:T(8,128)S(1)} %collective-permute-done.5.s1, f32[8,128]{1,0:T(8,128)S(1)} %collective-permute-done.6.s2, f32[8,128]{1,0:T(8,128)S(1)} %collective-permute-done.7.s3, ...), custom_call_target="tpu_custom_call" | custom-call | flops 30000001024 | tf_op jit(solution)/shard_map/conv2/pallas_call | solution.py:244
  38.8 0.1 collective-permute-start.10
  38.9 1.5 %collective-permute-start.9 = (f32[8,128]{1,0:T(8,128)S(1)}, f32[8,128]{1,0:T(8,128)S(1)}, u32[]{:S(2)}, u32[]{:S(2)}) collective-permute-start(f32[8,128]{1,0:T(8,128)S(1)} %get-tuple-element.20.s0), channel_id=1, source_target_pairs={{0,2},{1,3},{2,0},{3,1},{4,6},{5,7},{6,4},{7,5},{8,10},{9,11},{10,... | collective-permute-start | bytes 12296 | tf_op jit(solution)/shard_map/ppermute | solution.py:567
  40.4 0.2 collective-permute-start.8
  40.6 0.0 collective-permute-done.10.s3
  40.6 2.0 %collective-permute-done.9.s2 = f32[8,128]{1,0:T(8,128)S(1)} collective-permute-done((f32[8,128]{1,0:T(8,128)S(1)}, f32[8,128]{1,0:T(8,128)S(1)}, u32[]{:S(2)}, u32[]{:S(2)}) %collective-permute-start.9) | collective-permute-done | bytes 4128 | tf_op jit(solution)/shard_map/ppermute | solution.py:567
  42.6 0.9 collective-permute-done.8.s1
  43.5 0.0 copy-start.3
  43.5 0.0 copy-start.15
  43.5 2.3 %head.1 = (f32[4,1664]{1,0:T(4,128)S(1)}, f32[4,640]{1,0:T(4,128)S(1)}, f32[4,640]{1,0:T(4,128)S(1)}) custom-call(s32[2]{0:T(128)S(1)} %pad_add_fusion.meta, f32[8,128]{1,0:T(8,128)S(1)} %get-tuple-element.20.s0, f32[8,128]{1,0:T(8,128)S(1)} %collective-permute-done.8.s1, f32[8,128]{1,0:T(8,128)S(1)} %collective-permute-done.9.s2, ...), custom_call_target="tpu_custom_call" | custom-call | flops 10000000000 | tf_op jit(solution)/shard_map/head/pallas_call | solution.py:335
  45.9 0.1 collective-permute-start.11
  45.9 1.7 %collective-permute-start.12 = (f32[4,640]{1,0:T(4,128)S(1)}, f32[4,640]{1,0:T(4,128)S(1)}, u32[]{:S(2)}, u32[]{:S(2)}) collective-permute-start(f32[4,640]{1,0:T(4,128)S(1)} %get-tuple-element.24), channel_id=1, source_target_pairs={{0,3},{1,0},{2,1},{3,2},{4,7},{5,4},{6,5},{7,6},{8,11},{9,8},{10,9... | collective-permute-start | bytes 30728 | tf_op jit(solution)/shard_map/ppermute | solution.py:567
  47.7 1.4 %collective-permute-done.11 = f32[4,640]{1,0:T(4,128)S(1)} collective-permute-done((f32[4,640]{1,0:T(4,128)S(1)}, f32[4,640]{1,0:T(4,128)S(1)}, u32[]{:S(2)}, u32[]{:S(2)}) %collective-permute-start.11) | collective-permute-done | bytes 10272 | tf_op jit(solution)/shard_map/ppermute | solution.py:567
  49.0 0.0 collective-permute-done.12
  49.1 0.1 fusion.2
  49.2 13.7 %all_to_all.5.latents = bf16[8,4,2304]{2,1,0:T(4,128)(2,1)S(1)} all-to-all(bf16[8,4,2304]{2,1,0:T(4,128)(2,1)S(1)} %broadcast_in_dim.12), channel_id=1, replica_groups=mesh['frames'=8,'rows'=4] {'frames'}, dimensions={0} | all-to-all | bytes 294912 | tf_op jit(solution)/shard_map/all_to_all | solution.py:604
  62.9 2.7 %lift.1 = (f32[1920,640]{1,0:T(8,128)S(1)}, f32[16,128]{1,0:T(8,128)S(1)}) custom-call(s32[2]{0:T(128)S(1)} %pad_add_fusion.meta, bf16[27,4,128]{2,1,0:T(4,128)(2,1)S(1)} %bitcast.33, f32[1,128]{1,0:T(1,128)S(1)} %bitcast.43, bf16[8,4,2304]{2,1,0:T(4,128)(2,1)S(1)} %all_to_all.5.latents), custom_call_target="tpu_custom_call" | custom-call | flops 8000000000 | tf_op jit(solution)/shard_map/lift/pallas_call | solution.py:392
  65.6 0.6 collective-permute-start.15
  66.3 0.2 collective-permute-start.14
  66.5 0.2 collective-permute-start.13
  66.6 1.0 %collective-permute-done.15.s3 = f32[16,128]{1,0:T(8,128)S(1)} collective-permute-done((f32[16,128]{1,0:T(8,128)S(1)}, f32[16,128]{1,0:T(8,128)S(1)}, u32[]{:S(2)}, u32[]{:S(2)}) %collective-permute-start.15) | collective-permute-done | bytes 8224 | tf_op jit(solution)/shard_map/ppermute | solution.py:567
  67.6 2.3 %collective-permute-done.14.s2 = f32[16,128]{1,0:T(8,128)S(1)} collective-permute-done((f32[16,128]{1,0:T(8,128)S(1)}, f32[16,128]{1,0:T(8,128)S(1)}, u32[]{:S(2)}, u32[]{:S(2)}) %collective-permute-start.14) | collective-permute-done | bytes 8224 | tf_op jit(solution)/shard_map/ppermute | solution.py:567
  69.9 0.0 collective-permute-done.13.s1
  69.9 0.0 copy-start.18
  69.9 0.0 copy-start.19
  69.9 0.0 copy-start.20
  70.0 9.0 %time1.1 = (f32[3,10,80,256]{3,2,1,0:T(8,128)S(1)}, f32[8,128]{1,0:T(8,128)S(1)}) custom-call(s32[2]{0:T(128)S(1)} %pad_add_fusion.meta, f32[16,128]{1,0:T(8,128)S(1)} %get-tuple-element.25.s0, f32[16,128]{1,0:T(8,128)S(1)} %collective-permute-done.13.s1, f32[16,128]{1,0:T(8,128)S(1)} %collective-permute-done.14.s2, ...), custom_call_target="tpu_custom_call" | custom-call | flops 30000001024 | tf_op jit(solution)/shard_map/time1/pallas_call | solution.py:476
  78.9 0.1 collective-permute-start.18
  79.0 1.5 %collective-permute-start.17 = (f32[8,128]{1,0:T(8,128)S(1)}, f32[8,128]{1,0:T(8,128)S(1)}, u32[]{:S(2)}, u32[]{:S(2)}) collective-permute-start(f32[8,128]{1,0:T(8,128)S(1)} %get-tuple-element.27.s0), channel_id=1, source_target_pairs={{0,2},{1,3},{2,0},{3,1},{4,6},{5,7},{6,4},{7,5},{8,10},{9,11},{10,... | collective-permute-start | bytes 12296 | tf_op jit(solution)/shard_map/ppermute | solution.py:567
  80.5 0.2 collective-permute-start.16
  80.7 0.0 collective-permute-done.18.s3
  80.7 2.0 %collective-permute-done.17.s2 = f32[8,128]{1,0:T(8,128)S(1)} collective-permute-done((f32[8,128]{1,0:T(8,128)S(1)}, f32[8,128]{1,0:T(8,128)S(1)}, u32[]{:S(2)}, u32[]{:S(2)}) %collective-permute-start.17) | collective-permute-done | bytes 4128 | tf_op jit(solution)/shard_map/ppermute | solution.py:567
  82.7 0.9 collective-permute-done.16.s1
  83.5 4.5 %time2.1 = bf16[1,8,160,128]{3,2,1,0:T(8,128)(2,1)} custom-call(s32[2]{0:T(128)S(1)} %pad_add_fusion.meta, f32[8,128]{1,0:T(8,128)S(1)} %get-tuple-element.27.s0, f32[8,128]{1,0:T(8,128)S(1)} %collective-permute-done.16.s1, f32[8,128]{1,0:T(8,128)S(1)} %collective-permute-done.17.s2, f32[8,128]{1,0:T(8,128)S(1)} %collective-permute-done.18.s3, ...), custom_call_target="tpu_custom_call" | custom-call | flops 12000000000 | tf_op jit(solution)/shard_map/time2/pallas_call | solution.py:547
  (30 shorter events, 0.1 us)
Async XLA Ops:
  1.1 11.8 %collective-permute-start.4 = (bf16[2,160,512]{2,1,0:T(8,128)(2,1)S(1)}, bf16[2,160,512]{2,1,0:T(8,128)(2,1)S(1)}, u32[]{:S(2)}, u32[]{:S(2)}) collective-permute-start(bf16[2,160,512]{2,1,0:T(8,128)(2,1)S(1)} %get-tuple-element.29), channel_id=1, source_target_pairs={{0,3},{1,0},{2,1},{3,2},{4,7},{5,4},{6,5},{7,6},{8,11},{9,8},{10,9... | collective-permute-start | bytes 983048 | tf_op jit(solution)/shard_map/ppermute | solution.py:567
  3.6 9.3 %collective-permute-start.3 = (bf16[2,160,512]{2,1,0:T(8,128)(2,1)S(1)}, bf16[2,160,512]{2,1,0:T(8,128)(2,1)S(1)}, u32[]{:S(2)}, u32[]{:S(2)}) collective-permute-start(bf16[2,160,512]{2,1,0:T(8,128)(2,1)S(1)} %get-tuple-element.30), channel_id=1, source_target_pairs={{0,1},{1,2},{2,3},{3,0},{4,5},{5,6},{6,7},{7,4},{8,9},{9,10},{10,1... | collective-permute-start | bytes 983048 | tf_op jit(solution)/shard_map/ppermute | solution.py:567
  3.6 1.3 %copy-start = (bf16[1,8,160,512]{3,2,1,0:T(8,128)(2,1)S(1)}, bf16[1,8,160,512]{3,2,1,0:T(8,128)(2,1)}, u32[]{:S(2)}) copy-start(bf16[1,8,160,512]{3,2,1,0:T(8,128)(2,1)} %param.24) | copy-start | bytes 3932164
  4.9 8.0 %copy-start.1 = (bf16[1,8,160,512]{3,2,1,0:T(8,128)(2,1)S(1)}, bf16[1,8,160,512]{3,2,1,0:T(8,128)(2,1)}, u32[]{:S(2)}) copy-start(bf16[1,8,160,512]{3,2,1,0:T(8,128)(2,1)} %param.24) | copy-start | bytes 3932164
  4.9 8.0 %copy-start.4 = (f32[512]{0:T(512)S(1)}, f32[512]{0:T(512)}, u32[]{:S(2)}) copy-start(f32[512]{0:T(512)} %param.25) | copy-start | bytes 6148
  4.9 8.0 %copy-start.5 = (f32[512]{0:T(512)S(1)}, f32[512]{0:T(512)}, u32[]{:S(2)}) copy-start(f32[512]{0:T(512)} %param.26) | copy-start | bytes 6148
  4.9 8.0 %copy-start.6 = (f32[512]{0:T(512)S(1)}, f32[512]{0:T(512)}, u32[]{:S(2)}) copy-start(f32[512]{0:T(512)} %param.28) | copy-start | bytes 6148
  5.4 6.3 %collective-permute-start.2 = (f32[8,128]{1,0:T(8,128)S(1)}, f32[8,128]{1,0:T(8,128)S(1)}, u32[]{:S(2)}, u32[]{:S(2)}) collective-permute-start(f32[8,128]{1,0:T(8,128)S(1)} %input_sums.1.s0), channel_id=1, source_target_pairs={{0,3},{1,0},{2,1},{3,2},{4,7},{5,4},{6,5},{7,6},{8,11},{9,8},{10,9... | collective-permute-start | bytes 12296 | tf_op jit(solution)/shard_map/ppermute | solution.py:567
  7.2 4.8 %collective-permute-start.1 = (f32[8,128]{1,0:T(8,128)S(1)}, f32[8,128]{1,0:T(8,128)S(1)}, u32[]{:S(2)}, u32[]{:S(2)}) collective-permute-start(f32[8,128]{1,0:T(8,128)S(1)} %input_sums.1.s0), channel_id=1, source_target_pairs={{0,2},{1,3},{2,0},{3,1},{4,6},{5,7},{6,4},{7,5},{8,10},{9,11},{10,... | collective-permute-start | bytes 12296 | tf_op jit(solution)/shard_map/ppermute | solution.py:567
  7.8 5.1 %collective-permute-start = (f32[8,128]{1,0:T(8,128)S(1)}, f32[8,128]{1,0:T(8,128)S(1)}, u32[]{:S(2)}, u32[]{:S(2)}) collective-permute-start(f32[8,128]{1,0:T(8,128)S(1)} %input_sums.1.s0), channel_id=1, source_target_pairs={{0,1},{1,2},{2,3},{3,0},{4,5},{5,6},{6,7},{7,4},{8,9},{9,10},{10,1... | collective-permute-start | bytes 12296 | tf_op jit(solution)/shard_map/ppermute | solution.py:567
  12.9 16.1 %copy-start.7 = (f32[512]{0:T(512)S(1)}, f32[512]{0:T(512)}, u32[]{:S(2)}) copy-start(f32[512]{0:T(512)} %param.29) | copy-start | bytes 6148
  13.0 16.0 %copy-start.8 = (f32[512]{0:T(512)S(1)}, f32[512]{0:T(512)}, u32[]{:S(2)}) copy-start(f32[512]{0:T(512)} %param.30) | copy-start | bytes 6148
  13.0 16.0 %copy-start.9 = (f32[512]{0:T(512)S(1)}, f32[512]{0:T(512)}, u32[]{:S(2)}) copy-start(f32[512]{0:T(512)} %param.32) | copy-start | bytes 6148
  24.2 2.5 %collective-permute-start.7 = (f32[8,128]{1,0:T(8,128)S(1)}, f32[8,128]{1,0:T(8,128)S(1)}, u32[]{:S(2)}, u32[]{:S(2)}) collective-permute-start(f32[8,128]{1,0:T(8,128)S(1)} %get-tuple-element.17.s0), channel_id=1, source_target_pairs={{0,3},{1,0},{2,1},{3,2},{4,7},{5,4},{6,5},{7,6},{8,11},{9,8},{10,9... | collective-permute-start | bytes 12296 | tf_op jit(solution)/shard_map/ppermute | solution.py:567
  25.4 3.6 %collective-permute-start.6 = (f32[8,128]{1,0:T(8,128)S(1)}, f32[8,128]{1,0:T(8,128)S(1)}, u32[]{:S(2)}, u32[]{:S(2)}) collective-permute-start(f32[8,128]{1,0:T(8,128)S(1)} %get-tuple-element.17.s0), channel_id=1, source_target_pairs={{0,2},{1,3},{2,0},{3,1},{4,6},{5,7},{6,4},{7,5},{8,10},{9,11},{10,... | collective-permute-start | bytes 12296 | tf_op jit(solution)/shard_map/ppermute | solution.py:567
  25.9 3.1 %collective-permute-start.5 = (f32[8,128]{1,0:T(8,128)S(1)}, f32[8,128]{1,0:T(8,128)S(1)}, u32[]{:S(2)}, u32[]{:S(2)}) collective-permute-start(f32[8,128]{1,0:T(8,128)S(1)} %get-tuple-element.17.s0), channel_id=1, source_target_pairs={{0,1},{1,2},{2,3},{3,0},{4,5},{5,6},{6,7},{7,4},{8,9},{9,10},{10,1... | collective-permute-start | bytes 12296 | tf_op jit(solution)/shard_map/ppermute | solution.py:567
  29.0 14.4 %copy-start.2 = (bf16[3,3,512,8]{2,3,1,0:T(8,128)(2,1)S(1)}, bf16[3,3,512,8]{2,3,1,0:T(8,128)(2,1)}, u32[]{:S(2)}) copy-start(bf16[3,3,512,8]{2,3,1,0:T(8,128)(2,1)} %param.35) | copy-start | bytes 221188
  29.0 14.4 %copy-start.10 = (f32[512]{0:T(512)S(1)}, f32[512]{0:T(512)}, u32[]{:S(2)}) copy-start(f32[512]{0:T(512)} %param.33) | copy-start | bytes 6148
  29.0 14.4 %copy-start.11 = (f32[512]{0:T(512)S(1)}, f32[512]{0:T(512)}, u32[]{:S(2)}) copy-start(f32[512]{0:T(512)} %param.34) | copy-start | bytes 6148
  29.1 14.4 %copy-start.12 = (f32[8,4]{0,1:T(4,128)S(1)}, f32[8,4]{0,1:T(4,128)}, u32[]{:S(2)}) copy-start(f32[8,4]{0,1:T(4,128)} %param.37) | copy-start | bytes 388
  29.1 14.4 %copy-start.13 = (f32[8]{0:T(128)S(1)}, f32[8]{0:T(128)}, u32[]{:S(2)}) copy-start(f32[8]{0:T(128)} %b_ref.1) | copy-start | bytes 100
  29.1 14.4 %copy-start.14 = (f32[4]{0:T(128)S(1)}, f32[4]{0:T(128)}, u32[]{:S(2)}) copy-start(f32[4]{0:T(128)} %qb_ref.1) | copy-start | bytes 52
  38.8 1.7 %collective-permute-start.10 = (f32[8,128]{1,0:T(8,128)S(1)}, f32[8,128]{1,0:T(8,128)S(1)}, u32[]{:S(2)}, u32[]{:S(2)}) collective-permute-start(f32[8,128]{1,0:T(8,128)S(1)} %get-tuple-element.20.s0), channel_id=1, source_target_pairs={{0,3},{1,0},{2,1},{3,2},{4,7},{5,4},{6,5},{7,6},{8,11},{9,8},{10,9... | collective-permute-start | bytes 12296 | tf_op jit(solution)/shard_map/ppermute | solution.py:567
  38.9 3.7 %collective-permute-start.9 = (f32[8,128]{1,0:T(8,128)S(1)}, f32[8,128]{1,0:T(8,128)S(1)}, u32[]{:S(2)}, u32[]{:S(2)}) collective-permute-start(f32[8,128]{1,0:T(8,128)S(1)} %get-tuple-element.20.s0), channel_id=1, source_target_pairs={{0,2},{1,3},{2,0},{3,1},{4,6},{5,7},{6,4},{7,5},{8,10},{9,11},{10,... | collective-permute-start | bytes 12296 | tf_op jit(solution)/shard_map/ppermute | solution.py:567
  40.4 3.0 %collective-permute-start.8 = (f32[8,128]{1,0:T(8,128)S(1)}, f32[8,128]{1,0:T(8,128)S(1)}, u32[]{:S(2)}, u32[]{:S(2)}) collective-permute-start(f32[8,128]{1,0:T(8,128)S(1)} %get-tuple-element.20.s0), channel_id=1, source_target_pairs={{0,1},{1,2},{2,3},{3,0},{4,5},{5,6},{6,7},{7,4},{8,9},{9,10},{10,1... | collective-permute-start | bytes 12296 | tf_op jit(solution)/shard_map/ppermute | solution.py:567
  43.5 19.4 %copy-start.3 = (bf16[3,3,3,4,128]{4,3,2,1,0:T(4,128)(2,1)S(1)}, bf16[3,3,3,4,128]{4,3,2,1,0:T(4,128)(2,1)}, u32[]{:S(2)}) copy-start(bf16[3,3,3,4,128]{4,3,2,1,0:T(4,128)(2,1)} %param.39) | copy-start | bytes 82948
  43.5 19.4 %copy-start.15 = (f32[128]{0:T(128)S(1)}, f32[128]{0:T(128)}, u32[]{:S(2)}) copy-start(f32[128]{0:T(128)} %param.40) | copy-start | bytes 1540
  45.9 3.2 %collective-permute-start.11 = (f32[4,640]{1,0:T(4,128)S(1)}, f32[4,640]{1,0:T(4,128)S(1)}, u32[]{:S(2)}, u32[]{:S(2)}) collective-permute-start(f32[4,640]{1,0:T(4,128)S(1)} %get-tuple-element.23), channel_id=1, source_target_pairs={{0,1},{1,2},{2,3},{3,0},{4,5},{5,6},{6,7},{7,4},{8,9},{9,10},{10,1... | collective-permute-start | bytes 30728 | tf_op jit(solution)/shard_map/ppermute | solution.py:567
  45.9 3.1 %collective-permute-start.12 = (f32[4,640]{1,0:T(4,128)S(1)}, f32[4,640]{1,0:T(4,128)S(1)}, u32[]{:S(2)}, u32[]{:S(2)}) collective-permute-start(f32[4,640]{1,0:T(4,128)S(1)} %get-tuple-element.24), channel_id=1, source_target_pairs={{0,3},{1,0},{2,1},{3,2},{4,7},{5,4},{6,5},{7,6},{8,11},{9,8},{10,9... | collective-permute-start | bytes 30728 | tf_op jit(solution)/shard_map/ppermute | solution.py:567
  62.9 7.0 %copy-start.16 = (f32[128]{0:T(128)S(1)}, f32[128]{0:T(128)}, u32[]{:S(2)}) copy-start(f32[128]{0:T(128)} %param.41) | copy-start | bytes 1540
  62.9 7.0 %copy-start.17 = (f32[128]{0:T(128)S(1)}, f32[128]{0:T(128)}, u32[]{:S(2)}) copy-start(f32[128]{0:T(128)} %param.42) | copy-start | bytes 1540
  65.6 2.0 %collective-permute-start.15 = (f32[16,128]{1,0:T(8,128)S(1)}, f32[16,128]{1,0:T(8,128)S(1)}, u32[]{:S(2)}, u32[]{:S(2)}) collective-permute-start(f32[16,128]{1,0:T(8,128)S(1)} %get-tuple-element.25.s0), channel_id=1, source_target_pairs={{0,3},{1,0},{2,1},{3,2},{4,7},{5,4},{6,5},{7,6},{8,11},{9,8},{10,9... | collective-permute-start | bytes 24584 | tf_op jit(solution)/shard_map/ppermute | solution.py:567
  66.3 3.7 %collective-permute-start.14 = (f32[16,128]{1,0:T(8,128)S(1)}, f32[16,128]{1,0:T(8,128)S(1)}, u32[]{:S(2)}, u32[]{:S(2)}) collective-permute-start(f32[16,128]{1,0:T(8,128)S(1)} %get-tuple-element.25.s0), channel_id=1, source_target_pairs={{0,2},{1,3},{2,0},{3,1},{4,6},{5,7},{6,4},{7,5},{8,10},{9,11},{10,... | collective-permute-start | bytes 24584 | tf_op jit(solution)/shard_map/ppermute | solution.py:567
  66.5 3.4 %collective-permute-start.13 = (f32[16,128]{1,0:T(8,128)S(1)}, f32[16,128]{1,0:T(8,128)S(1)}, u32[]{:S(2)}, u32[]{:S(2)}) collective-permute-start(f32[16,128]{1,0:T(8,128)S(1)} %get-tuple-element.25.s0), channel_id=1, source_target_pairs={{0,1},{1,2},{2,3},{3,0},{4,5},{5,6},{6,7},{7,4},{8,9},{9,10},{10,1... | collective-permute-start | bytes 24584 | tf_op jit(solution)/shard_map/ppermute | solution.py:567
  69.9 13.6 %copy-start.18 = (f32[128]{0:T(128)S(1)}, f32[128]{0:T(128)}, u32[]{:S(2)}) copy-start(f32[128]{0:T(128)} %param.44) | copy-start | bytes 1540
  69.9 13.6 %copy-start.19 = (f32[128]{0:T(128)S(1)}, f32[128]{0:T(128)}, u32[]{:S(2)}) copy-start(f32[128]{0:T(128)} %param.45) | copy-start | bytes 1540
  69.9 13.6 %copy-start.20 = (f32[128]{0:T(128)S(1)}, f32[128]{0:T(128)}, u32[]{:S(2)}) copy-start(f32[128]{0:T(128)} %param.47) | copy-start | bytes 1540
  78.9 1.7 %collective-permute-start.18 = (f32[8,128]{1,0:T(8,128)S(1)}, f32[8,128]{1,0:T(8,128)S(1)}, u32[]{:S(2)}, u32[]{:S(2)}) collective-permute-start(f32[8,128]{1,0:T(8,128)S(1)} %get-tuple-element.27.s0), channel_id=1, source_target_pairs={{0,3},{1,0},{2,1},{3,2},{4,7},{5,4},{6,5},{7,6},{8,11},{9,8},{10,9... | collective-permute-start | bytes 12296 | tf_op jit(solution)/shard_map/ppermute | solution.py:567
  79.0 3.7 %collective-permute-start.17 = (f32[8,128]{1,0:T(8,128)S(1)}, f32[8,128]{1,0:T(8,128)S(1)}, u32[]{:S(2)}, u32[]{:S(2)}) collective-permute-start(f32[8,128]{1,0:T(8,128)S(1)} %get-tuple-element.27.s0), channel_id=1, source_target_pairs={{0,2},{1,3},{2,0},{3,1},{4,6},{5,7},{6,4},{7,5},{8,10},{9,11},{10,... | collective-permute-start | bytes 12296 | tf_op jit(solution)/shard_map/ppermute | solution.py:567
  80.5 3.0 %collective-permute-start.16 = (f32[8,128]{1,0:T(8,128)S(1)}, f32[8,128]{1,0:T(8,128)S(1)}, u32[]{:S(2)}, u32[]{:S(2)}) collective-permute-start(f32[8,128]{1,0:T(8,128)S(1)} %get-tuple-element.27.s0), channel_id=1, source_target_pairs={{0,1},{1,2},{2,3},{3,0},{4,5},{5,6},{6,7},{7,4},{8,9},{9,10},{10,1... | collective-permute-start | bytes 12296 | tf_op jit(solution)/shard_map/ppermute | solution.py:567

commit v2 on v1

--- a/solution.py
+++ b/solution.py
@@ -78,102 +78,172 @@
         slots[row, :, slot * channels + at : slot * channels + at + width] = piece.astype(BF16)
 
 
-def input_sums_kernel(x_ref, out_ref):
+def input_sums_kernel(x_hbm, x_ref, top_ref, bottom_ref, out_ref, sems):
     lines, width, channels = x_ref.shape
+    halo = top_ref.shape[0]
     rows = channels // LANES
-
-    def step(r, carry):
-        first, second = list(carry[0]), list(carry[1])
+    copies = [pltpu.make_async_copy(x_hbm.at[r], x_ref.at[r], sems.at[r]) for r in range(lines)]
+    for copy in copies:
+        copy.start()
+    first = [jnp.zeros((8, LANES), F32) for _ in range(rows)]
+    second = list(first)
+    for r in range(lines):
+        copies[r].wait()
         for k in range(rows):
             v = x_ref[r, :, k * LANES : (k + 1) * LANES].astype(F32).reshape(width // 8, 8, LANES)
             first[k] = first[k] + v.sum(0)
             second[k] = second[k] + (v * v).sum(0)
-        return tuple(first), tuple(second)
-
-    zero = tuple(jnp.zeros((8, LANES), F32) for _ in range(rows))
-    first, second = lax.fori_loop(0, lines, step, (zero, zero))
+        if r < halo:
+            top_ref[r] = x_ref[r]
+        if r >= lines - halo:
+            bottom_ref[r - (lines - halo)] = x_ref[r]
     for k in range(rows):
         out_ref[k : k + 1, :] = first[k].sum(0, keepdims=True)
         out_ref[rows + k : rows + k + 1, :] = second[k].sum(0, keepdims=True)
 
 
-def input_sums(x):
-    channels = x.shape[2]
+def input_sums(x, halo):
+    lines, width, channels = x.shape
+    edge = pltpu.VMEM((halo, width, channels), BF16)
     return pl.pallas_call(
         input_sums_kernel,
-        out_shape=jax.ShapeDtypeStruct((2 * channels // LANES, LANES), F32),
-        in_specs=[VMEM],
-        out_specs=VMEM,
-        compiler_params=params(6),
+        out_shape=(pltpu.VMEM(x.shape, BF16), edge, edge, jax.ShapeDtypeStruct((2 * channels // LANES, LANES), F32)),
+        in_specs=[HBM],
+        out_specs=(VMEM, VMEM, VMEM, VMEM),
+        scratch_shapes=[pltpu.SemaphoreType.DMA((lines,))],
+        compiler_params=params(8),
         cost_estimate=cost(6e9),
         name="input_sums",
-    )(x)
-
-
-def conv_rows(slots, weights, bias_ref, out, sums, out_lines, own_at, own_lines, half, channels, residual):
-    tile = 256
-    n_tiles = channels // tile
-    sums[...] = jnp.zeros_like(sums)
-
-    def step(index, _):
-        parity = index // n_tiles
-        at = pl.multiple_of((index % n_tiles) * tile, tile)
-        left = pl.multiple_of(parity * channels, channels)
-        acc = None
-        for i in range(3):
-            lhs = slots[i : i + out_lines, :, pl.ds(left, 3 * channels)].reshape(out_lines * half, 3 * channels)
-            part = jnp.dot(lhs, weights[i, :, pl.ds(at, tile)], preferred_element_type=F32)
-            acc = part if acc is None else acc + part
-        acc = acc.reshape(out_lines, half, tile) + bias_ref[:, pl.ds(at, tile)].reshape(1, 1, tile)
-        if residual is not None:
-            acc = acc + residual[:, parity, :, pl.ds(at, tile)].astype(F32)
-        out[:, parity, :, pl.ds(at, tile)] = acc
-        own = acc[own_at : own_at + own_lines].reshape(own_lines * half, tile)
-        sums[0:1, pl.ds(at, tile)] += own.sum(0, keepdims=True)
-        sums[1:2, pl.ds(at, tile)] += (own * own).sum(0, keepdims=True)
-        return 0
-
-    lax.fori_loop(0, 2 * n_tiles, step, 0)
-
-
-def conv1_kernel(
-    meta, s0, s1, s2, s3, gain, shift, bias, x_ref, up_ref, low_ref, w_hbm,
-    h_ref, xp_ref, stats_ref,
-    rowf, slots, wv, sums, wsem,
-    *, count, per_group, n_blocks,
+    )(in_hbm(x))
+
+
+def norm_line(slots, row, read, scale, move, inside, channels, keep=None):
+    for at in range(0, channels, LANES):
+        cols = slice(at, at + LANES)
+        even, odd = read(at // LANES, cols)
+        if keep is not None:
+            keep[0, :, cols] = even.astype(BF16)
+            keep[1, :, cols] = odd.astype(BF16)
+        even = jnp.where(inside, half_silu(even, scale[:, cols], move[:, cols]), 0.0)
+        odd = jnp.where(inside, half_silu(odd, scale[:, cols], move[:, cols]), 0.0)
+        spread_columns(slots, row, at, even, odd, channels)
+
+
+def block_conv(slots, weights, first, lines, channels, between=(), waits=None):
+    half = slots.shape[1]
+    acc = None
+    for i in range(3):
+
+        def dot(j, taps, i=i):
+            parts = [
+                slots[first + i : first + i + lines, :, (p + j) * channels : (p + j + taps) * channels].reshape(
+                    lines * half, taps * channels
+                )
+                for p in range(2)
+            ]
+            tap_weights = weights[i, j * channels : (j + taps) * channels, :]
+            return jnp.dot(jnp.concatenate(parts, axis=0), tap_weights, preferred_element_type=F32)
+
+        if waits is None:
+            part = dot(0, 3)
+        else:
+            part = None
+            for j in range(3):
+                waits[3 * i + j].wait()
+                one = dot(j, 1)
+                part = one if part is None else part + one
+        acc = part if acc is None else acc + part
+        if i < len(between):
+            between[i]()
+    return acc.reshape(2, lines, half, channels)
+
+
+class Sums:
+    def __init__(self, channels):
+        self.channels = channels
+        self.first = jnp.zeros((8, channels), F32)
+        self.second = jnp.zeros((8, channels), F32)
+
+    def add(self, line):
+        line = line.reshape(-1, 8, self.channels)
+        self.first = self.first + line.sum(0)
+        self.second = self.second + (line * line).sum(0)
+
+    def put(self, out_ref, base=None):
+        rows = self.channels // LANES
+        put_sums(out_ref, self.first.sum(0, keepdims=True), self.second.sum(0, keepdims=True), rows)
+        if base is not None:
+            out_ref[...] += base[...]
+
+
+def conv1a_kernel(
+    s0, s1, s2, s3, gain, shift, bias, x_ref, w_hbm, h_ref, xp_ref, slots, wv, stats_ref, rowf, wsems,
+    *, halo, count, per_group,
 ):
     own, width, channels = x_ref.shape
-    halo = up_ref.shape[0]
-    lines = own + 2 * halo
     half = width // 2
-    weight_load = pltpu.make_async_copy(w_hbm, wv, wsem)
-    weight_load.start()
+    loads = []
+    for i in range(3):
+        for j in range(3):
+            rows = pl.ds(j * channels, channels)
+            loads.append(pltpu.make_async_copy(w_hbm.at[i, rows], wv.at[i, rows], wsems.at[3 * i + j]))
+            loads[-1].start()
     scale, move = half_affine((s0, s1, s2, s3), channels // LANES, gain[...], shift[...], count, per_group)
     scale, move = as_row(scale), as_row(move)
-    first_line = meta[0] * own - halo
-
-    def norm(source, at_line, r, keep):
-        line = first_line + at_line + r
-        inside = (line >= 0) & (line < n_blocks * own)
-        for at in range(0, channels, LANES):
-            cols = slice(at, at + LANES)
-            chunk = at // LANES
-            rowf[chunk] = source[r, :, cols].astype(F32)
-            even = rowf[chunk, pl.ds(0, half, stride=2), :]
-            odd = rowf[chunk, pl.ds(1, half, stride=2), :]
-            if keep:
-                xp_ref[r, 0, :, cols] = even.astype(BF16)
-                xp_ref[r, 1, :, cols] = odd.astype(BF16)
-            even = jnp.where(inside, half_silu(even, scale[:, cols], move[:, cols]), 0.0)
-            odd = jnp.where(inside, half_silu(odd, scale[:, cols], move[:, cols]), 0.0)
-            spread_columns(slots, at_line + r, at, even, odd, channels)
-
-    pl.loop(0, halo)(lambda r: norm(up_ref, 0, r, False))
-    pl.loop(0, own)(lambda r: norm(x_ref, halo, r, True))
-    pl.loop(0, halo)(lambda r: norm(low_ref, halo + own, r, False))
-    weight_load.wait()
-    conv_rows(slots, wv, bias, h_ref, sums, lines - 2, halo - 1, own, half, channels, None)
-    put_sums(stats_ref, sums[0:1, :], sums[1:2, :], channels // LANES)
+    offset = bias[...].reshape(1, 1, 1, channels)
+
+    def norm(r):
+        def read(chunk, cols):
+            rowf[r, chunk] = x_ref[r, :, cols].astype(F32)
+            return rowf[r, chunk, pl.ds(0, half, stride=2), :], rowf[r, chunk, pl.ds(1, half, stride=2), :]
+
+        norm_line(slots, halo + r, read, scale, move, True, channels, xp_ref.at[r])
+
+    sums = Sums(channels)
+    norm(0)
+    norm(1)
+    for b in range(0, own - 2, 2):
+        lines = [functools.partial(norm, r) for r in (range(2, 6) if b == 0 else range(b + 4, b + 6)) if r < own]
+        acc = block_conv(slots, wv, halo + b, 2, channels, lines[:2], loads if b == 0 else None) + offset
+        for line in lines[2:]:
+            line()
+        for r in range(2):
+            for p in range(2):
+                h_ref[halo + b + r, p] = acc[p, r]
+                sums.add(acc[p, r])
+    sums.put(stats_ref)
+
+
+def conv1b_kernel(
+    meta, s0, s1, s2, s3, gain, shift, bias, up_ref, low_ref, base, wv, h_in, slots_in,
+    h_ref, slots, stats_ref, rowf, *, count, per_group, n_blocks,
+):
+    halo, width, channels = up_ref.shape
+    half = width // 2
+    lines = slots.shape[0]
+    scale, move = half_affine((s0, s1, s2, s3), channels // LANES, gain[...], shift[...], count, per_group)
+    scale, move = as_row(scale), as_row(move)
+    offset = bias[...].reshape(1, 1, 1, channels)
+    sums = Sums(channels)
+
+    def norm(source, r, inside, at):
+        def read(chunk, cols):
+            rowf[at, chunk] = source[r, :, cols].astype(F32)
+            return rowf[at, chunk, pl.ds(0, half, stride=2), :], rowf[at, chunk, pl.ds(1, half, stride=2), :]
+
+        norm_line(slots, at, read, scale, move, inside, channels)
+
+    for r in range(halo):
+        norm(up_ref, r, meta[0] > 0, r)
+    later = [functools.partial(norm, low_ref, r, meta[0] < n_blocks - 1, lines - halo + r) for r in range(halo)]
+    for first, mine in ((0, 1), (lines - 4, 0)):
+        acc = block_conv(slots, wv, first, 2, channels, later if first == 0 else ()) + offset
+        for r in range(2):
+            for p in range(2):
+                h_ref[first + r, p] = acc[p, r]
+                if r == mine:
+                    sums.add(acc[p, r])
+    sums.put(stats_ref, base)
 
 
 def conv1(meta, stats, gain, shift, bias, x, up, low, weight, n_blocks):
@@ -182,58 +252,76 @@
     lines = own + 2 * halo
     half = width // 2
     rows = channels // LANES
-    count = float(n_blocks * own * width * (channels // GROUPS))
-    return pl.pallas_call(
-        functools.partial(conv1_kernel, count=count, per_group=channels // GROUPS, n_blocks=n_blocks),
+    settings = dict(count=float(n_blocks * own * width * (channels // GROUPS)), per_group=channels // GROUPS)
+    gain, shift, bias = gain.reshape(rows, LANES), shift.reshape(rows, LANES), bias.reshape(1, channels)
+    h_type = pltpu.VMEM((lines - 2, 2, half, channels), F32)
+    slots_type = pltpu.VMEM((lines, half, 4 * channels), BF16)
+    stats_type = jax.ShapeDtypeStruct((2 * rows, LANES), F32)
+    h, xp, slots, wv, base = pl.pallas_call(
+        functools.partial(conv1a_kernel, halo=halo, **settings),
         out_shape=(
-            pltpu.VMEM((lines - 2, 2, half, channels), F32),
+            h_type,
             pltpu.VMEM((own, 2, half, channels), BF16),
-            jax.ShapeDtypeStruct((2 * rows, LANES), F32),
+            slots_type,
+            pltpu.VMEM((3, 3 * channels, channels), BF16),
+            stats_type,
         ),
-        in_specs=[SMEM] + [VMEM] * 10 + [HBM],
-        out_specs=(VMEM, VMEM, VMEM),
+        in_specs=[VMEM] * 8 + [HBM],
+        out_specs=(VMEM,) * 5,
         scratch_shapes=[
-            pltpu.VMEM((channels // LANES, width, LANES), F32),
-            pltpu.VMEM((lines, half, 4 * channels), BF16),
-            pltpu.VMEM((3, 3 * channels, channels), BF16),
-            pltpu.VMEM((2, channels), F32),
-            pltpu.SemaphoreType.DMA,
+            pltpu.VMEM((own, channels // LANES, width, LANES), F32),
+            pltpu.SemaphoreType.DMA((9,)),
         ],
         compiler_params=params(26),
-        cost_estimate=cost(40e9),
-        name="conv1",
-    )(meta, *stats, gain.reshape(rows, LANES), shift.reshape(rows, LANES), bias.reshape(1, channels), x, up, low,
-      in_hbm(weight.reshape(3, 3 * channels, channels)))
+        cost_estimate=cost(25e9),
+        name="conv1a",
+    )(*stats, gain, shift, bias, x, in_hbm(weight.reshape(3, 3 * channels, channels)))
+    h, _, sums = pl.pallas_call(
+        functools.partial(conv1b_kernel, n_blocks=n_blocks, **settings),
+        out_shape=(h_type, slots_type, stats_type),
+        in_specs=[SMEM] + [VMEM] * 13,
+        out_specs=(VMEM,) * 3,
+        scratch_shapes=[pltpu.VMEM((lines, channels // LANES, width, LANES), F32)],
+        input_output_aliases={12: 0, 13: 1},
+        compiler_params=params(26),
+        cost_estimate=cost(20e9),
+        name="conv1b",
+    )(meta, *stats, gain, shift, bias, up, low, base, wv, h, slots)
+    return h, xp, sums
 
 
 def conv2_kernel(
-    meta, s0, s1, s2, s3, gain, shift, bias, hs, xs, w_hbm,
-    y_ref, stats_ref,
-    slots, wv, sums, wsem,
+    meta, s0, s1, s2, s3, gain, shift, bias, hs, xs, wv, y_ref, stats_ref, slots,
     *, count, per_group, n_blocks,
 ):
     lines, _, half, channels = hs.shape
     own = lines - 2
-    weight_load = pltpu.make_async_copy(w_hbm, wv, wsem)
-    weight_load.start()
     scale, move = half_affine((s0, s1, s2, s3), channels // LANES, gain[...], shift[...], count, per_group)
     scale, move = as_row(scale), as_row(move)
-    first_line = meta[0] * own - 1
-
-    def norm(r, _):
-        line = first_line + r
-        inside = (line >= 0) & (line < n_blocks * own)
-        for at in range(0, channels, LANES):
-            cols = slice(at, at + LANES)
-            even = jnp.where(inside, half_silu(hs[r, 0, :, cols], scale[:, cols], move[:, cols]), 0.0)
-            odd = jnp.where(inside, half_silu(hs[r, 1, :, cols], scale[:, cols], move[:, cols]), 0.0)
-            spread_columns(slots, r, at, even, odd, channels)
-        return 0
-
-    lax.fori_loop(0, lines, norm, 0)
-    weight_load.wait()
-    conv_rows(slots, wv, bias, y_ref, sums, own, 0, own, half, channels, xs)
-    put_sums(stats_ref, sums[0:1, :], sums[1:2, :], channels // LANES)
+    offset = bias[...].reshape(1, 1, 1, channels)
+
+    def norm(r):
+        inside = True
+        if r == 0:
+            inside = meta[0] > 0
+        if r == lines - 1:
+            inside = meta[0] < n_blocks - 1
+        norm_line(slots, r, lambda chunk, cols: (hs[r, 0, :, cols], hs[r, 1, :, cols]), scale, move, inside, channels)
+
+    sums = Sums(channels)
+    norm(0)
+    norm(1)
+    for b in range(0, own, 2):
+        ahead = [functools.partial(norm, r) for r in (range(2, 6) if b == 0 else range(b + 4, b + 6)) if r < lines]
+        acc = block_conv(slots, wv, b, 2, channels, ahead[:2]) + offset
+        for line in ahead[2:]:
+            line()
+        for r in range(2):
+            for p in range(2):
+                value = acc[p, r] + xs[b + r, p].astype(F32)
+                y_ref[b + r, p] = value
+                sums.add(value)
+    sums.put(stats_ref)
 
 
 def conv2(meta, stats, gain, shift, bias, h, xp, weight, n_blocks):
@@ -247,19 +335,14 @@
             pltpu.VMEM((own, 2, half, channels), F32),
             jax.ShapeDtypeStruct((2 * rows, LANES), F32),
         ),
-        in_specs=[SMEM] + [VMEM] * 9 + [HBM],
+        in_specs=[SMEM] + [VMEM] * 10,
         out_specs=(VMEM, VMEM),
-        scratch_shapes=[
-            pltpu.VMEM((lines, half, 4 * channels), BF16),
-            pltpu.VMEM((3, 3 * channels, channels), BF16),
-            pltpu.VMEM((2, channels), F32),
-            pltpu.SemaphoreType.DMA,
-        ],
+        scratch_shapes=[pltpu.VMEM((lines, half, 4 * channels), BF16)],
         compiler_params=params(26),
         cost_estimate=cost(30e9),
         name="conv2",
     )(meta, *stats, gain.reshape(rows, LANES), shift.reshape(rows, LANES), bias.reshape(1, channels), h, xp,
-      in_hbm(weight.reshape(3, 3 * channels, channels)))
+      weight.reshape(3, 3 * channels, channels))
 
 
 def column_shift(values, tap, half):
@@ -408,65 +491,83 @@
     )(meta, weight.reshape(27, each, channels), bias.reshape(1, channels), latents)
 
 
-def pair_weight_copies(w_hbm, wv, sems, channels):
-    copies = []
-    for c in range(2):
-        for j in range(3):
-            target = wv.at[:, pl.ds((j + c) * channels, channels), pl.ds(c * channels, channels)]
-            copies.append(pltpu.make_async_copy(w_hbm.at[:, j], target, sems.at[3 * c + j]))
-    return copies
-
-
-def clear_pair_weights(wv, channels):
-    zero = jnp.zeros((wv.shape[0], channels, channels), BF16)
-    wv[:, 3 * channels : 4 * channels, 0:channels] = zero
-    wv[:, 0:channels, channels : 2 * channels] = zero
+def pair_weights(w_ref, tap):
+    first, second, third = (w_ref[tap, j] for j in range(3))
+    none = jnp.zeros_like(first)
+    rows = ((first, none), (second, first), (third, second), (none, third))
+    return jnp.concatenate([jnp.concatenate(row, axis=1) for row in rows], axis=0)
+
+
+class Ahead:
+    def __init__(self, order, emit):
+        self.order, self.emit, self.done = list(dict.fromkeys(order)), emit, set()
+
+    def need(self, items):
+        while not self.done.issuperset(items):
+            self.more(1)
+
+    def more(self, count):
+        for _ in range(min(count, len(self.order))):
+            item = self.order.pop(0)
+            self.emit(*item)
+            self.done.add(item)
+
+
+def clip_blocks(slots, w_ref, blocks, lines, ahead, finish, pace):
+    half, depth = slots.shape[2], slots.shape[3]
+    for k, first in blocks:
+        acc = None
+        for t in range(3):
+            frame = k + 2 - t
+            ahead.need([(frame, r) for r in range(first, first + lines + 2)])
+            for i in range(3):
+                lhs = slots[frame, first + i : first + i + lines].reshape(lines * half, depth)
+                part = jnp.dot(lhs, pair_weights(w_ref, 3 * t + i), preferred_element_type=F32)
+                acc = part if acc is None else acc + part
+            ahead.more(pace)
+        finish(k, first, acc)
+
+
+def block_order(blocks, lines):
+    return [(k + 2 - t, r) for k, first in blocks for t in range(3) for r in range(first, first + lines + 2)]
 
 
 def time1_kernel(
-    meta, s0, s1, s2, s3, gain, shift, ts, w_hbm, t1v, stats_ref, slots, wv, wsems,
+    meta, s0, s1, s2, s3, gain, shift, ts, w_ref, t1v, stats_ref, slots,
     *, count, per_group, n_blocks, own, n_out,
 ):
     frames, lines, half, _ = slots.shape
     channels = gain.shape[1]
     width = 2 * half
-    weight_loads = pair_weight_copies(w_hbm, wv, wsems, channels)
-    for copy in weight_loads:
-        copy.start()
-    clear_pair_weights(wv, channels)
     scale, move = half_affine((s0, s1, s2, s3), frames, gain[...], shift[...], count, per_group)
     first_line = meta[0] * own - 2
-    for k in range(frames):
+
+    def norm(k, r):
+        line = first_line + r
+        inside = (line >= 0) & (line < n_blocks * own) & (meta[1] >= k)
+        at = r * width
         cols = slice(k * channels, (k + 1) * channels)
-
-        def norm(r, _, k=k, cols=cols):
-            line = first_line + r
-            inside = (line >= 0) & (line < n_blocks * own) & (meta[1] >= k)
-            at = pl.multiple_of(r * width, width)
-            even = half_silu(ts[pl.ds(at, half), cols], scale[k : k + 1], move[k : k + 1])
-            odd = half_silu(ts[pl.ds(at + half, half), cols], scale[k : k + 1], move[k : k + 1])
-            even = jnp.where(inside, even, 0.0)
-            odd = jnp.where(inside, odd, 0.0)
-            spread_columns(slots.at[k], r, 0, even, odd, channels)
-            return 0
-
-        lax.fori_loop(0, lines, norm, 0)
-    for copy in weight_loads:
-        copy.wait()
-    out_lines = lines - 2
+        even = half_silu(ts[at : at + half, cols], scale[k : k + 1], move[k : k + 1])
+        odd = half_silu(ts[at + half : at + width, cols], scale[k : k + 1], move[k : k + 1])
+        spread_columns(slots.at[k], r, 0, jnp.where(inside, even, 0.0), jnp.where(inside, odd, 0.0), channels)
+
+    part_lines = (lines - 2) // 2
+    blocks = [(k, first) for first in (0, part_lines) for k in reversed(range(n_out))]
+    sums = [[jnp.zeros((8, 2 * channels), F32)] * 2 for _ in range(n_out)]
+
+    def finish(k, first, acc):
+        t1v[k, first : first + part_lines] = acc.reshape(part_lines, half, 2 * channels)
+        skip = 1 if first == 0 else 0
+        mine = acc[skip * half : (skip + part_lines - 1) * half].reshape(-1, 8, 2 * channels)
+        sums[k] = [sums[k][0] + mine.sum(0), sums[k][1] + (mine * mine).sum(0)]
+
+    ahead = Ahead(block_order(blocks, part_lines), norm)
+    clip_blocks(slots, w_ref, blocks, part_lines, ahead, finish, 4)
     for k in range(n_out):
-        acc = None
-        for t in range(3):
-            for i in range(3):
-                lhs = slots[k + 2 - t, i : i + out_lines].reshape(out_lines * half, 4 * channels)
-                part = jnp.dot(lhs, wv[3 * t + i], preferred_element_type=F32)
-                acc = part if acc is None else acc + part
-        t1v[k] = acc.reshape(out_lines, half, 2 * channels)
-        mine = acc[half : (1 + own) * half]
-        first = mine.sum(0, keepdims=True)
-        second = (mine * mine).sum(0, keepdims=True)
-        stats_ref[k : k + 1, :] = first[:, :channels] + first[:, channels:]
-        stats_ref[n_out + k : n_out + k + 1, :] = second[:, :channels] + second[:, channels:]
+        for at, value in enumerate(sums[k]):
+            value = value.sum(0, keepdims=True)
+            row = at * n_out + k
+            stats_ref[row : row + 1, :] = value[:, :channels] + value[:, channels:]
 
 
 def time1(meta, stats, gain, shift, t0, weight, n_blocks, own, half, n_frames, n_out):
@@ -481,62 +582,50 @@
             pltpu.VMEM((n_out, lines - 2, half, 2 * channels), F32),
             jax.ShapeDtypeStruct((-(-2 * n_out // 8) * 8, channels), F32),
         ),
-        in_specs=[SMEM] + [VMEM] * 7 + [HBM],
+        in_specs=[SMEM] + [VMEM] * 8,
         out_specs=(VMEM, VMEM),
         scratch_shapes=[
             pltpu.VMEM((n_frames, lines, half, 4 * channels), BF16),
-            pltpu.VMEM((9, 4 * channels, 2 * channels), BF16),
-            pltpu.SemaphoreType.DMA((6,)),
         ],
         compiler_params=params(26),
         cost_estimate=cost(30e9),
         name="time1",
     )(meta, *stats, gain.reshape(1, channels), shift.reshape(1, channels), t0,
-      in_hbm(weight.reshape(9, 3, channels, channels)))
+      weight.reshape(9, 3, channels, channels))
 
 
 def time2_kernel(
-    meta, s0, s1, s2, s3, gain, shift, bias, ts, t0s, w_hbm, outv, slots, wv, rowf, wsems,
+    meta, s0, s1, s2, s3, gain, shift, bias, ts, t0s, w_ref, outv, slots, rowf,
     *, count, per_group, n_blocks,
 ):
     frames, lines, half, _ = slots.shape
     own = lines - 2
     channels = gain.shape[1]
     width = 2 * half
-    weight_loads = pair_weight_copies(w_hbm, wv, wsems, channels)
-    for copy in weight_loads:
-        copy.start()
-    clear_pair_weights(wv, channels)
     scale, move = half_affine((s0, s1, s2, s3), frames, gain[...], shift[...], count, per_group)
     first_line = meta[0] * own - 1
-    for k in range(frames):
-
-        def norm(r, _, k=k):
-            line = first_line + r
-            inside = (line >= 0) & (line < n_blocks * own) & (meta[1] >= k)
-            even = half_silu(ts[k, r, :, 0:channels], scale[k : k + 1], move[k : k + 1])
-            odd = half_silu(ts[k, r, :, channels : 2 * channels], scale[k : k + 1], move[k : k + 1])
-            even = jnp.where(inside, even, 0.0)
-            odd = jnp.where(inside, odd, 0.0)
-            spread_columns(slots.at[k], r, 0, even, odd, channels)
-            return 0
-
-        lax.fori_loop(0, lines, norm, 0)
-    for copy in weight_loads:
-        copy.wait()
-    acc = None
-    for t in range(3):
-        for i in range(3):
-            lhs = slots[2 - t, i : i + own].reshape(own * half, 4 * channels)
-            part = jnp.dot(lhs, wv[3 * t + i], preferred_element_type=F32)
-            acc = part if acc is None else acc + part
-    acc = acc.reshape(own, half, 2 * channels)
-    for r in range(own):
-        for parity in range(2):
-            at = (2 + r) * width + parity * half
-            value = acc[r, :, parity * channels : (parity + 1) * channels] + bias[...]
-            rowf[r, pl.ds(parity, half, stride=2), :] = value + t0s[at : at + half, 0:channels]
-        outv[0, r] = rowf[r].astype(BF16)
+
+    def norm(k, r):
+        line = first_line + r
+        inside = (line >= 0) & (line < n_blocks * own) & (meta[1] >= k)
+        even = half_silu(ts[k, r, :, 0:channels], scale[k : k + 1], move[k : k + 1])
+        odd = half_silu(ts[k, r, :, channels : 2 * channels], scale[k : k + 1], move[k : k + 1])
+        spread_columns(slots.at[k], r, 0, jnp.where(inside, even, 0.0), jnp.where(inside, odd, 0.0), channels)
+
+    part_lines = own // 2
+    blocks = [(0, 0), (0, part_lines)]
+
+    def finish(k, first, acc):
+        acc = acc.reshape(part_lines, half, 2 * channels)
+        for r in range(part_lines):
+            for parity in range(2):
+                at = (2 + first + r) * width + parity * half
+                value = acc[r, :, parity * channels : (parity + 1) * channels] + bias[...]
+                rowf[first + r, pl.ds(parity, half, stride=2), :] = value + t0s[at : at + half, 0:channels]
+            outv[0, first + r] = rowf[first + r].astype(BF16)
+
+    ahead = Ahead(block_order(blocks, part_lines), norm)
+    clip_blocks(slots, w_ref, blocks, part_lines, ahead, finish, 4)
 
 
 def time2(meta, stats, gain, shift, bias, t1, t0, weight, n_blocks):
@@ -547,19 +636,17 @@
     return pl.pallas_call(
         functools.partial(time2_kernel, count=count, per_group=channels // GROUPS, n_blocks=n_blocks),
         out_shape=jax.ShapeDtypeStruct((1, own, 2 * half, channels), BF16),
-        in_specs=[SMEM] + [VMEM] * 9 + [HBM],
+        in_specs=[SMEM] + [VMEM] * 10,
         out_specs=VMEM,
         scratch_shapes=[
             pltpu.VMEM((frames, lines, half, 4 * channels), BF16),
-            pltpu.VMEM((9, 4 * channels, 2 * channels), BF16),
             pltpu.VMEM((own, 2 * half, channels), F32),
-            pltpu.SemaphoreType.DMA((6,)),
         ],
         compiler_params=params(24),
         cost_estimate=cost(12e9),
         name="time2",
     )(meta, *stats, gain.reshape(1, channels), shift.reshape(1, channels), bias.reshape(1, channels), t1, t0,
-      in_hbm(weight.reshape(9, 3, channels, channels)))
+      weight.reshape(9, 3, channels, channels))
 
 
 def turned(block, axis, distance):
@@ -581,9 +668,10 @@
     half = width // 2
     n_blocks = lax.axis_size("rows")
     meta = jnp.stack([lax.axis_index("rows"), lax.axis_index("frames")]).astype(jnp.int32)
-    up = turned(x[own - 2 :], "rows", 1)
-    low = turned(x[:2], "rows", -1)
-    stats = from_all(input_sums(x))
+    x, top, bottom, sums = input_sums(x, 2)
+    stats = from_all(sums)
+    up = turned(bottom, "rows", 1)
+    low = turned(top, "rows", -1)
     h, xp, sums = conv1(meta, stats, norm1_gain, norm1_shift, conv1_bias, x, up, low, conv1_weight, n_blocks)
     y, sums = conv2(meta, from_all(sums), norm2_gain, norm2_shift, conv2_bias, h, xp, conv2_weight, n_blocks)
     part, to_up, to_low = head(

time: 88.3 us -> 77.4 us (0.88)
  waiting for transfers between devices: 18.5 us -> 9.44 us
  starting transfers between devices: 12.9 us -> 17.8 us
  Pallas kernels: 39.9 us -> 35.6 us
  local copies, waits for them, and re-layouts: 2.58 us -> 0.16 us
    ppermute x19, waiting for transfers between devices: 18.5 us -> 9.44 us  [turned(): lax.ppermute(block, axis, [(i, (i + distance) % count) for i in range(cou...]
    ppermute x19, starting transfers between devices: 12.9 us -> 17.8 us  [turned(): lax.ppermute(block, axis, [(i, (i + distance) % count) for i in range(cou...]
    pallas_call x1, Pallas kernels: 9.75 us -> 7.3 us  [conv2(): pl.pallas_call(functools.partial(conv2_kernel, count=count, per_group=cha...]
    pallas_call x1, Pallas kernels: 8.98 us -> 6.96 us  [time1(): pl.pallas_call(functools.partial(time1_kernel, count=count, per_group=cha...]
    unnamed x42 -> x46, local copies, waits for them, and re-layouts: 1.43 us -> 0.12 us
    pallas_call x2 -> x3, Pallas kernels: 11.7 us -> 12.9 us  [the longest x1 7.08 us: conv1(): pl.pallas_call(functools.partial(conv1a_kernel, halo=halo, **settings), o...]
    pallas_call x1, Pallas kernels: 4.5 us -> 3.39 us  [time2(): pl.pallas_call(functools.partial(time2_kernel, count=count, per_group=cha...]
    slice x1 -> x0, local copies, waits for them, and re-layouts: 1.11 us -> none  [body(): low = turned(x[:2], 'rows', -1)]
  transfers between devices with their start and end apart: 19 -> 19, of which waited for: 12 -> 11; matrix products, arithmetic and copies ran while one was open for 0% -> 0% of each run, Pallas kernels for 1% -> 9%
where the time goes in v2:
time: 77.4 us; the launch traced here: 77.2 us
  Pallas kernels  35.6 us (46%)
  starting transfers between devices  17.8 us (23%)
  blocking collectives  13.6 us (18%)
  waiting for transfers between devices  9.44 us (12%)
    ppermute x19, starting transfers between devices, turned(): lax.ppermute(block, axis, [(i, (i + distance) % count) for i in range(cou...  17.8 us
    all_to_all x1, blocking collectives, body(): lax.all_to_all(jnp.broadcast_to(latent[None], (n_frames,) + latent.shape)...  13.6 us
    ppermute x19, waiting for transfers between devices, turned(): lax.ppermute(block, axis, [(i, (i + distance) % count) for i in range(cou...  9.44 us
    pallas_call x1, Pallas kernels, conv2(): pl.pallas_call(functools.partial(conv2_kernel, count=count, per_group=cha...  7.3 us
    pallas_call x1, Pallas kernels, conv1(): pl.pallas_call(functools.partial(conv1a_kernel, halo=halo, **settings), o...  7.08 us
    pallas_call x1, Pallas kernels, time1(): pl.pallas_call(functools.partial(time1_kernel, count=count, per_group=cha...  6.96 us
    pallas_call x1, Pallas kernels, conv1(): pl.pallas_call(functools.partial(conv1b_kernel, n_blocks=n_blocks, **sett...  4.24 us
    pallas_call x1, Pallas kernels, time2(): pl.pallas_call(functools.partial(time2_kernel, count=count, per_group=cha...  3.39 us
  transfers between devices with their start and end apart: 19, of which 11 were waited for; matrix products, arithmetic and copies ran while one was open for 0% of the time, Pallas kernels for 9%

profile of v2, /device:TPU:0, one launch (start us, length us, event | category | flops | bytes accessed | tf_op | source)
XLA Modules:
  0.0 77.2 jit_solution(4708239631174615208)
XLA Ops:
  0.0 1.6 %input_sums.1 = (bf16[8,160,512]{2,1,0:T(8,128)(2,1)S(1)}, bf16[2,160,512]{2,1,0:T(8,128)(2,1)S(1)}, bf16[2,160,512]{2,1,0:T(8,128)(2,1)S(1)}, f32[8,128]{1,0:T(8,128)S(1)}) custom-call(bf16[8,160,512]{2,1,0:T(8,128)(2,1)} %bitcast.52), custom_call_target="tpu_custom_call" | custom-call | flops 6000000000 | tf_op jit(solution)/shard_map/input_sums/pallas_call | solution.py:108
  1.6 0.6 collective-permute-start
  2.2 2.6 %collective-permute-start.1 = (f32[8,128]{1,0:T(8,128)S(1)}, f32[8,128]{1,0:T(8,128)S(1)}, u32[]{:S(2)}, u32[]{:S(2)}) collective-permute-start(f32[8,128]{1,0:T(8,128)S(1)} %get-tuple-element.25.s0), channel_id=1, source_target_pairs={{0,2},{1,3},{2,0},{3,1},{4,6},{5,7},{6,4},{7,5},{8,10},{9,11},{10,... | collective-permute-start | bytes 12296 | tf_op jit(solution)/shard_map/ppermute | solution.py:654
  4.8 1.4 %collective-permute-start.2 = (f32[8,128]{1,0:T(8,128)S(1)}, f32[8,128]{1,0:T(8,128)S(1)}, u32[]{:S(2)}, u32[]{:S(2)}) collective-permute-start(f32[8,128]{1,0:T(8,128)S(1)} %get-tuple-element.25.s0), channel_id=1, source_target_pairs={{0,3},{1,0},{2,1},{3,2},{4,7},{5,4},{6,5},{7,6},{8,11},{9,8},{10,9... | collective-permute-start | bytes 12296 | tf_op jit(solution)/shard_map/ppermute | solution.py:654
  6.1 0.0 collective-permute-start.3
  6.2 1.7 %collective-permute-start.4 = (bf16[2,160,512]{2,1,0:T(8,128)(2,1)S(1)}, bf16[2,160,512]{2,1,0:T(8,128)(2,1)S(1)}, u32[]{:S(2)}, u32[]{:S(2)}) collective-permute-start(bf16[2,160,512]{2,1,0:T(8,128)(2,1)S(1)} %get-tuple-element.27), channel_id=1, source_target_pairs={{0,3},{1,0},{2,1},{3,2},{4,7},{5,4},{6,5},{7,6},{8,11},{9,8},{10,9... | collective-permute-start | bytes 983048 | tf_op jit(solution)/shard_map/ppermute | solution.py:654
  7.9 0.1 pad_add_fusion.meta
  8.0 0.0 collective-permute-done.s1
  8.0 0.0 collective-permute-done.1.s2
  8.0 0.0 collective-permute-done.2.s3
  8.0 0.0 copy-done.4
  8.0 0.0 slice-start.1
  8.0 7.1 %conv1a.1 = (f32[10,2,80,512]{3,2,1,0:T(8,128)S(1)}, bf16[8,2,80,512]{3,2,1,0:T(8,128)(2,1)S(1)}, bf16[12,80,2048]{2,1,0:T(8,128)(2,1)S(1)}, bf16[3,1536,512]{2,1,0:T(8,128)(2,1)S(1)}, f32[8,128]{1,0:T(8,128)S(1)}) custom-call(f32[8,128]{1,0:T(8,128)S(1)} %get-tuple-element.25.s0, f32[8,128]{1,0:T(8,128)S(1)} %collective-permute-done.s1, ...), custom_call_target="tpu_custom_call" | custom-call | flops 24999999488 | tf_op jit(solution)/shard_map/conv1a/pallas_call | solution.py:260
  15.1 0.5 collective-permute-done.3.up_ref
  15.6 0.0 collective-permute-done.4.low_ref
  15.6 4.2 %conv1b.1 = (f32[10,2,80,512]{3,2,1,0:T(8,128)S(1)}, bf16[12,80,2048]{2,1,0:T(8,128)(2,1)S(1)}, f32[8,128]{1,0:T(8,128)S(1)}) custom-call(s32[2]{0:T(128)S(1)} %pad_add_fusion.meta, f32[8,128]{1,0:T(8,128)S(1)} %get-tuple-element.25.s0, f32[8,128]{1,0:T(8,128)S(1)} %collective-permute-done.s1, ...), custom_call_target="tpu_custom_call", output_to_operand_aliasing={{0}: (12, {}), {1}: (13, {})} | custom-call | flops 20000000000 | tf_op jit(solution)/shard_map/conv1b/pallas_call | solution.py:279
  19.8 0.4 collective-permute-start.5
  20.3 1.1 %collective-permute-start.6 = (f32[8,128]{1,0:T(8,128)S(1)}, f32[8,128]{1,0:T(8,128)S(1)}, u32[]{:S(2)}, u32[]{:S(2)}) collective-permute-start(f32[8,128]{1,0:T(8,128)S(1)} %get-tuple-element.33.s0), channel_id=1, source_target_pairs={{0,2},{1,3},{2,0},{3,1},{4,6},{5,7},{6,4},{7,5},{8,10},{9,11},{10,... | collective-permute-start | bytes 12296 | tf_op jit(solution)/shard_map/ppermute | solution.py:654
  21.4 0.3 collective-permute-start.7
  21.7 1.2 %collective-permute-done.5.s1 = f32[8,128]{1,0:T(8,128)S(1)} collective-permute-done((f32[8,128]{1,0:T(8,128)S(1)}, f32[8,128]{1,0:T(8,128)S(1)}, u32[]{:S(2)}, u32[]{:S(2)}) %collective-permute-start.5) | collective-permute-done | bytes 4128 | tf_op jit(solution)/shard_map/ppermute | solution.py:654
  22.9 1.0 %collective-permute-done.6.s2 = f32[8,128]{1,0:T(8,128)S(1)} collective-permute-done((f32[8,128]{1,0:T(8,128)S(1)}, f32[8,128]{1,0:T(8,128)S(1)}, u32[]{:S(2)}, u32[]{:S(2)}) %collective-permute-start.6) | collective-permute-done | bytes 4128 | tf_op jit(solution)/shard_map/ppermute | solution.py:654
  23.9 0.0 collective-permute-done.7.s3
  23.9 0.0 copy-start.2
  23.9 0.0 copy-start.10
  24.0 0.0 copy-start.11
  24.0 0.0 copy-start.12
  24.0 0.0 copy-start.13
  24.0 0.0 copy-start.14
  24.0 7.3 %conv2.1 = (f32[8,2,80,512]{3,2,1,0:T(8,128)S(1)}, f32[8,128]{1,0:T(8,128)S(1)}) custom-call(s32[2]{0:T(128)S(1)} %pad_add_fusion.meta, f32[8,128]{1,0:T(8,128)S(1)} %get-tuple-element.33.s0, f32[8,128]{1,0:T(8,128)S(1)} %collective-permute-done.5.s1, f32[8,128]{1,0:T(8,128)S(1)} %collective-permute-done.6.s2, f32[8,128]{1,0:T(8,128)S(1)} %collective-permute-done.7.s3, ...), custom_call_target="tpu_custom_call" | custom-call | flops 30000001024 | tf_op jit(solution)/shard_map/conv2/pallas_call | solution.py:332
  31.3 0.9 %collective-permute-start.10 = (f32[8,128]{1,0:T(8,128)S(1)}, f32[8,128]{1,0:T(8,128)S(1)}, u32[]{:S(2)}, u32[]{:S(2)}) collective-permute-start(f32[8,128]{1,0:T(8,128)S(1)} %get-tuple-element.36.s0), channel_id=1, source_target_pairs={{0,3},{1,0},{2,1},{3,2},{4,7},{5,4},{6,5},{7,6},{8,11},{9,8},{10,9... | collective-permute-start | bytes 12296 | tf_op jit(solution)/shard_map/ppermute | solution.py:654
  32.2 0.1 collective-permute-start.8
  32.3 1.6 %collective-permute-start.9 = (f32[8,128]{1,0:T(8,128)S(1)}, f32[8,128]{1,0:T(8,128)S(1)}, u32[]{:S(2)}, u32[]{:S(2)}) collective-permute-start(f32[8,128]{1,0:T(8,128)S(1)} %get-tuple-element.36.s0), channel_id=1, source_target_pairs={{0,2},{1,3},{2,0},{3,1},{4,6},{5,7},{6,4},{7,5},{8,10},{9,11},{10,... | collective-permute-start | bytes 12296 | tf_op jit(solution)/shard_map/ppermute | solution.py:654
  33.9 0.0 collective-permute-done.10.s3
  33.9 1.3 %collective-permute-done.8.s1 = f32[8,128]{1,0:T(8,128)S(1)} collective-permute-done((f32[8,128]{1,0:T(8,128)S(1)}, f32[8,128]{1,0:T(8,128)S(1)}, u32[]{:S(2)}, u32[]{:S(2)}) %collective-permute-start.8) | collective-permute-done | bytes 4128 | tf_op jit(solution)/shard_map/ppermute | solution.py:654
  35.2 0.7 collective-permute-done.9.s2
  36.0 0.0 copy-start.3
  36.0 0.0 copy-start.15
  36.0 2.3 %head.1 = (f32[4,1664]{1,0:T(4,128)S(1)}, f32[4,640]{1,0:T(4,128)S(1)}, f32[4,640]{1,0:T(4,128)S(1)}) custom-call(s32[2]{0:T(128)S(1)} %pad_add_fusion.meta, f32[8,128]{1,0:T(8,128)S(1)} %get-tuple-element.36.s0, f32[8,128]{1,0:T(8,128)S(1)} %collective-permute-done.8.s1, f32[8,128]{1,0:T(8,128)S(1)} %collective-permute-done.9.s2, ...), custom_call_target="tpu_custom_call" | custom-call | flops 10000000000 | tf_op jit(solution)/shard_map/head/pallas_call | solution.py:418
  38.4 0.6 collective-permute-start.11
  38.9 1.2 %collective-permute-start.12 = (f32[4,640]{1,0:T(4,128)S(1)}, f32[4,640]{1,0:T(4,128)S(1)}, u32[]{:S(2)}, u32[]{:S(2)}) collective-permute-start(f32[4,640]{1,0:T(4,128)S(1)} %get-tuple-element.40), channel_id=1, source_target_pairs={{0,3},{1,0},{2,1},{3,2},{4,7},{5,4},{6,5},{7,6},{8,11},{9,8},{10,9... | collective-permute-start | bytes 30728 | tf_op jit(solution)/shard_map/ppermute | solution.py:654
  40.1 1.4 %collective-permute-done.11 = f32[4,640]{1,0:T(4,128)S(1)} collective-permute-done((f32[4,640]{1,0:T(4,128)S(1)}, f32[4,640]{1,0:T(4,128)S(1)}, u32[]{:S(2)}, u32[]{:S(2)}) %collective-permute-start.11) | collective-permute-done | bytes 10272 | tf_op jit(solution)/shard_map/ppermute | solution.py:654
  41.5 0.0 collective-permute-done.12
  41.5 0.1 fusion.2
  41.7 13.6 %all_to_all.5.latents = bf16[8,4,2304]{2,1,0:T(4,128)(2,1)S(1)} all-to-all(bf16[8,4,2304]{2,1,0:T(4,128)(2,1)S(1)} %broadcast_in_dim.12), channel_id=1, replica_groups=mesh['frames'=8,'rows'=4] {'frames'}, dimensions={0} | all-to-all | bytes 294912 | tf_op jit(solution)/shard_map/all_to_all | solution.py:692
  55.3 0.0 copy-start.17
  55.4 2.7 %lift.1 = (f32[1920,640]{1,0:T(8,128)S(1)}, f32[16,128]{1,0:T(8,128)S(1)}) custom-call(s32[2]{0:T(128)S(1)} %pad_add_fusion.meta, bf16[27,4,128]{2,1,0:T(4,128)(2,1)S(1)} %bitcast.32, f32[1,128]{1,0:T(1,128)S(1)} %bitcast.45, bf16[8,4,2304]{2,1,0:T(4,128)(2,1)S(1)} %all_to_all.5.latents), custom_call_target="tpu_custom_call" | custom-call | flops 8000000000 | tf_op jit(solution)/shard_map/lift/pallas_call | solution.py:475
  58.1 0.4 collective-permute-start.13
  58.4 1.1 %collective-permute-start.14 = (f32[16,128]{1,0:T(8,128)S(1)}, f32[16,128]{1,0:T(8,128)S(1)}, u32[]{:S(2)}, u32[]{:S(2)}) collective-permute-start(f32[16,128]{1,0:T(8,128)S(1)} %get-tuple-element.41.s0), channel_id=1, source_target_pairs={{0,2},{1,3},{2,0},{3,1},{4,6},{5,7},{6,4},{7,5},{8,10},{9,11},{10,... | collective-permute-start | bytes 24584 | tf_op jit(solution)/shard_map/ppermute | solution.py:654
  59.5 1.4 %collective-permute-start.15 = (f32[16,128]{1,0:T(8,128)S(1)}, f32[16,128]{1,0:T(8,128)S(1)}, u32[]{:S(2)}, u32[]{:S(2)}) collective-permute-start(f32[16,128]{1,0:T(8,128)S(1)} %get-tuple-element.41.s0), channel_id=1, source_target_pairs={{0,3},{1,0},{2,1},{3,2},{4,7},{5,4},{6,5},{7,6},{8,11},{9,8},{10,9... | collective-permute-start | bytes 24584 | tf_op jit(solution)/shard_map/ppermute | solution.py:654
  60.9 0.3 collective-permute-done.13.s1
  61.2 0.9 %collective-permute-done.14.s2 = f32[16,128]{1,0:T(8,128)S(1)} collective-permute-done((f32[16,128]{1,0:T(8,128)S(1)}, f32[16,128]{1,0:T(8,128)S(1)}, u32[]{:S(2)}, u32[]{:S(2)}) %collective-permute-start.14) | collective-permute-done | bytes 8224 | tf_op jit(solution)/shard_map/ppermute | solution.py:654
  62.1 0.2 collective-permute-done.15.s3
  62.3 0.0 copy-done.16
  62.3 0.0 copy-start.18
  62.3 0.0 copy-start.19
  62.3 0.0 copy-start.20
  62.3 7.0 %time1.1 = (f32[3,10,80,256]{3,2,1,0:T(8,128)S(1)}, f32[8,128]{1,0:T(8,128)S(1)}) custom-call(s32[2]{0:T(128)S(1)} %pad_add_fusion.meta, f32[16,128]{1,0:T(8,128)S(1)} %get-tuple-element.41.s0, f32[16,128]{1,0:T(8,128)S(1)} %collective-permute-done.13.s1, f32[16,128]{1,0:T(8,128)S(1)} %collective-permute-done.14.s2, ...), custom_call_target="tpu_custom_call" | custom-call | flops 30000001024 | tf_op jit(solution)/shard_map/time1/pallas_call | solution.py:577
  69.3 0.8 %collective-permute-start.16 = (f32[8,128]{1,0:T(8,128)S(1)}, f32[8,128]{1,0:T(8,128)S(1)}, u32[]{:S(2)}, u32[]{:S(2)}) collective-permute-start(f32[8,128]{1,0:T(8,128)S(1)} %get-tuple-element.43.s0), channel_id=1, source_target_pairs={{0,1},{1,2},{2,3},{3,0},{4,5},{5,6},{6,7},{7,4},{8,9},{9,10},{10,1... | collective-permute-start | bytes 12296 | tf_op jit(solution)/shard_map/ppermute | solution.py:654
  70.1 1.3 %collective-permute-start.17 = (f32[8,128]{1,0:T(8,128)S(1)}, f32[8,128]{1,0:T(8,128)S(1)}, u32[]{:S(2)}, u32[]{:S(2)}) collective-permute-start(f32[8,128]{1,0:T(8,128)S(1)} %get-tuple-element.43.s0), channel_id=1, source_target_pairs={{0,2},{1,3},{2,0},{3,1},{4,6},{5,7},{6,4},{7,5},{8,10},{9,11},{10,... | collective-permute-start | bytes 12296 | tf_op jit(solution)/shard_map/ppermute | solution.py:654
  71.5 0.3 collective-permute-start.18
  71.7 0.7 collective-permute-done.16.s1
  72.4 1.3 %collective-permute-done.17.s2 = f32[8,128]{1,0:T(8,128)S(1)} collective-permute-done((f32[8,128]{1,0:T(8,128)S(1)}, f32[8,128]{1,0:T(8,128)S(1)}, u32[]{:S(2)}, u32[]{:S(2)}) %collective-permute-start.17) | collective-permute-done | bytes 4128 | tf_op jit(solution)/shard_map/ppermute | solution.py:654
  73.7 0.0 collective-permute-done.18.s3
  73.8 3.4 %time2.1 = bf16[1,8,160,128]{3,2,1,0:T(8,128)(2,1)} custom-call(s32[2]{0:T(128)S(1)} %pad_add_fusion.meta, f32[8,128]{1,0:T(8,128)S(1)} %get-tuple-element.43.s0, f32[8,128]{1,0:T(8,128)S(1)} %collective-permute-done.16.s1, f32[8,128]{1,0:T(8,128)S(1)} %collective-permute-done.17.s2, f32[8,128]{1,0:T(8,128)S(1)} %collective-permute-done.18.s3, ...), custom_call_target="tpu_custom_call" | custom-call | flops 12000000000 | tf_op jit(solution)/shard_map/time2/pallas_call | solution.py:636
  (35 shorter events, 0.1 us)
Async XLA Ops:
  0.0 8.0 %copy-start.4 = (f32[512]{0:T(512)S(1)}, f32[512]{0:T(512)}, u32[]{:S(2)}) copy-start(f32[512]{0:T(512)} %param.25) | copy-start | bytes 6148
  0.0 8.0 %copy-start.5 = (f32[512]{0:T(512)S(1)}, f32[512]{0:T(512)}, u32[]{:S(2)}) copy-start(f32[512]{0:T(512)} %param.26) | copy-start | bytes 6148
  0.0 8.0 %copy-start.6 = (f32[512]{0:T(512)S(1)}, f32[512]{0:T(512)}, u32[]{:S(2)}) copy-start(f32[512]{0:T(512)} %param.28) | copy-start | bytes 6148
  0.0 23.9 %slice-start = ((s8[4718592]{0:T(1024)(128)(4,1)}), s8[524288]{0:T(1024)(128)(4,1)S(1)}, s32[]{:S(2)}) async-start(s8[4718592]{0:T(1024)(128)(4,1)} %bitcast.26), calls=%async_computation.1 | async-start | bytes 1048576
  1.6 6.4 %collective-permute-start = (f32[8,128]{1,0:T(8,128)S(1)}, f32[8,128]{1,0:T(8,128)S(1)}, u32[]{:S(2)}, u32[]{:S(2)}) collective-permute-start(f32[8,128]{1,0:T(8,128)S(1)} %get-tuple-element.25.s0), channel_id=1, source_target_pairs={{0,1},{1,2},{2,3},{3,0},{4,5},{5,6},{6,7},{7,4},{8,9},{9,10},{10,1... | collective-permute-start | bytes 12296 | tf_op jit(solution)/shard_map/ppermute | solution.py:654
  2.2 5.8 %collective-permute-start.1 = (f32[8,128]{1,0:T(8,128)S(1)}, f32[8,128]{1,0:T(8,128)S(1)}, u32[]{:S(2)}, u32[]{:S(2)}) collective-permute-start(f32[8,128]{1,0:T(8,128)S(1)} %get-tuple-element.25.s0), channel_id=1, source_target_pairs={{0,2},{1,3},{2,0},{3,1},{4,6},{5,7},{6,4},{7,5},{8,10},{9,11},{10,... | collective-permute-start | bytes 12296 | tf_op jit(solution)/shard_map/ppermute | solution.py:654
  4.8 3.2 %collective-permute-start.2 = (f32[8,128]{1,0:T(8,128)S(1)}, f32[8,128]{1,0:T(8,128)S(1)}, u32[]{:S(2)}, u32[]{:S(2)}) collective-permute-start(f32[8,128]{1,0:T(8,128)S(1)} %get-tuple-element.25.s0), channel_id=1, source_target_pairs={{0,3},{1,0},{2,1},{3,2},{4,7},{5,4},{6,5},{7,6},{8,11},{9,8},{10,9... | collective-permute-start | bytes 12296 | tf_op jit(solution)/shard_map/ppermute | solution.py:654
  6.1 9.4 %collective-permute-start.3 = (bf16[2,160,512]{2,1,0:T(8,128)(2,1)S(1)}, bf16[2,160,512]{2,1,0:T(8,128)(2,1)S(1)}, u32[]{:S(2)}, u32[]{:S(2)}) collective-permute-start(bf16[2,160,512]{2,1,0:T(8,128)(2,1)S(1)} %get-tuple-element.26), channel_id=1, source_target_pairs={{0,1},{1,2},{2,3},{3,0},{4,5},{5,6},{6,7},{7,4},{8,9},{9,10},{10,1... | collective-permute-start | bytes 983048 | tf_op jit(solution)/shard_map/ppermute | solution.py:654
  6.2 9.4 %collective-permute-start.4 = (bf16[2,160,512]{2,1,0:T(8,128)(2,1)S(1)}, bf16[2,160,512]{2,1,0:T(8,128)(2,1)S(1)}, u32[]{:S(2)}, u32[]{:S(2)}) collective-permute-start(bf16[2,160,512]{2,1,0:T(8,128)(2,1)S(1)} %get-tuple-element.27), channel_id=1, source_target_pairs={{0,3},{1,0},{2,1},{3,2},{4,7},{5,4},{6,5},{7,6},{8,11},{9,8},{10,9... | collective-permute-start | bytes 983048 | tf_op jit(solution)/shard_map/ppermute | solution.py:654
  8.0 15.9 %slice-start.1 = ((s8[4718592]{0:T(1024)(128)(4,1)}), s8[4194304]{0:T(1024)(128)(4,1)S(1)}, s32[]{:S(2)}) async-start(s8[4718592]{0:T(1024)(128)(4,1)} %bitcast.26), calls=%async_computation.2 | async-start | bytes 8388608
  15.6 8.3 %copy-start.7 = (f32[512]{0:T(512)S(1)}, f32[512]{0:T(512)}, u32[]{:S(2)}) copy-start(f32[512]{0:T(512)} %param.29) | copy-start | bytes 6148
  15.6 8.3 %copy-start.8 = (f32[512]{0:T(512)S(1)}, f32[512]{0:T(512)}, u32[]{:S(2)}) copy-start(f32[512]{0:T(512)} %param.30) | copy-start | bytes 6148
  15.6 8.3 %copy-start.9 = (f32[512]{0:T(512)S(1)}, f32[512]{0:T(512)}, u32[]{:S(2)}) copy-start(f32[512]{0:T(512)} %param.32) | copy-start | bytes 6148
  19.8 3.1 %collective-permute-start.5 = (f32[8,128]{1,0:T(8,128)S(1)}, f32[8,128]{1,0:T(8,128)S(1)}, u32[]{:S(2)}, u32[]{:S(2)}) collective-permute-start(f32[8,128]{1,0:T(8,128)S(1)} %get-tuple-element.33.s0), channel_id=1, source_target_pairs={{0,1},{1,2},{2,3},{3,0},{4,5},{5,6},{6,7},{7,4},{8,9},{9,10},{10,1... | collective-permute-start | bytes 12296 | tf_op jit(solution)/shard_map/ppermute | solution.py:654
  20.3 3.6 %collective-permute-start.6 = (f32[8,128]{1,0:T(8,128)S(1)}, f32[8,128]{1,0:T(8,128)S(1)}, u32[]{:S(2)}, u32[]{:S(2)}) collective-permute-start(f32[8,128]{1,0:T(8,128)S(1)} %get-tuple-element.33.s0), channel_id=1, source_target_pairs={{0,2},{1,3},{2,0},{3,1},{4,6},{5,7},{6,4},{7,5},{8,10},{9,11},{10,... | collective-permute-start | bytes 12296 | tf_op jit(solution)/shard_map/ppermute | solution.py:654
  21.4 2.5 %collective-permute-start.7 = (f32[8,128]{1,0:T(8,128)S(1)}, f32[8,128]{1,0:T(8,128)S(1)}, u32[]{:S(2)}, u32[]{:S(2)}) collective-permute-start(f32[8,128]{1,0:T(8,128)S(1)} %get-tuple-element.33.s0), channel_id=1, source_target_pairs={{0,3},{1,0},{2,1},{3,2},{4,7},{5,4},{6,5},{7,6},{8,11},{9,8},{10,9... | collective-permute-start | bytes 12296 | tf_op jit(solution)/shard_map/ppermute | solution.py:654
  23.9 12.0 %copy-start.2 = (bf16[3,3,512,8]{2,3,1,0:T(8,128)(2,1)S(1)}, bf16[3,3,512,8]{2,3,1,0:T(8,128)(2,1)}, u32[]{:S(2)}) copy-start(bf16[3,3,512,8]{2,3,1,0:T(8,128)(2,1)} %param.35) | copy-start | bytes 221188
  23.9 12.0 %copy-start.10 = (f32[512]{0:T(512)S(1)}, f32[512]{0:T(512)}, u32[]{:S(2)}) copy-start(f32[512]{0:T(512)} %param.33) | copy-start | bytes 6148
  24.0 12.0 %copy-start.11 = (f32[512]{0:T(512)S(1)}, f32[512]{0:T(512)}, u32[]{:S(2)}) copy-start(f32[512]{0:T(512)} %param.34) | copy-start | bytes 6148
  24.0 12.0 %copy-start.12 = (f32[8,4]{0,1:T(4,128)S(1)}, f32[8,4]{0,1:T(4,128)}, u32[]{:S(2)}) copy-start(f32[8,4]{0,1:T(4,128)} %param.37) | copy-start | bytes 388
  24.0 12.0 %copy-start.13 = (f32[8]{0:T(128)S(1)}, f32[8]{0:T(128)}, u32[]{:S(2)}) copy-start(f32[8]{0:T(128)} %b_ref.1) | copy-start | bytes 100
  24.0 12.0 %copy-start.14 = (f32[4]{0:T(128)S(1)}, f32[4]{0:T(128)}, u32[]{:S(2)}) copy-start(f32[4]{0:T(128)} %qb_ref.1) | copy-start | bytes 52
  31.3 2.6 %collective-permute-start.10 = (f32[8,128]{1,0:T(8,128)S(1)}, f32[8,128]{1,0:T(8,128)S(1)}, u32[]{:S(2)}, u32[]{:S(2)}) collective-permute-start(f32[8,128]{1,0:T(8,128)S(1)} %get-tuple-element.36.s0), channel_id=1, source_target_pairs={{0,3},{1,0},{2,1},{3,2},{4,7},{5,4},{6,5},{7,6},{8,11},{9,8},{10,9... | collective-permute-start | bytes 12296 | tf_op jit(solution)/shard_map/ppermute | solution.py:654
  32.2 3.0 %collective-permute-start.8 = (f32[8,128]{1,0:T(8,128)S(1)}, f32[8,128]{1,0:T(8,128)S(1)}, u32[]{:S(2)}, u32[]{:S(2)}) collective-permute-start(f32[8,128]{1,0:T(8,128)S(1)} %get-tuple-element.36.s0), channel_id=1, source_target_pairs={{0,1},{1,2},{2,3},{3,0},{4,5},{5,6},{6,7},{7,4},{8,9},{9,10},{10,1... | collective-permute-start | bytes 12296 | tf_op jit(solution)/shard_map/ppermute | solution.py:654
  32.3 3.6 %collective-permute-start.9 = (f32[8,128]{1,0:T(8,128)S(1)}, f32[8,128]{1,0:T(8,128)S(1)}, u32[]{:S(2)}, u32[]{:S(2)}) collective-permute-start(f32[8,128]{1,0:T(8,128)S(1)} %get-tuple-element.36.s0), channel_id=1, source_target_pairs={{0,2},{1,3},{2,0},{3,1},{4,6},{5,7},{6,4},{7,5},{8,10},{9,11},{10,... | collective-permute-start | bytes 12296 | tf_op jit(solution)/shard_map/ppermute | solution.py:654
  36.0 19.4 %copy-start.3 = (bf16[3,3,3,4,128]{4,3,2,1,0:T(4,128)(2,1)S(1)}, bf16[3,3,3,4,128]{4,3,2,1,0:T(4,128)(2,1)}, u32[]{:S(2)}) copy-start(bf16[3,3,3,4,128]{4,3,2,1,0:T(4,128)(2,1)} %param.39) | copy-start | bytes 82948
  36.0 19.3 %copy-start.15 = (f32[128]{0:T(128)S(1)}, f32[128]{0:T(128)}, u32[]{:S(2)}) copy-start(f32[128]{0:T(128)} %param.40) | copy-start | bytes 1540
  38.4 3.2 %collective-permute-start.11 = (f32[4,640]{1,0:T(4,128)S(1)}, f32[4,640]{1,0:T(4,128)S(1)}, u32[]{:S(2)}, u32[]{:S(2)}) collective-permute-start(f32[4,640]{1,0:T(4,128)S(1)} %get-tuple-element.39), channel_id=1, source_target_pairs={{0,1},{1,2},{2,3},{3,0},{4,5},{5,6},{6,7},{7,4},{8,9},{9,10},{10,1... | collective-permute-start | bytes 30728 | tf_op jit(solution)/shard_map/ppermute | solution.py:654
  38.9 2.6 %collective-permute-start.12 = (f32[4,640]{1,0:T(4,128)S(1)}, f32[4,640]{1,0:T(4,128)S(1)}, u32[]{:S(2)}, u32[]{:S(2)}) collective-permute-start(f32[4,640]{1,0:T(4,128)S(1)} %get-tuple-element.40), channel_id=1, source_target_pairs={{0,3},{1,0},{2,1},{3,2},{4,7},{5,4},{6,5},{7,6},{8,11},{9,8},{10,9... | collective-permute-start | bytes 30728 | tf_op jit(solution)/shard_map/ppermute | solution.py:654
  55.3 7.0 %copy-start = (bf16[3,3,3,128,128]{4,3,2,1,0:T(8,128)(2,1)S(1)}, bf16[3,3,3,128,128]{4,3,2,1,0:T(8,128)(2,1)}, u32[]{:S(2)}) copy-start(bf16[3,3,3,128,128]{4,3,2,1,0:T(8,128)(2,1)} %param.43) | copy-start | bytes 2654212
  55.3 7.0 %copy-start.16 = (f32[128]{0:T(128)S(1)}, f32[128]{0:T(128)}, u32[]{:S(2)}) copy-start(f32[128]{0:T(128)} %param.41) | copy-start | bytes 1540
  55.3 7.0 %copy-start.17 = (f32[128]{0:T(128)S(1)}, f32[128]{0:T(128)}, u32[]{:S(2)}) copy-start(f32[128]{0:T(128)} %param.42) | copy-start | bytes 1540
  58.1 3.1 %collective-permute-start.13 = (f32[16,128]{1,0:T(8,128)S(1)}, f32[16,128]{1,0:T(8,128)S(1)}, u32[]{:S(2)}, u32[]{:S(2)}) collective-permute-start(f32[16,128]{1,0:T(8,128)S(1)} %get-tuple-element.41.s0), channel_id=1, source_target_pairs={{0,1},{1,2},{2,3},{3,0},{4,5},{5,6},{6,7},{7,4},{8,9},{9,10},{10,1... | collective-permute-start | bytes 24584 | tf_op jit(solution)/shard_map/ppermute | solution.py:654
  58.4 3.7 %collective-permute-start.14 = (f32[16,128]{1,0:T(8,128)S(1)}, f32[16,128]{1,0:T(8,128)S(1)}, u32[]{:S(2)}, u32[]{:S(2)}) collective-permute-start(f32[16,128]{1,0:T(8,128)S(1)} %get-tuple-element.41.s0), channel_id=1, source_target_pairs={{0,2},{1,3},{2,0},{3,1},{4,6},{5,7},{6,4},{7,5},{8,10},{9,11},{10,... | collective-permute-start | bytes 24584 | tf_op jit(solution)/shard_map/ppermute | solution.py:654
  59.5 2.8 %collective-permute-start.15 = (f32[16,128]{1,0:T(8,128)S(1)}, f32[16,128]{1,0:T(8,128)S(1)}, u32[]{:S(2)}, u32[]{:S(2)}) collective-permute-start(f32[16,128]{1,0:T(8,128)S(1)} %get-tuple-element.41.s0), channel_id=1, source_target_pairs={{0,3},{1,0},{2,1},{3,2},{4,7},{5,4},{6,5},{7,6},{8,11},{9,8},{10,9... | collective-permute-start | bytes 24584 | tf_op jit(solution)/shard_map/ppermute | solution.py:654
  62.3 11.4 %copy-start.1 = (bf16[3,3,3,128,128]{4,3,2,1,0:T(8,128)(2,1)S(1)}, bf16[3,3,3,128,128]{4,3,2,1,0:T(8,128)(2,1)}, u32[]{:S(2)}) copy-start(bf16[3,3,3,128,128]{4,3,2,1,0:T(8,128)(2,1)} %param.46) | copy-start | bytes 2654212
  62.3 11.4 %copy-start.18 = (f32[128]{0:T(128)S(1)}, f32[128]{0:T(128)}, u32[]{:S(2)}) copy-start(f32[128]{0:T(128)} %param.44) | copy-start | bytes 1540
  62.3 11.4 %copy-start.19 = (f32[128]{0:T(128)S(1)}, f32[128]{0:T(128)}, u32[]{:S(2)}) copy-start(f32[128]{0:T(128)} %param.45) | copy-start | bytes 1540
  62.3 11.4 %copy-start.20 = (f32[128]{0:T(128)S(1)}, f32[128]{0:T(128)}, u32[]{:S(2)}) copy-start(f32[128]{0:T(128)} %param.47) | copy-start | bytes 1540
  69.3 3.1 %collective-permute-start.16 = (f32[8,128]{1,0:T(8,128)S(1)}, f32[8,128]{1,0:T(8,128)S(1)}, u32[]{:S(2)}, u32[]{:S(2)}) collective-permute-start(f32[8,128]{1,0:T(8,128)S(1)} %get-tuple-element.43.s0), channel_id=1, source_target_pairs={{0,1},{1,2},{2,3},{3,0},{4,5},{5,6},{6,7},{7,4},{8,9},{9,10},{10,1... | collective-permute-start | bytes 12296 | tf_op jit(solution)/shard_map/ppermute | solution.py:654
  70.1 3.6 %collective-permute-start.17 = (f32[8,128]{1,0:T(8,128)S(1)}, f32[8,128]{1,0:T(8,128)S(1)}, u32[]{:S(2)}, u32[]{:S(2)}) collective-permute-start(f32[8,128]{1,0:T(8,128)S(1)} %get-tuple-element.43.s0), channel_id=1, source_target_pairs={{0,2},{1,3},{2,0},{3,1},{4,6},{5,7},{6,4},{7,5},{8,10},{9,11},{10,... | collective-permute-start | bytes 12296 | tf_op jit(solution)/shard_map/ppermute | solution.py:654
  71.5 2.3 %collective-permute-start.18 = (f32[8,128]{1,0:T(8,128)S(1)}, f32[8,128]{1,0:T(8,128)S(1)}, u32[]{:S(2)}, u32[]{:S(2)}) collective-permute-start(f32[8,128]{1,0:T(8,128)S(1)} %get-tuple-element.43.s0), channel_id=1, source_target_pairs={{0,3},{1,0},{2,1},{3,2},{4,7},{5,4},{6,5},{7,6},{8,11},{9,8},{10,9... | collective-permute-start | bytes 12296 | tf_op jit(solution)/shard_map/ppermute | solution.py:654

commit v3 on v2

--- a/solution.py
+++ b/solution.py
@@ -6,6 +6,7 @@
 from jax.experimental import pallas as pl
 from jax.experimental.pallas import tpu as pltpu
 from jax.sharding import PartitionSpec as P
+
 
 GROUPS = 32
 EPS = 1e-06
@@ -78,10 +79,11 @@
         slots[row, :, slot * channels + at : slot * channels + at + width] = piece.astype(BF16)
 
 
-def input_sums_kernel(x_hbm, x_ref, top_ref, bottom_ref, out_ref, sems):
+def input_sums_kernel(meta, x_hbm, x_ref, near_ref, far_ref, out_ref, sems):
     lines, width, channels = x_ref.shape
-    halo = top_ref.shape[0]
+    halo = near_ref.shape[0]
     rows = channels // LANES
+    even = (meta[0] & 1) == 0
     copies = [pltpu.make_async_copy(x_hbm.at[r], x_ref.at[r], sems.at[r]) for r in range(lines)]
     for copy in copies:
         copy.start()
@@ -93,28 +95,33 @@
             v = x_ref[r, :, k * LANES : (k + 1) * LANES].astype(F32).reshape(width // 8, 8, LANES)
             first[k] = first[k] + v.sum(0)
             second[k] = second[k] + (v * v).sum(0)
-        if r < halo:
-            top_ref[r] = x_ref[r]
-        if r >= lines - halo:
-            bottom_ref[r - (lines - halo)] = x_ref[r]
+    for r in range(halo):
+        top, bottom = x_ref[r], x_ref[lines - halo + r]
+        near_ref[r] = jnp.where(even, bottom, top)
+        far_ref[r] = jnp.where(even, top, bottom)
     for k in range(rows):
         out_ref[k : k + 1, :] = first[k].sum(0, keepdims=True)
         out_ref[rows + k : rows + k + 1, :] = second[k].sum(0, keepdims=True)
 
 
-def input_sums(x, halo):
+def input_sums(meta, x, halo):
     lines, width, channels = x.shape
     edge = pltpu.VMEM((halo, width, channels), BF16)
     return pl.pallas_call(
         input_sums_kernel,
-        out_shape=(pltpu.VMEM(x.shape, BF16), edge, edge, jax.ShapeDtypeStruct((2 * channels // LANES, LANES), F32)),
-        in_specs=[HBM],
-        out_specs=(VMEM, VMEM, VMEM, VMEM),
+        out_shape=(
+            pltpu.VMEM(x.shape, BF16),
+            edge,
+            edge,
+            jax.ShapeDtypeStruct((2 * channels // LANES, LANES), F32),
+        ),
+        in_specs=[SMEM, HBM],
+        out_specs=(VMEM,) * 4,
         scratch_shapes=[pltpu.SemaphoreType.DMA((lines,))],
         compiler_params=params(8),
         cost_estimate=cost(6e9),
         name="input_sums",
-    )(in_hbm(x))
+    )(meta, in_hbm(x))
 
 
 def norm_line(slots, row, read, scale, move, inside, channels, keep=None):
@@ -129,33 +136,20 @@
         spread_columns(slots, row, at, even, odd, channels)
 
 
-def block_conv(slots, weights, first, lines, channels, between=(), waits=None):
+def block_conv(slots, weights, firsts, lines, channels, between=()):
     half = slots.shape[1]
     acc = None
     for i in range(3):
-
-        def dot(j, taps, i=i):
-            parts = [
-                slots[first + i : first + i + lines, :, (p + j) * channels : (p + j + taps) * channels].reshape(
-                    lines * half, taps * channels
-                )
-                for p in range(2)
-            ]
-            tap_weights = weights[i, j * channels : (j + taps) * channels, :]
-            return jnp.dot(jnp.concatenate(parts, axis=0), tap_weights, preferred_element_type=F32)
-
-        if waits is None:
-            part = dot(0, 3)
-        else:
-            part = None
-            for j in range(3):
-                waits[3 * i + j].wait()
-                one = dot(j, 1)
-                part = one if part is None else part + one
+        parts = [
+            slots[f + i : f + i + lines, :, p * channels : (p + 3) * channels].reshape(lines * half, 3 * channels)
+            for p in range(2)
+            for f in firsts
+        ]
+        part = jnp.dot(jnp.concatenate(parts, axis=0), weights[i], preferred_element_type=F32)
         acc = part if acc is None else acc + part
         if i < len(between):
             between[i]()
-    return acc.reshape(2, lines, half, channels)
+    return acc.reshape(2, len(firsts) * lines, half, channels)
 
 
 class Sums:
@@ -176,18 +170,12 @@
             out_ref[...] += base[...]
 
 
-def conv1a_kernel(
-    s0, s1, s2, s3, gain, shift, bias, x_ref, w_hbm, h_ref, xp_ref, slots, wv, stats_ref, rowf, wsems,
+def conv1_kernel(
+    s0, s1, s2, s3, gain, shift, bias, x_ref, w_ref, h_ref, xp_ref, slots, stats_ref, rowf,
     *, halo, count, per_group,
 ):
     own, width, channels = x_ref.shape
     half = width // 2
-    loads = []
-    for i in range(3):
-        for j in range(3):
-            rows = pl.ds(j * channels, channels)
-            loads.append(pltpu.make_async_copy(w_hbm.at[i, rows], wv.at[i, rows], wsems.at[3 * i + j]))
-            loads[-1].start()
     scale, move = half_affine((s0, s1, s2, s3), channels // LANES, gain[...], shift[...], count, per_group)
     scale, move = as_row(scale), as_row(move)
     offset = bias[...].reshape(1, 1, 1, channels)
@@ -204,7 +192,7 @@
     norm(1)
     for b in range(0, own - 2, 2):
         lines = [functools.partial(norm, r) for r in (range(2, 6) if b == 0 else range(b + 4, b + 6)) if r < own]
-        acc = block_conv(slots, wv, halo + b, 2, channels, lines[:2], loads if b == 0 else None) + offset
+        acc = block_conv(slots, w_ref, [halo + b], 2, channels, lines[:2]) + offset
         for line in lines[2:]:
             line()
         for r in range(2):
@@ -214,41 +202,46 @@
     sums.put(stats_ref)
 
 
-def conv1b_kernel(
-    meta, s0, s1, s2, s3, gain, shift, bias, up_ref, low_ref, base, wv, h_in, slots_in,
-    h_ref, slots, stats_ref, rowf, *, count, per_group, n_blocks,
+def conv1_edge_kernel(
+    meta, s0, s1, s2, s3, gain, shift, bias, near_ref, far_ref, base, w_ref, h_in, slots_in, h_ref, slots, *rest,
+    distance, count, per_group, n_blocks,
 ):
-    halo, width, channels = up_ref.shape
+    rowf = rest[-1]
+    halo, width, channels = near_ref.shape
     half = width // 2
     lines = slots.shape[0]
+    even_block = (meta[0] & 1) == 0
     scale, move = half_affine((s0, s1, s2, s3), channels // LANES, gain[...], shift[...], count, per_group)
     scale, move = as_row(scale), as_row(move)
     offset = bias[...].reshape(1, 1, 1, channels)
+
+    def norm(above, r, inside, at, spare):
+        def read(chunk, cols):
+            near, far = near_ref[r, :, cols].astype(F32), far_ref[r, :, cols].astype(F32)
+            rowf[spare, chunk] = jnp.where(even_block == above, far, near)
+            return rowf[spare, chunk, pl.ds(0, half, stride=2), :], rowf[spare, chunk, pl.ds(1, half, stride=2), :]
+
+        norm_line(slots, at, read, scale, move, inside, channels)
+
+    top, bottom = halo - 1 - distance, lines - halo + distance
+    norm(True, top, meta[0] > 0, top, 0)
+    norm(False, distance, meta[0] < n_blocks - 1, bottom, 1)
+    places = (top, bottom - 2)
+    acc = block_conv(slots, w_ref, places, 1, channels) + offset
     sums = Sums(channels)
-
-    def norm(source, r, inside, at):
-        def read(chunk, cols):
-            rowf[at, chunk] = source[r, :, cols].astype(F32)
-            return rowf[at, chunk, pl.ds(0, half, stride=2), :], rowf[at, chunk, pl.ds(1, half, stride=2), :]
-
-        norm_line(slots, at, read, scale, move, inside, channels)
-
-    for r in range(halo):
-        norm(up_ref, r, meta[0] > 0, r)
-    later = [functools.partial(norm, low_ref, r, meta[0] < n_blocks - 1, lines - halo + r) for r in range(halo)]
-    for first, mine in ((0, 1), (lines - 4, 0)):
-        acc = block_conv(slots, wv, first, 2, channels, later if first == 0 else ()) + offset
-        for r in range(2):
-            for p in range(2):
-                h_ref[first + r, p] = acc[p, r]
-                if r == mine:
-                    sums.add(acc[p, r])
-    sums.put(stats_ref, base)
-
-
-def conv1(meta, stats, gain, shift, bias, x, up, low, weight, n_blocks):
+    for k, place in enumerate(places):
+        for p in range(2):
+            h_ref[place, p] = acc[p, k]
+            if distance == 0:
+                sums.add(acc[p, k])
+    if distance == 0:
+        sums.put(rest[0], base)
+
+
+def conv1(meta, stats, gain, shift, bias, x, halos, weight, n_blocks):
+    near, far = halos
     own, width, channels = x.shape
-    halo = up.shape[0]
+    halo = near.shape[0]
     lines = own + 2 * halo
     half = width // 2
     rows = channels // LANES
@@ -257,44 +250,43 @@
     h_type = pltpu.VMEM((lines - 2, 2, half, channels), F32)
     slots_type = pltpu.VMEM((lines, half, 4 * channels), BF16)
     stats_type = jax.ShapeDtypeStruct((2 * rows, LANES), F32)
-    h, xp, slots, wv, base = pl.pallas_call(
-        functools.partial(conv1a_kernel, halo=halo, **settings),
+    h, xp, slots, base = pl.pallas_call(
+        functools.partial(conv1_kernel, halo=halo, **settings),
         out_shape=(
             h_type,
             pltpu.VMEM((own, 2, half, channels), BF16),
             slots_type,
-            pltpu.VMEM((3, 3 * channels, channels), BF16),
             stats_type,
         ),
-        in_specs=[VMEM] * 8 + [HBM],
-        out_specs=(VMEM,) * 5,
-        scratch_shapes=[
-            pltpu.VMEM((own, channels // LANES, width, LANES), F32),
-            pltpu.SemaphoreType.DMA((9,)),
-        ],
+        in_specs=[VMEM] * 9,
+        out_specs=(VMEM,) * 4,
+        scratch_shapes=[pltpu.VMEM((own, channels // LANES, width, LANES), F32)],
         compiler_params=params(26),
         cost_estimate=cost(25e9),
-        name="conv1a",
-    )(*stats, gain, shift, bias, x, in_hbm(weight.reshape(3, 3 * channels, channels)))
-    h, _, sums = pl.pallas_call(
-        functools.partial(conv1b_kernel, n_blocks=n_blocks, **settings),
-        out_shape=(h_type, slots_type, stats_type),
-        in_specs=[SMEM] + [VMEM] * 13,
-        out_specs=(VMEM,) * 3,
-        scratch_shapes=[pltpu.VMEM((lines, channels // LANES, width, LANES), F32)],
-        input_output_aliases={12: 0, 13: 1},
-        compiler_params=params(26),
-        cost_estimate=cost(20e9),
-        name="conv1b",
-    )(meta, *stats, gain, shift, bias, up, low, base, wv, h, slots)
-    return h, xp, sums
+        name="conv1",
+    )(*stats, gain, shift, bias, x, weight)
+
+    def edge(distance, h, slots):
+        return pl.pallas_call(
+            functools.partial(conv1_edge_kernel, distance=distance, n_blocks=n_blocks, **settings),
+            out_shape=(h_type, slots_type) + ((stats_type,) if distance == 0 else ()),
+            in_specs=[SMEM] + [VMEM] * 13,
+            out_specs=(VMEM,) * (3 if distance == 0 else 2),
+            scratch_shapes=[pltpu.VMEM((2, channels // LANES, width, LANES), F32)],
+            input_output_aliases={12: 0, 13: 1},
+            compiler_params=params(26),
+            cost_estimate=cost(10e9),
+        )(meta, *stats, gain, shift, bias, near, far, base, weight, h, slots)
+
+    h, slots, sums = edge(0, h, slots)
+    return xp, sums, lambda: edge(1, h, slots)[0]
 
 
 def conv2_kernel(
     meta, s0, s1, s2, s3, gain, shift, bias, hs, xs, wv, y_ref, stats_ref, slots,
     *, count, per_group, n_blocks,
 ):
-    lines, _, half, channels = hs.shape
+    lines, _, _, channels = hs.shape
     own = lines - 2
     scale, move = half_affine((s0, s1, s2, s3), channels // LANES, gain[...], shift[...], count, per_group)
     scale, move = as_row(scale), as_row(move)
@@ -313,7 +305,7 @@
     norm(1)
     for b in range(0, own, 2):
         ahead = [functools.partial(norm, r) for r in (range(2, 6) if b == 0 else range(b + 4, b + 6)) if r < lines]
-        acc = block_conv(slots, wv, b, 2, channels, ahead[:2]) + offset
+        acc = block_conv(slots, wv, [b], 2, channels, ahead[:2]) + offset
         for line in ahead[2:]:
             line()
         for r in range(2):
@@ -457,13 +449,15 @@
                     row = at + (n_frames - 3 - g + t) * each
                     weights[row : row + each, g * channels : (g + 1) * channels] = tap
     lhs = jnp.transpose(patches[...], (1, 0)).astype(BF16)
-    for g in range(n_out):
-        cols = slice(g * channels, (g + 1) * channels)
-        value = jnp.dot(lhs, weights[:, cols].astype(BF16), preferred_element_type=F32) + bias_ref[...]
-        t0_ref[:, cols] = value
-        mine = value[2 * width : (2 + own) * width]
-        stats_ref[g : g + 1, :] = mine.sum(0, keepdims=True)
-        stats_ref[n_out + g : n_out + g + 1, :] = (mine * mine).sum(0, keepdims=True)
+    for start in range(0, n_out, 2):
+        pair = slice(start * channels, min(start + 2, n_out) * channels)
+        values = jnp.dot(lhs, weights[:, pair].astype(BF16), preferred_element_type=F32)
+        for g in range(start, min(start + 2, n_out)):
+            value = values[:, (g - start) * channels : (g - start + 1) * channels] + bias_ref[...]
+            t0_ref[:, g * channels : (g + 1) * channels] = value
+            mine = value[2 * width : (2 + own) * width].reshape(-1, 8, channels)
+            stats_ref[g : g + 1, :] = mine.sum(0).sum(0, keepdims=True)
+            stats_ref[n_out + g : n_out + g + 1, :] = (mine * mine).sum(0).sum(0, keepdims=True)
 
 
 def lift(meta, weight, bias, latents, own, half, n_frames, n_out):
@@ -532,33 +526,39 @@
     return [(k + 2 - t, r) for k, first in blocks for t in range(3) for r in range(first, first + lines + 2)]
 
 
-def time1_kernel(
-    meta, s0, s1, s2, s3, gain, shift, ts, w_ref, t1v, stats_ref, slots,
-    *, count, per_group, n_blocks, own, n_out,
-):
-    frames, lines, half, _ = slots.shape
-    channels = gain.shape[1]
+def time1_line(ts, slots, meta, scale, move, n_blocks, own):
+    half, depth = slots.shape[2], slots.shape[3]
+    channels = depth // 4
     width = 2 * half
-    scale, move = half_affine((s0, s1, s2, s3), frames, gain[...], shift[...], count, per_group)
-    first_line = meta[0] * own - 2
 
     def norm(k, r):
-        line = first_line + r
-        inside = (line >= 0) & (line < n_blocks * own) & (meta[1] >= k)
+        line = meta[0] * own - 2 + r
+        inside = meta[1] >= k
+        if r < 2 or r >= own + 2:
+            inside = inside & (line >= 0) & (line < n_blocks * own)
         at = r * width
         cols = slice(k * channels, (k + 1) * channels)
         even = half_silu(ts[at : at + half, cols], scale[k : k + 1], move[k : k + 1])
         odd = half_silu(ts[at + half : at + width, cols], scale[k : k + 1], move[k : k + 1])
         spread_columns(slots.at[k], r, 0, jnp.where(inside, even, 0.0), jnp.where(inside, odd, 0.0), channels)
 
-    part_lines = (lines - 2) // 2
-    blocks = [(k, first) for first in (0, part_lines) for k in reversed(range(n_out))]
+    return norm
+
+
+def time1_kernel(
+    meta, s0, s1, s2, s3, gain, shift, ts, w_ref, t1v, slots, stats_ref, *, count, per_group, n_blocks, own, n_out,
+):
+    frames, _, half, _ = slots.shape
+    channels = gain.shape[1]
+    scale, move = half_affine((s0, s1, s2, s3), frames, gain[...], shift[...], count, per_group)
+    norm = time1_line(ts, slots, meta, scale, move, n_blocks, own)
+    part_lines = own // 2
+    blocks = [(k, first) for first in (1, 1 + part_lines) for k in reversed(range(n_out))]
     sums = [[jnp.zeros((8, 2 * channels), F32)] * 2 for _ in range(n_out)]
 
     def finish(k, first, acc):
         t1v[k, first : first + part_lines] = acc.reshape(part_lines, half, 2 * channels)
-        skip = 1 if first == 0 else 0
-        mine = acc[skip * half : (skip + part_lines - 1) * half].reshape(-1, 8, 2 * channels)
+        mine = acc.reshape(-1, 8, 2 * channels)
         sums[k] = [sums[k][0] + mine.sum(0), sums[k][1] + (mine * mine).sum(0)]
 
     ahead = Ahead(block_order(blocks, part_lines), norm)
@@ -570,28 +570,64 @@
             stats_ref[row : row + 1, :] = value[:, :channels] + value[:, channels:]
 
 
+def time1_edge_kernel(
+    meta, s0, s1, s2, s3, gain, shift, ts, w_ref, t1_in, slots_in, t1v, slots, *, count, per_group, n_blocks, own,
+):
+    frames, lines, half, _ = slots.shape
+    n_out = t1v.shape[0]
+    scale, move = half_affine((s0, s1, s2, s3), frames, gain[...], shift[...], count, per_group)
+    norm = time1_line(ts, slots, meta, scale, move, n_blocks, own)
+    ends = (0, lines - 1)
+    ahead = Ahead([(k + 2 - t, r) for t in range(3) for k in range(n_out) for r in ends], norm)
+    places = [(k, first) for k in range(n_out) for first in (0, lines - 3)]
+    acc = None
+    for t in range(3):
+        ahead.need([(k + 2 - t, r) for k in range(n_out) for r in ends])
+        for i in range(3):
+            lhs = jnp.concatenate([slots[k + 2 - t, first + i] for k, first in places], axis=0)
+            part = jnp.dot(lhs, pair_weights(w_ref, 3 * t + i), preferred_element_type=F32)
+            acc = part if acc is None else acc + part
+        ahead.more(2)
+    for at, (k, first) in enumerate(places):
+        t1v[k, first] = acc[at * half : (at + 1) * half]
+
+
 def time1(meta, stats, gain, shift, t0, weight, n_blocks, own, half, n_frames, n_out):
     channels = gain.shape[0]
-    count = float(n_blocks * own * 2 * half * (channels // GROUPS))
     lines = own + 4
-    return pl.pallas_call(
-        functools.partial(
-            time1_kernel, count=count, per_group=channels // GROUPS, n_blocks=n_blocks, own=own, n_out=n_out
-        ),
-        out_shape=(
-            pltpu.VMEM((n_out, lines - 2, half, 2 * channels), F32),
-            jax.ShapeDtypeStruct((-(-2 * n_out // 8) * 8, channels), F32),
-        ),
+    settings = dict(
+        count=float(n_blocks * own * 2 * half * (channels // GROUPS)),
+        per_group=channels // GROUPS,
+        n_blocks=n_blocks,
+        own=own,
+    )
+    t1_type = pltpu.VMEM((n_out, lines - 2, half, 2 * channels), F32)
+    slots_type = pltpu.VMEM((n_frames, lines, half, 4 * channels), BF16)
+    operands = (meta, *stats, gain.reshape(1, channels), shift.reshape(1, channels), t0,
+                weight.reshape(9, 3, channels, channels))
+    t1, slots, sums = pl.pallas_call(
+        functools.partial(time1_kernel, n_out=n_out, **settings),
+        out_shape=(t1_type, slots_type, jax.ShapeDtypeStruct((-(-2 * n_out // 8) * 8, channels), F32)),
         in_specs=[SMEM] + [VMEM] * 8,
-        out_specs=(VMEM, VMEM),
-        scratch_shapes=[
-            pltpu.VMEM((n_frames, lines, half, 4 * channels), BF16),
-        ],
+        out_specs=(VMEM, VMEM, VMEM),
         compiler_params=params(26),
         cost_estimate=cost(30e9),
         name="time1",
-    )(meta, *stats, gain.reshape(1, channels), shift.reshape(1, channels), t0,
-      weight.reshape(9, 3, channels, channels))
+    )(*operands)
+
+    def outer_lines():
+        return pl.pallas_call(
+            functools.partial(time1_edge_kernel, **settings),
+            out_shape=(t1_type, slots_type),
+            in_specs=[SMEM] + [VMEM] * 10,
+            out_specs=(VMEM, VMEM),
+            input_output_aliases={9: 0, 10: 1},
+            compiler_params=params(26),
+            cost_estimate=cost(8e9),
+            name="time1_edge",
+        )(*operands, t1, slots)[0]
+
+    return sums, outer_lines
 
 
 def time2_kernel(
@@ -654,11 +690,22 @@
     return lax.ppermute(block, axis, [(i, (i + distance) % count) for i in range(count)])
 
 
+def swapped(block, first):
+    count = lax.axis_size("rows")
+    route = {i: i for i in range(count)}
+    for i in range(first, count - 1, 2):
+        route[i], route[i + 1] = i + 1, i
+    return lax.ppermute(block, "rows", list(route.items()))
+
+
 def from_all(block):
-    return [block] + [turned(block, "rows", d) for d in range(1, lax.axis_size("rows"))]
-
-
-def body(
+    parts = [block]
+    for distance in range(1, lax.axis_size("rows")):
+        parts.append(turned(block, "rows", distance))
+    return parts
+
+
+def window(
     video, norm1_gain, norm1_shift, conv1_weight, conv1_bias, norm2_gain, norm2_shift, conv2_weight, conv2_bias,
     out_gain, out_shift, out_weight, out_bias, quant_weight, quant_bias, time_in_weight, time_in_bias,
     tnorm1_gain, tnorm1_shift, time1_weight, tnorm2_gain, tnorm2_shift, time2_weight, time2_bias,
@@ -668,12 +715,16 @@
     half = width // 2
     n_blocks = lax.axis_size("rows")
     meta = jnp.stack([lax.axis_index("rows"), lax.axis_index("frames")]).astype(jnp.int32)
-    x, top, bottom, sums = input_sums(x, 2)
+    channels = x.shape[2]
+    weight = conv1_weight.reshape(3, 3 * channels, channels)
+    x, near, far, sums = input_sums(meta, x, 2)
     stats = from_all(sums)
-    up = turned(bottom, "rows", 1)
-    low = turned(top, "rows", -1)
-    h, xp, sums = conv1(meta, stats, norm1_gain, norm1_shift, conv1_bias, x, up, low, conv1_weight, n_blocks)
-    y, sums = conv2(meta, from_all(sums), norm2_gain, norm2_shift, conv2_bias, h, xp, conv2_weight, n_blocks)
+    far = swapped(far, 1)
+    near = swapped(near, 0)
+    xp, sums, outer_lines = conv1(meta, stats, norm1_gain, norm1_shift, conv1_bias, x, (near, far), weight, n_blocks)
+    stats = from_all(sums)
+    h = outer_lines()
+    y, sums = conv2(meta, stats, norm2_gain, norm2_shift, conv2_bias, h, xp, conv2_weight, n_blocks)
     part, to_up, to_low = head(
         meta, from_all(sums), out_gain, out_shift, y, out_weight, out_bias, quant_weight, quant_bias, n_blocks, 4
     )
@@ -691,13 +742,15 @@
     n_frames = lax.axis_size("frames")
     latents = lax.all_to_all(jnp.broadcast_to(latent[None], (n_frames,) + latent.shape), "frames", 0, 0)
     t0, sums = lift(meta, time_in_weight, time_in_bias, latents, own, half, 7, 5)
-    t1, sums = time1(meta, from_all(sums), tnorm1_gain, tnorm1_shift, t0, time1_weight, n_blocks, own, half, 5, 3)
-    return time2(meta, from_all(sums), tnorm2_gain, tnorm2_shift, time2_bias, t1, t0, time2_weight, n_blocks)
+    sums, outer_lines = time1(meta, from_all(sums), tnorm1_gain, tnorm1_shift, t0, time1_weight, n_blocks, own, half, 5, 3)
+    stats = from_all(sums)
+    t1 = outer_lines()
+    return time2(meta, stats, tnorm2_gain, tnorm2_shift, time2_bias, t1, t0, time2_weight, n_blocks)
 
 
 def solution(mesh):
     return jax.shard_map(
-        body,
+        window,
         mesh=mesh,
         in_specs=(P("frames", "rows", None, None),) + (P(),) * 23,
         out_specs=P("frames", "rows", None, None),

time: 77.4 us -> 74.5 us (0.963)
  starting transfers between devices: 17.8 us -> 14.4 us
  waiting for transfers between devices: 9.44 us -> 10.4 us
    ppermute x19 -> x17, starting transfers between devices: 17.8 us -> 12.4 us  [turned(): lax.ppermute(block, axis, [(i, (i + distance) % count) for i in range(cou...]
    ppermute x0 -> x2, starting transfers between devices: none -> 2.02 us  [swapped(): return lax.ppermute(block, 'rows', list(route.items()))]
    ppermute x19 -> x17, waiting for transfers between devices: 9.44 us -> 10.4 us  [turned(): lax.ppermute(block, axis, [(i, (i + distance) % count) for i in range(cou...]
    pallas_call x1, Pallas kernels: 1.6 us -> 2.38 us  [input_sums(): pl.pallas_call(input_sums_kernel, out_shape=(pltpu.VMEM(x.shape, BF16), e...]
    pallas_call x3 -> x5, Pallas kernels: 18.3 us -> 17.5 us  [the longest x1 5.74 us: time1(): pl.pallas_call(functools.partial(time1_kernel, n_out=n_out, **settings),...]
  transfers between devices with their start and end apart: 19 -> 19, of which waited for: 11 -> 9; matrix products, arithmetic and copies ran while one was open for 0% -> 0% of each run, Pallas kernels for 9% -> 13%
where the time goes in v3:
time: 74.5 us; the launch traced here: 74.3 us
  Pallas kernels  35.1 us (47%)
  starting transfers between devices  14.4 us (19%)
  blocking collectives  13.8 us (19%)
  waiting for transfers between devices  10.4 us (14%)
    all_to_all x1, blocking collectives, window(): lax.all_to_all(jnp.broadcast_to(latent[None], (n_frames,) + latent.shape)...  13.8 us
    ppermute x17, starting transfers between devices, turned(): lax.ppermute(block, axis, [(i, (i + distance) % count) for i in range(cou...  12.4 us
    ppermute x17, waiting for transfers between devices, turned(): lax.ppermute(block, axis, [(i, (i + distance) % count) for i in range(cou...  10.4 us
    pallas_call x1, Pallas kernels, conv2(): pl.pallas_call(functools.partial(conv2_kernel, count=count, per_group=cha...  7.27 us
    pallas_call x1, Pallas kernels, time1(): pl.pallas_call(functools.partial(time1_kernel, n_out=n_out, **settings),...  5.74 us
    pallas_call x1, Pallas kernels, conv1(): pl.pallas_call(functools.partial(conv1_kernel, halo=halo, **settings), ou...  5.3 us
    pallas_call x2, Pallas kernels, edge(): pl.pallas_call(functools.partial(conv1_edge_kernel, distance=distance, n_...  4.56 us
    pallas_call x1, Pallas kernels, time2(): pl.pallas_call(functools.partial(time2_kernel, count=count, per_group=cha...  3.35 us
  transfers between devices with their start and end apart: 19, of which 9 were waited for; matrix products, arithmetic and copies ran while one was open for 0% of the time, Pallas kernels for 13%

profile of v3, /device:TPU:0, one launch (start us, length us, event | category | flops | bytes accessed | tf_op | source)
XLA Modules:
  0.0 74.3 jit_solution(14016472435405508461)
XLA Ops:
  0.0 0.1 pad_add_fusion.meta
  0.1 2.4 %input_sums.1 = (bf16[8,160,512]{2,1,0:T(8,128)(2,1)S(1)}, bf16[2,160,512]{2,1,0:T(8,128)(2,1)S(1)}, bf16[2,160,512]{2,1,0:T(8,128)(2,1)S(1)}, f32[8,128]{1,0:T(8,128)S(1)}) custom-call(s32[2]{0:T(128)S(1)} %pad_add_fusion.meta, bf16[8,160,512]{2,1,0:T(8,128)(2,1)} %bitcast.60), custom_call_target="tpu_custom_call" | custom-call | flops 6000000000 | tf_op jit(solution)/shard_map/input_sums/pallas_call | solution.py:110
  2.5 2.5 %collective-permute-start.2 = (f32[8,128]{1,0:T(8,128)S(1)}, f32[8,128]{1,0:T(8,128)S(1)}, u32[]{:S(2)}, u32[]{:S(2)}) collective-permute-start(f32[8,128]{1,0:T(8,128)S(1)} %get-tuple-element.28.s0), channel_id=1, source_target_pairs={{0,3},{1,0},{2,1},{3,2},{4,7},{5,4},{6,5},{7,6},{8,11},{9,8},{10,9... | collective-permute-start | bytes 12296 | tf_op jit(solution)/shard_map/ppermute | solution.py:690
  5.0 0.6 collective-permute-start.1
  5.6 0.2 collective-permute-start
  5.8 1.4 %collective-permute-start.3 = (bf16[2,160,512]{2,1,0:T(8,128)(2,1)S(1)}, bf16[2,160,512]{2,1,0:T(8,128)(2,1)S(1)}, u32[]{:S(2)}, u32[]{:S(2)}) collective-permute-start(bf16[2,160,512]{2,1,0:T(8,128)(2,1)S(1)} %get-tuple-element.29), channel_id=1, source_target_pairs={{0,1},{1,0},{2,3},{3,2},{4,5},{5,4},{6,7},{7,6},{8,9},{9,8},{10,11... | collective-permute-start | bytes 983048 | tf_op jit(solution)/shard_map/ppermute | solution.py:698
  7.1 0.7 collective-permute-start.4
  7.8 0.0 collective-permute-done.2.s3
  7.8 0.8 %collective-permute-done.1.s2 = f32[8,128]{1,0:T(8,128)S(1)} collective-permute-done((f32[8,128]{1,0:T(8,128)S(1)}, f32[8,128]{1,0:T(8,128)S(1)}, u32[]{:S(2)}, u32[]{:S(2)}) %collective-permute-start.1) | collective-permute-done | bytes 4128 | tf_op jit(solution)/shard_map/ppermute | solution.py:690
  8.6 0.1 collective-permute-done.s1
  8.7 5.3 %conv1.1 = (f32[10,2,80,512]{3,2,1,0:T(8,128)S(1)}, bf16[8,2,80,512]{3,2,1,0:T(8,128)(2,1)S(1)}, bf16[12,80,2048]{2,1,0:T(8,128)(2,1)S(1)}, f32[8,128]{1,0:T(8,128)S(1)}) custom-call(f32[8,128]{1,0:T(8,128)S(1)} %get-tuple-element.28.s0, f32[8,128]{1,0:T(8,128)S(1)} %collective-permute-done.s1, f32[8,128]{1,0:T(8,128)S(1)} %collective-permute-done.1.s2, ...), custom_call_target="tpu_custom_call" | custom-call | flops 24999999488 | tf_op jit(solution)/shard_map/conv1/pallas_call | solution.py:253
  14.0 0.0 collective-permute-done.3.near_ref
  14.0 0.0 collective-permute-done.4.far_ref
  14.0 0.0 slice-start
  14.0 2.3 %shard_map.226 = (f32[10,2,80,512]{3,2,1,0:T(8,128)S(1)}, bf16[12,80,2048]{2,1,0:T(8,128)(2,1)S(1)}, f32[8,128]{1,0:T(8,128)S(1)}) custom-call(s32[2]{0:T(128)S(1)} %pad_add_fusion.meta, f32[8,128]{1,0:T(8,128)S(1)} %get-tuple-element.28.s0, f32[8,128]{1,0:T(8,128)S(1)} %collective-permute-done.s1, ...), custom_call_target="tpu_custom_call", output_to_operand_aliasing={{0}: (12, {}), {1}: (13, {})} | custom-call | flops 10000000000 | tf_op jit(solution)/shard_map/pallas_call | solution.py:270
  16.3 0.1 collective-permute-start.7
  16.4 3.1 %collective-permute-start.6 = (f32[8,128]{1,0:T(8,128)S(1)}, f32[8,128]{1,0:T(8,128)S(1)}, u32[]{:S(2)}, u32[]{:S(2)}) collective-permute-start(f32[8,128]{1,0:T(8,128)S(1)} %get-tuple-element.35.s0), channel_id=1, source_target_pairs={{0,2},{1,3},{2,0},{3,1},{4,6},{5,7},{6,4},{7,5},{8,10},{9,11},{10,... | collective-permute-start | bytes 12296 | tf_op jit(solution)/shard_map/ppermute | solution.py:690
  19.5 0.0 collective-permute-start.5
  19.5 0.0 copy-start.10
  19.5 2.3 %shard_map.227 = (f32[10,2,80,512]{3,2,1,0:T(8,128)S(1)}, bf16[12,80,2048]{2,1,0:T(8,128)(2,1)S(1)}) custom-call(s32[2]{0:T(128)S(1)} %pad_add_fusion.meta, f32[8,128]{1,0:T(8,128)S(1)} %get-tuple-element.28.s0, f32[8,128]{1,0:T(8,128)S(1)} %collective-permute-done.s1, ...), custom_call_target="tpu_custom_call", output_to_operand_aliasing={{0}: (12, {}), {1}: (13, {})} | custom-call | flops 10000000000 | tf_op jit(solution)/shard_map/pallas_call | solution.py:270
  21.8 0.0 collective-permute-done.7.s3
  21.8 0.0 collective-permute-done.6.s2
  21.8 0.7 collective-permute-done.5.s1
  22.5 0.0 copy-done.9
  22.5 0.0 copy-done.10
  22.5 0.0 copy-start.3
  22.6 0.0 copy-start.11
  22.6 0.0 copy-start.12
  22.6 0.0 copy-start.13
  22.6 0.0 copy-start.14
  22.6 0.0 copy-start.15
  22.6 7.3 %conv2.1 = (f32[8,2,80,512]{3,2,1,0:T(8,128)S(1)}, f32[8,128]{1,0:T(8,128)S(1)}) custom-call(s32[2]{0:T(128)S(1)} %pad_add_fusion.meta, f32[8,128]{1,0:T(8,128)S(1)} %get-tuple-element.35.s0, f32[8,128]{1,0:T(8,128)S(1)} %collective-permute-done.5.s1, f32[8,128]{1,0:T(8,128)S(1)} %collective-permute-done.6.s2, f32[8,128]{1,0:T(8,128)S(1)} %collective-permute-done.7.s3, ...), custom_call_target="tpu_custom_call" | custom-call | flops 30000001024 | tf_op jit(solution)/shard_map/conv2/pallas_call | solution.py:324
  29.9 1.1 %collective-permute-start.10 = (f32[8,128]{1,0:T(8,128)S(1)}, f32[8,128]{1,0:T(8,128)S(1)}, u32[]{:S(2)}, u32[]{:S(2)}) collective-permute-start(f32[8,128]{1,0:T(8,128)S(1)} %get-tuple-element.40.s0), channel_id=1, source_target_pairs={{0,3},{1,0},{2,1},{3,2},{4,7},{5,4},{6,5},{7,6},{8,11},{9,8},{10,9... | collective-permute-start | bytes 12296 | tf_op jit(solution)/shard_map/ppermute | solution.py:690
  31.0 0.0 collective-permute-start.9
  31.0 0.2 collective-permute-start.8
  31.2 1.1 %collective-permute-done.10.s3 = f32[8,128]{1,0:T(8,128)S(1)} collective-permute-done((f32[8,128]{1,0:T(8,128)S(1)}, f32[8,128]{1,0:T(8,128)S(1)}, u32[]{:S(2)}, u32[]{:S(2)}) %collective-permute-start.10) | collective-permute-done | bytes 4128 | tf_op jit(solution)/shard_map/ppermute | solution.py:690
  32.3 2.3 %collective-permute-done.9.s2 = f32[8,128]{1,0:T(8,128)S(1)} collective-permute-done((f32[8,128]{1,0:T(8,128)S(1)}, f32[8,128]{1,0:T(8,128)S(1)}, u32[]{:S(2)}, u32[]{:S(2)}) %collective-permute-start.9) | collective-permute-done | bytes 4128 | tf_op jit(solution)/shard_map/ppermute | solution.py:690
  34.6 0.0 collective-permute-done.8.s1
  34.7 0.0 copy-start.4
  34.7 0.0 copy-start.16
  34.7 2.3 %head.1 = (f32[4,1664]{1,0:T(4,128)S(1)}, f32[4,640]{1,0:T(4,128)S(1)}, f32[4,640]{1,0:T(4,128)S(1)}) custom-call(s32[2]{0:T(128)S(1)} %pad_add_fusion.meta, f32[8,128]{1,0:T(8,128)S(1)} %get-tuple-element.40.s0, f32[8,128]{1,0:T(8,128)S(1)} %collective-permute-done.8.s1, f32[8,128]{1,0:T(8,128)S(1)} %collective-permute-done.9.s2, ...), custom_call_target="tpu_custom_call" | custom-call | flops 10000000000 | tf_op jit(solution)/shard_map/head/pallas_call | solution.py:410
  37.0 0.1 collective-permute-start.11
  37.1 1.7 %collective-permute-start.12 = (f32[4,640]{1,0:T(4,128)S(1)}, f32[4,640]{1,0:T(4,128)S(1)}, u32[]{:S(2)}, u32[]{:S(2)}) collective-permute-start(f32[4,640]{1,0:T(4,128)S(1)} %get-tuple-element.44), channel_id=1, source_target_pairs={{0,3},{1,0},{2,1},{3,2},{4,7},{5,4},{6,5},{7,6},{8,11},{9,8},{10,9... | collective-permute-start | bytes 30728 | tf_op jit(solution)/shard_map/ppermute | solution.py:690
  38.8 1.4 %collective-permute-done.11 = f32[4,640]{1,0:T(4,128)S(1)} collective-permute-done((f32[4,640]{1,0:T(4,128)S(1)}, f32[4,640]{1,0:T(4,128)S(1)}, u32[]{:S(2)}, u32[]{:S(2)}) %collective-permute-start.11) | collective-permute-done | bytes 10272 | tf_op jit(solution)/shard_map/ppermute | solution.py:690
  40.2 0.0 collective-permute-done.12
  40.2 0.1 fusion.2
  40.4 13.8 %all_to_all.5.latents = bf16[8,4,2304]{2,1,0:T(4,128)(2,1)S(1)} all-to-all(bf16[8,4,2304]{2,1,0:T(4,128)(2,1)S(1)} %broadcast_in_dim.12), channel_id=1, replica_groups=mesh['frames'=8,'rows'=4] {'frames'}, dimensions={0} | all-to-all | bytes 294912 | tf_op jit(solution)/shard_map/all_to_all | solution.py:743
  54.1 0.0 copy-start.18
  54.2 2.2 %lift.1 = (f32[1920,640]{1,0:T(8,128)S(1)}, f32[16,128]{1,0:T(8,128)S(1)}) custom-call(s32[2]{0:T(128)S(1)} %pad_add_fusion.meta, bf16[27,4,128]{2,1,0:T(4,128)(2,1)S(1)} %bitcast.36, f32[1,128]{1,0:T(1,128)S(1)} %bitcast.52, bf16[8,4,2304]{2,1,0:T(4,128)(2,1)S(1)} %all_to_all.5.latents), custom_call_target="tpu_custom_call" | custom-call | flops 8000000000 | tf_op jit(solution)/shard_map/lift/pallas_call | solution.py:469
  56.4 0.1 collective-permute-start.15
  56.5 1.9 %collective-permute-start.14 = (f32[16,128]{1,0:T(8,128)S(1)}, f32[16,128]{1,0:T(8,128)S(1)}, u32[]{:S(2)}, u32[]{:S(2)}) collective-permute-start(f32[16,128]{1,0:T(8,128)S(1)} %get-tuple-element.45.s0), channel_id=1, source_target_pairs={{0,2},{1,3},{2,0},{3,1},{4,6},{5,7},{6,4},{7,5},{8,10},{9,11},{10,... | collective-permute-start | bytes 24584 | tf_op jit(solution)/shard_map/ppermute | solution.py:690
  58.4 0.0 collective-permute-start.13
  58.4 0.0 collective-permute-done.15.s3
  58.4 1.8 %collective-permute-done.14.s2 = f32[16,128]{1,0:T(8,128)S(1)} collective-permute-done((f32[16,128]{1,0:T(8,128)S(1)}, f32[16,128]{1,0:T(8,128)S(1)}, u32[]{:S(2)}, u32[]{:S(2)}) %collective-permute-start.14) | collective-permute-done | bytes 8224 | tf_op jit(solution)/shard_map/ppermute | solution.py:690
  60.2 1.3 %collective-permute-done.13.s1 = f32[16,128]{1,0:T(8,128)S(1)} collective-permute-done((f32[16,128]{1,0:T(8,128)S(1)}, f32[16,128]{1,0:T(8,128)S(1)}, u32[]{:S(2)}, u32[]{:S(2)}) %collective-permute-start.13) | collective-permute-done | bytes 8224 | tf_op jit(solution)/shard_map/ppermute | solution.py:690
  61.4 5.7 %time1.1 = (f32[3,10,80,256]{3,2,1,0:T(8,128)S(1)}, bf16[5,12,80,512]{3,2,1,0:T(8,128)(2,1)S(1)}, f32[8,128]{1,0:T(8,128)S(1)}) custom-call(s32[2]{0:T(128)S(1)} %pad_add_fusion.meta, f32[16,128]{1,0:T(8,128)S(1)} %get-tuple-element.45.s0, f32[16,128]{1,0:T(8,128)S(1)} %collective-permute-done.13.s1, f32[16,128]{1,0:T(8,128)S(1)} %collective-permute-done.14.s2, ...), custom_call_target="tpu_custom_call" | custom-call | flops 30000001024 | tf_op jit(solution)/shard_map/time1/pallas_call | solution.py:608
  67.2 0.1 collective-permute-start.18
  67.3 0.6 collective-permute-start.17
  67.9 0.2 collective-permute-start.16
  68.1 1.9 %time1_edge.1 = (f32[3,10,80,256]{3,2,1,0:T(8,128)S(1)}, bf16[5,12,80,512]{3,2,1,0:T(8,128)(2,1)S(1)}) custom-call(s32[2]{0:T(128)S(1)} %pad_add_fusion.meta, f32[16,128]{1,0:T(8,128)S(1)} %get-tuple-element.45.s0, f32[16,128]{1,0:T(8,128)S(1)} %collective-permute-done.13.s1, ...), custom_call_target="tpu_custom_call", output_to_operand_aliasing={{0}: (9, {}), {1}: (10, {})} | custom-call | flops 8000000000 | tf_op jit(solution)/shard_map/time1_edge/pallas_call | solution.py:619
  70.0 0.0 collective-permute-done.18.s3
  70.0 0.9 %collective-permute-done.17.s2 = f32[8,128]{1,0:T(8,128)S(1)} collective-permute-done((f32[8,128]{1,0:T(8,128)S(1)}, f32[8,128]{1,0:T(8,128)S(1)}, u32[]{:S(2)}, u32[]{:S(2)}) %collective-permute-start.17) | collective-permute-done | bytes 4128 | tf_op jit(solution)/shard_map/ppermute | solution.py:690
  71.0 0.0 collective-permute-done.16.s1
  71.0 3.3 %time2.1 = bf16[1,8,160,128]{3,2,1,0:T(8,128)(2,1)} custom-call(s32[2]{0:T(128)S(1)} %pad_add_fusion.meta, f32[8,128]{1,0:T(8,128)S(1)} %get-tuple-element.47.s0, f32[8,128]{1,0:T(8,128)S(1)} %collective-permute-done.16.s1, f32[8,128]{1,0:T(8,128)S(1)} %collective-permute-done.17.s2, f32[8,128]{1,0:T(8,128)S(1)} %collective-permute-done.18.s3, ...), custom_call_target="tpu_custom_call" | custom-call | flops 12000000000 | tf_op jit(solution)/shard_map/time2/pallas_call | solution.py:672
  (39 shorter events, 0.1 us)
Async XLA Ops:
  0.1 8.6 %copy-start = (bf16[3,3,512,512]{3,2,1,0:T(8,128)(2,1)S(1)}, bf16[3,3,512,512]{3,2,1,0:T(8,128)(2,1)}, u32[]{:S(2)}) copy-start(bf16[3,3,512,512]{3,2,1,0:T(8,128)(2,1)} %param.27) | copy-start | bytes 14155780
  0.1 8.6 %copy-start.5 = (f32[512]{0:T(512)S(1)}, f32[512]{0:T(512)}, u32[]{:S(2)}) copy-start(f32[512]{0:T(512)} %param.25) | copy-start | bytes 6148
  0.1 8.6 %copy-start.6 = (f32[512]{0:T(512)S(1)}, f32[512]{0:T(512)}, u32[]{:S(2)}) copy-start(f32[512]{0:T(512)} %param.26) | copy-start | bytes 6148
  0.1 8.6 %copy-start.7 = (f32[512]{0:T(512)S(1)}, f32[512]{0:T(512)}, u32[]{:S(2)}) copy-start(f32[512]{0:T(512)} %param.28) | copy-start | bytes 6148
  2.5 5.3 %collective-permute-start.2 = (f32[8,128]{1,0:T(8,128)S(1)}, f32[8,128]{1,0:T(8,128)S(1)}, u32[]{:S(2)}, u32[]{:S(2)}) collective-permute-start(f32[8,128]{1,0:T(8,128)S(1)} %get-tuple-element.28.s0), channel_id=1, source_target_pairs={{0,3},{1,0},{2,1},{3,2},{4,7},{5,4},{6,5},{7,6},{8,11},{9,8},{10,9... | collective-permute-start | bytes 12296 | tf_op jit(solution)/shard_map/ppermute | solution.py:690
  5.0 3.6 %collective-permute-start.1 = (f32[8,128]{1,0:T(8,128)S(1)}, f32[8,128]{1,0:T(8,128)S(1)}, u32[]{:S(2)}, u32[]{:S(2)}) collective-permute-start(f32[8,128]{1,0:T(8,128)S(1)} %get-tuple-element.28.s0), channel_id=1, source_target_pairs={{0,2},{1,3},{2,0},{3,1},{4,6},{5,7},{6,4},{7,5},{8,10},{9,11},{10,... | collective-permute-start | bytes 12296 | tf_op jit(solution)/shard_map/ppermute | solution.py:690
  5.6 3.0 %collective-permute-start = (f32[8,128]{1,0:T(8,128)S(1)}, f32[8,128]{1,0:T(8,128)S(1)}, u32[]{:S(2)}, u32[]{:S(2)}) collective-permute-start(f32[8,128]{1,0:T(8,128)S(1)} %get-tuple-element.28.s0), channel_id=1, source_target_pairs={{0,1},{1,2},{2,3},{3,0},{4,5},{5,6},{6,7},{7,4},{8,9},{9,10},{10,1... | collective-permute-start | bytes 12296 | tf_op jit(solution)/shard_map/ppermute | solution.py:690
  5.8 8.2 %collective-permute-start.3 = (bf16[2,160,512]{2,1,0:T(8,128)(2,1)S(1)}, bf16[2,160,512]{2,1,0:T(8,128)(2,1)S(1)}, u32[]{:S(2)}, u32[]{:S(2)}) collective-permute-start(bf16[2,160,512]{2,1,0:T(8,128)(2,1)S(1)} %get-tuple-element.29), channel_id=1, source_target_pairs={{0,1},{1,0},{2,3},{3,2},{4,5},{5,4},{6,7},{7,6},{8,9},{9,8},{10,11... | collective-permute-start | bytes 983048 | tf_op jit(solution)/shard_map/ppermute | solution.py:698
  7.1 6.9 %collective-permute-start.4 = (bf16[2,160,512]{2,1,0:T(8,128)(2,1)S(1)}, bf16[2,160,512]{2,1,0:T(8,128)(2,1)S(1)}, u32[]{:S(2)}, u32[]{:S(2)}) collective-permute-start(bf16[2,160,512]{2,1,0:T(8,128)(2,1)S(1)} %get-tuple-element.30), channel_id=1, source_target_pairs={{0,0},{1,2},{2,1},{3,3},{4,4},{5,6},{6,5},{7,7},{8,8},{9,10},{10,9... | collective-permute-start | bytes 983048 | tf_op jit(solution)/shard_map/ppermute | solution.py:698
  14.0 8.5 %slice-start = ((s8[4718592]{0:T(1024)(128)(4,1)}), s8[4194304]{0:T(1024)(128)(4,1)S(1)}, s32[]{:S(2)}) async-start(s8[4718592]{0:T(1024)(128)(4,1)} %bitcast.29), calls=%async_computation.1 | async-start | bytes 8388608
  16.3 5.5 %collective-permute-start.7 = (f32[8,128]{1,0:T(8,128)S(1)}, f32[8,128]{1,0:T(8,128)S(1)}, u32[]{:S(2)}, u32[]{:S(2)}) collective-permute-start(f32[8,128]{1,0:T(8,128)S(1)} %get-tuple-element.35.s0), channel_id=1, source_target_pairs={{0,3},{1,0},{2,1},{3,2},{4,7},{5,4},{6,5},{7,6},{8,11},{9,8},{10,9... | collective-permute-start | bytes 12296 | tf_op jit(solution)/shard_map/ppermute | solution.py:690
  16.4 5.4 %collective-permute-start.6 = (f32[8,128]{1,0:T(8,128)S(1)}, f32[8,128]{1,0:T(8,128)S(1)}, u32[]{:S(2)}, u32[]{:S(2)}) collective-permute-start(f32[8,128]{1,0:T(8,128)S(1)} %get-tuple-element.35.s0), channel_id=1, source_target_pairs={{0,2},{1,3},{2,0},{3,1},{4,6},{5,7},{6,4},{7,5},{8,10},{9,11},{10,... | collective-permute-start | bytes 12296 | tf_op jit(solution)/shard_map/ppermute | solution.py:690
  19.5 3.0 %collective-permute-start.5 = (f32[8,128]{1,0:T(8,128)S(1)}, f32[8,128]{1,0:T(8,128)S(1)}, u32[]{:S(2)}, u32[]{:S(2)}) collective-permute-start(f32[8,128]{1,0:T(8,128)S(1)} %get-tuple-element.35.s0), channel_id=1, source_target_pairs={{0,1},{1,2},{2,3},{3,0},{4,5},{5,6},{6,7},{7,4},{8,9},{9,10},{10,1... | collective-permute-start | bytes 12296 | tf_op jit(solution)/shard_map/ppermute | solution.py:690
  19.5 3.0 %slice-start.1 = ((s8[4718592]{0:T(1024)(128)(4,1)}), s8[524288]{0:T(1024)(128)(4,1)S(1)}, s32[]{:S(2)}) async-start(s8[4718592]{0:T(1024)(128)(4,1)} %bitcast.29), calls=%async_computation.2 | async-start | bytes 1048576
  19.5 3.0 %copy-start.8 = (f32[512]{0:T(512)S(1)}, f32[512]{0:T(512)}, u32[]{:S(2)}) copy-start(f32[512]{0:T(512)} %param.29) | copy-start | bytes 6148
  19.5 3.0 %copy-start.9 = (f32[512]{0:T(512)S(1)}, f32[512]{0:T(512)}, u32[]{:S(2)}) copy-start(f32[512]{0:T(512)} %param.30) | copy-start | bytes 6148
  19.5 3.0 %copy-start.10 = (f32[512]{0:T(512)S(1)}, f32[512]{0:T(512)}, u32[]{:S(2)}) copy-start(f32[512]{0:T(512)} %param.32) | copy-start | bytes 6148
  22.5 12.1 %copy-start.3 = (bf16[3,3,512,8]{2,3,1,0:T(8,128)(2,1)S(1)}, bf16[3,3,512,8]{2,3,1,0:T(8,128)(2,1)}, u32[]{:S(2)}) copy-start(bf16[3,3,512,8]{2,3,1,0:T(8,128)(2,1)} %param.35) | copy-start | bytes 221188
  22.6 12.1 %copy-start.11 = (f32[512]{0:T(512)S(1)}, f32[512]{0:T(512)}, u32[]{:S(2)}) copy-start(f32[512]{0:T(512)} %param.33) | copy-start | bytes 6148
  22.6 12.1 %copy-start.12 = (f32[512]{0:T(512)S(1)}, f32[512]{0:T(512)}, u32[]{:S(2)}) copy-start(f32[512]{0:T(512)} %param.34) | copy-start | bytes 6148
  22.6 12.1 %copy-start.13 = (f32[8,4]{0,1:T(4,128)S(1)}, f32[8,4]{0,1:T(4,128)}, u32[]{:S(2)}) copy-start(f32[8,4]{0,1:T(4,128)} %param.37) | copy-start | bytes 388
  22.6 12.1 %copy-start.14 = (f32[8]{0:T(128)S(1)}, f32[8]{0:T(128)}, u32[]{:S(2)}) copy-start(f32[8]{0:T(128)} %b_ref.1) | copy-start | bytes 100
  22.6 12.1 %copy-start.15 = (f32[4]{0:T(128)S(1)}, f32[4]{0:T(128)}, u32[]{:S(2)}) copy-start(f32[4]{0:T(128)} %qb_ref.1) | copy-start | bytes 52
  29.9 2.4 %collective-permute-start.10 = (f32[8,128]{1,0:T(8,128)S(1)}, f32[8,128]{1,0:T(8,128)S(1)}, u32[]{:S(2)}, u32[]{:S(2)}) collective-permute-start(f32[8,128]{1,0:T(8,128)S(1)} %get-tuple-element.40.s0), channel_id=1, source_target_pairs={{0,3},{1,0},{2,1},{3,2},{4,7},{5,4},{6,5},{7,6},{8,11},{9,8},{10,9... | collective-permute-start | bytes 12296 | tf_op jit(solution)/shard_map/ppermute | solution.py:690
  31.0 3.6 %collective-permute-start.9 = (f32[8,128]{1,0:T(8,128)S(1)}, f32[8,128]{1,0:T(8,128)S(1)}, u32[]{:S(2)}, u32[]{:S(2)}) collective-permute-start(f32[8,128]{1,0:T(8,128)S(1)} %get-tuple-element.40.s0), channel_id=1, source_target_pairs={{0,2},{1,3},{2,0},{3,1},{4,6},{5,7},{6,4},{7,5},{8,10},{9,11},{10,... | collective-permute-start | bytes 12296 | tf_op jit(solution)/shard_map/ppermute | solution.py:690
  31.0 3.6 %collective-permute-start.8 = (f32[8,128]{1,0:T(8,128)S(1)}, f32[8,128]{1,0:T(8,128)S(1)}, u32[]{:S(2)}, u32[]{:S(2)}) collective-permute-start(f32[8,128]{1,0:T(8,128)S(1)} %get-tuple-element.40.s0), channel_id=1, source_target_pairs={{0,1},{1,2},{2,3},{3,0},{4,5},{5,6},{6,7},{7,4},{8,9},{9,10},{10,1... | collective-permute-start | bytes 12296 | tf_op jit(solution)/shard_map/ppermute | solution.py:690
  34.7 19.5 %copy-start.4 = (bf16[3,3,3,4,128]{4,3,2,1,0:T(4,128)(2,1)S(1)}, bf16[3,3,3,4,128]{4,3,2,1,0:T(4,128)(2,1)}, u32[]{:S(2)}) copy-start(bf16[3,3,3,4,128]{4,3,2,1,0:T(4,128)(2,1)} %param.39) | copy-start | bytes 82948
  34.7 19.5 %copy-start.16 = (f32[128]{0:T(128)S(1)}, f32[128]{0:T(128)}, u32[]{:S(2)}) copy-start(f32[128]{0:T(128)} %param.40) | copy-start | bytes 1540
  37.0 3.2 %collective-permute-start.11 = (f32[4,640]{1,0:T(4,128)S(1)}, f32[4,640]{1,0:T(4,128)S(1)}, u32[]{:S(2)}, u32[]{:S(2)}) collective-permute-start(f32[4,640]{1,0:T(4,128)S(1)} %get-tuple-element.43), channel_id=1, source_target_pairs={{0,1},{1,2},{2,3},{3,0},{4,5},{5,6},{6,7},{7,4},{8,9},{9,10},{10,1... | collective-permute-start | bytes 30728 | tf_op jit(solution)/shard_map/ppermute | solution.py:690
  37.1 3.1 %collective-permute-start.12 = (f32[4,640]{1,0:T(4,128)S(1)}, f32[4,640]{1,0:T(4,128)S(1)}, u32[]{:S(2)}, u32[]{:S(2)}) collective-permute-start(f32[4,640]{1,0:T(4,128)S(1)} %get-tuple-element.44), channel_id=1, source_target_pairs={{0,3},{1,0},{2,1},{3,2},{4,7},{5,4},{6,5},{7,6},{8,11},{9,8},{10,9... | collective-permute-start | bytes 30728 | tf_op jit(solution)/shard_map/ppermute | solution.py:690
  54.1 7.3 %copy-start.1 = (bf16[3,3,3,128,128]{4,3,2,1,0:T(8,128)(2,1)S(1)}, bf16[3,3,3,128,128]{4,3,2,1,0:T(8,128)(2,1)}, u32[]{:S(2)}) copy-start(bf16[3,3,3,128,128]{4,3,2,1,0:T(8,128)(2,1)} %param.43) | copy-start | bytes 2654212
  54.1 7.3 %copy-start.17 = (f32[128]{0:T(128)S(1)}, f32[128]{0:T(128)}, u32[]{:S(2)}) copy-start(f32[128]{0:T(128)} %param.41) | copy-start | bytes 1540
  54.1 7.3 %copy-start.18 = (f32[128]{0:T(128)S(1)}, f32[128]{0:T(128)}, u32[]{:S(2)}) copy-start(f32[128]{0:T(128)} %param.42) | copy-start | bytes 1540
  56.4 2.0 %collective-permute-start.15 = (f32[16,128]{1,0:T(8,128)S(1)}, f32[16,128]{1,0:T(8,128)S(1)}, u32[]{:S(2)}, u32[]{:S(2)}) collective-permute-start(f32[16,128]{1,0:T(8,128)S(1)} %get-tuple-element.45.s0), channel_id=1, source_target_pairs={{0,3},{1,0},{2,1},{3,2},{4,7},{5,4},{6,5},{7,6},{8,11},{9,8},{10,9... | collective-permute-start | bytes 24584 | tf_op jit(solution)/shard_map/ppermute | solution.py:690
  56.5 3.7 %collective-permute-start.14 = (f32[16,128]{1,0:T(8,128)S(1)}, f32[16,128]{1,0:T(8,128)S(1)}, u32[]{:S(2)}, u32[]{:S(2)}) collective-permute-start(f32[16,128]{1,0:T(8,128)S(1)} %get-tuple-element.45.s0), channel_id=1, source_target_pairs={{0,2},{1,3},{2,0},{3,1},{4,6},{5,7},{6,4},{7,5},{8,10},{9,11},{10,... | collective-permute-start | bytes 24584 | tf_op jit(solution)/shard_map/ppermute | solution.py:690
  58.4 3.1 %collective-permute-start.13 = (f32[16,128]{1,0:T(8,128)S(1)}, f32[16,128]{1,0:T(8,128)S(1)}, u32[]{:S(2)}, u32[]{:S(2)}) collective-permute-start(f32[16,128]{1,0:T(8,128)S(1)} %get-tuple-element.45.s0), channel_id=1, source_target_pairs={{0,1},{1,2},{2,3},{3,0},{4,5},{5,6},{6,7},{7,4},{8,9},{9,10},{10,1... | collective-permute-start | bytes 24584 | tf_op jit(solution)/shard_map/ppermute | solution.py:690
  67.2 2.8 %collective-permute-start.18 = (f32[8,128]{1,0:T(8,128)S(1)}, f32[8,128]{1,0:T(8,128)S(1)}, u32[]{:S(2)}, u32[]{:S(2)}) collective-permute-start(f32[8,128]{1,0:T(8,128)S(1)} %get-tuple-element.47.s0), channel_id=1, source_target_pairs={{0,3},{1,0},{2,1},{3,2},{4,7},{5,4},{6,5},{7,6},{8,11},{9,8},{10,9... | collective-permute-start | bytes 12296 | tf_op jit(solution)/shard_map/ppermute | solution.py:690
  67.3 3.7 %collective-permute-start.17 = (f32[8,128]{1,0:T(8,128)S(1)}, f32[8,128]{1,0:T(8,128)S(1)}, u32[]{:S(2)}, u32[]{:S(2)}) collective-permute-start(f32[8,128]{1,0:T(8,128)S(1)} %get-tuple-element.47.s0), channel_id=1, source_target_pairs={{0,2},{1,3},{2,0},{3,1},{4,6},{5,7},{6,4},{7,5},{8,10},{9,11},{10,... | collective-permute-start | bytes 12296 | tf_op jit(solution)/shard_map/ppermute | solution.py:690
  67.9 3.1 %collective-permute-start.16 = (f32[8,128]{1,0:T(8,128)S(1)}, f32[8,128]{1,0:T(8,128)S(1)}, u32[]{:S(2)}, u32[]{:S(2)}) collective-permute-start(f32[8,128]{1,0:T(8,128)S(1)} %get-tuple-element.47.s0), channel_id=1, source_target_pairs={{0,1},{1,2},{2,3},{3,0},{4,5},{5,6},{6,7},{7,4},{8,9},{9,10},{10,1... | collective-permute-start | bytes 12296 | tf_op jit(solution)/shard_map/ppermute | solution.py:690
  68.1 2.9 %copy-start.2 = (bf16[3,3,3,128,128]{4,3,2,1,0:T(8,128)(2,1)S(1)}, bf16[3,3,3,128,128]{4,3,2,1,0:T(8,128)(2,1)}, u32[]{:S(2)}) copy-start(bf16[3,3,3,128,128]{4,3,2,1,0:T(8,128)(2,1)} %param.46) | copy-start | bytes 2654212
  68.1 2.9 %copy-start.19 = (f32[128]{0:T(128)S(1)}, f32[128]{0:T(128)}, u32[]{:S(2)}) copy-start(f32[128]{0:T(128)} %param.44) | copy-start | bytes 1540
  68.1 2.9 %copy-start.20 = (f32[128]{0:T(128)S(1)}, f32[128]{0:T(128)}, u32[]{:S(2)}) copy-start(f32[128]{0:T(128)} %param.45) | copy-start | bytes 1540
  68.1 2.9 %copy-start.21 = (f32[128]{0:T(128)S(1)}, f32[128]{0:T(128)}, u32[]{:S(2)}) copy-start(f32[128]{0:T(128)} %param.47) | copy-start | bytes 1540

commit v4 on v3

--- a/solution.py
+++ b/solution.py
@@ -47,7 +47,7 @@
     total = parts[0][...]
     for part in parts[1:]:
         total = total + part[...]
-    total = lane_groups(total, per_group) / count
+    total = lane_groups(total, per_group) * (1.0 / count)
     mean = total[0:rows]
     variance = total[rows : 2 * rows] - mean * mean
     scale = lax.rsqrt(variance + EPS) * gain
@@ -357,14 +357,11 @@
     scale, move = half_affine((s0, s1, s2, s3), channels // LANES, gain[...], shift[...], count, per_group)
     scale, move = as_row(scale), as_row(move)
 
-    def norm(r, _):
+    for r in range(own):
         for parity in range(2):
             for at in range(0, channels, LANES):
                 cols = slice(at, at + LANES)
                 act[r, parity, :, cols] = half_silu(ys[r, parity, :, cols], scale[:, cols], move[:, cols]).astype(BF16)
-        return 0
-
-    lax.fori_loop(0, own, norm, 0)
     flat = act[...].reshape(own * width, channels)
     taps = lax.dot_general(w_ref[...], flat, (((1,), (1,)), ((), ())), preferred_element_type=F32)
     size = part_ref.shape[1]
@@ -699,9 +696,13 @@
 
 
 def from_all(block):
+    count = lax.axis_size("rows")
     parts = [block]
-    for distance in range(1, lax.axis_size("rows")):
-        parts.append(turned(block, "rows", distance))
+    for distance in range(1, count):
+        if count & (count - 1) == 0:
+            parts.append(lax.ppermute(block, "rows", [(i, i ^ distance) for i in range(count)]))
+        else:
+            parts.append(turned(block, "rows", distance))
     return parts
 
 

time: 74.5 us -> 72.3 us (0.970)
  waiting for transfers between devices: 10.4 us -> 7.59 us
    ppermute x0 -> x15, starting transfers between devices: none -> 11.9 us  [from_all(): lax.ppermute(block, 'rows', [(i, i ^ distance) for i in range(count)])]
    ppermute x17 -> x2, starting transfers between devices: 12.4 us -> 1.78 us  [turned(): lax.ppermute(block, axis, [(i, (i + distance) % count) for i in range(cou...]
    ppermute x17 -> x2, waiting for transfers between devices: 10.4 us -> 1.38 us  [turned(): lax.ppermute(block, axis, [(i, (i + distance) % count) for i in range(cou...]
    ppermute x0 -> x15, waiting for transfers between devices: none -> 6.21 us  [from_all(): lax.ppermute(block, 'rows', [(i, i ^ distance) for i in range(count)])]
    ppermute x2, starting transfers between devices: 2.02 us -> 1.14 us  [swapped(): return lax.ppermute(block, 'rows', list(route.items()))]
  transfers between devices with their start and end apart: 19 -> 19, of which waited for: 9 -> 7; matrix products, arithmetic and copies ran while one was open for 0% -> 0% of each run, Pallas kernels for 13% -> 13%
where the time goes in v4:
time: 72.3 us; the launch traced here: 72.1 us
  Pallas kernels  35.1 us (49%)
  starting transfers between devices  14.8 us (20%)
  blocking collectives  13.9 us (19%)
  waiting for transfers between devices  7.59 us (10%)
    all_to_all x1, blocking collectives, window(): lax.all_to_all(jnp.broadcast_to(latent[None], (n_frames,) + latent.shape)...  13.9 us
    ppermute x15, starting transfers between devices, from_all(): lax.ppermute(block, 'rows', [(i, i ^ distance) for i in range(count)])  11.9 us
    pallas_call x1, Pallas kernels, conv2(): pl.pallas_call(functools.partial(conv2_kernel, count=count, per_group=cha...  7.27 us
    ppermute x15, waiting for transfers between devices, from_all(): lax.ppermute(block, 'rows', [(i, i ^ distance) for i in range(count)])  6.21 us
    pallas_call x1, Pallas kernels, time1(): pl.pallas_call(functools.partial(time1_kernel, n_out=n_out, **settings),...  5.74 us
    pallas_call x1, Pallas kernels, conv1(): pl.pallas_call(functools.partial(conv1_kernel, halo=halo, **settings), ou...  5.3 us
    pallas_call x2, Pallas kernels, edge(): pl.pallas_call(functools.partial(conv1_edge_kernel, distance=distance, n_...  4.57 us
    pallas_call x1, Pallas kernels, time2(): pl.pallas_call(functools.partial(time2_kernel, count=count, per_group=cha...  3.34 us
  transfers between devices with their start and end apart: 19, of which 7 were waited for; matrix products, arithmetic and copies ran while one was open for 0% of the time, Pallas kernels for 13%

profile of v4, /device:TPU:0, one launch (start us, length us, event | category | flops | bytes accessed | tf_op | source)
XLA Modules:
  0.0 72.1 jit_solution(6508042544537362521)
XLA Ops:
  0.0 0.1 pad_add_fusion.meta
  0.1 2.4 %input_sums.1 = (bf16[8,160,512]{2,1,0:T(8,128)(2,1)S(1)}, bf16[2,160,512]{2,1,0:T(8,128)(2,1)S(1)}, bf16[2,160,512]{2,1,0:T(8,128)(2,1)S(1)}, f32[8,128]{1,0:T(8,128)S(1)}) custom-call(s32[2]{0:T(128)S(1)} %pad_add_fusion.meta, bf16[8,160,512]{2,1,0:T(8,128)(2,1)} %bitcast.60), custom_call_target="tpu_custom_call" | custom-call | flops 6000000000 | tf_op jit(solution)/shard_map/input_sums/pallas_call | solution.py:110
  2.5 2.5 %collective-permute-start.2 = (f32[8,128]{1,0:T(8,128)S(1)}, f32[8,128]{1,0:T(8,128)S(1)}, u32[]{:S(2)}, u32[]{:S(2)}) collective-permute-start(f32[8,128]{1,0:T(8,128)S(1)} %get-tuple-element.28.s0), channel_id=1, source_target_pairs={{0,3},{1,2},{2,1},{3,0},{4,7},{5,6},{6,5},{7,4},{8,11},{9,10},{10,... | collective-permute-start | bytes 12296 | tf_op jit(solution)/shard_map/ppermute | solution.py:703
  5.0 0.6 collective-permute-start.1
  5.6 0.0 collective-permute-start
  5.7 0.5 collective-permute-start.3
  6.1 0.7 collective-permute-start.4
  6.8 0.0 collective-permute-done.2.s3
  6.8 1.8 %collective-permute-done.1.s2 = f32[8,128]{1,0:T(8,128)S(1)} collective-permute-done((f32[8,128]{1,0:T(8,128)S(1)}, f32[8,128]{1,0:T(8,128)S(1)}, u32[]{:S(2)}, u32[]{:S(2)}) %collective-permute-start.1) | collective-permute-done | bytes 4128 | tf_op jit(solution)/shard_map/ppermute | solution.py:703
  8.6 0.0 collective-permute-done.s1
  8.6 0.0 copy-done.6
  8.6 0.0 copy-done.7
  8.6 5.3 %conv1.1 = (f32[10,2,80,512]{3,2,1,0:T(8,128)S(1)}, bf16[8,2,80,512]{3,2,1,0:T(8,128)(2,1)S(1)}, bf16[12,80,2048]{2,1,0:T(8,128)(2,1)S(1)}, f32[8,128]{1,0:T(8,128)S(1)}) custom-call(f32[8,128]{1,0:T(8,128)S(1)} %get-tuple-element.28.s0, f32[8,128]{1,0:T(8,128)S(1)} %collective-permute-done.s1, f32[8,128]{1,0:T(8,128)S(1)} %collective-permute-done.1.s2, ...), custom_call_target="tpu_custom_call" | custom-call | flops 24999999488 | tf_op jit(solution)/shard_map/conv1/pallas_call | solution.py:253
  13.9 0.0 collective-permute-done.3.near_ref
  13.9 0.0 collective-permute-done.4.far_ref
  13.9 0.0 slice-start
  14.0 2.3 %shard_map.226 = (f32[10,2,80,512]{3,2,1,0:T(8,128)S(1)}, bf16[12,80,2048]{2,1,0:T(8,128)(2,1)S(1)}, f32[8,128]{1,0:T(8,128)S(1)}) custom-call(s32[2]{0:T(128)S(1)} %pad_add_fusion.meta, f32[8,128]{1,0:T(8,128)S(1)} %get-tuple-element.28.s0, f32[8,128]{1,0:T(8,128)S(1)} %collective-permute-done.s1, ...), custom_call_target="tpu_custom_call", output_to_operand_aliasing={{0}: (12, {}), {1}: (13, {})} | custom-call | flops 10000000000 | tf_op jit(solution)/shard_map/pallas_call | solution.py:270
  16.3 0.1 collective-permute-start.7
  16.3 2.6 %collective-permute-start.6 = (f32[8,128]{1,0:T(8,128)S(1)}, f32[8,128]{1,0:T(8,128)S(1)}, u32[]{:S(2)}, u32[]{:S(2)}) collective-permute-start(f32[8,128]{1,0:T(8,128)S(1)} %get-tuple-element.35.s0), channel_id=1, source_target_pairs={{0,2},{1,3},{2,0},{3,1},{4,6},{5,7},{6,4},{7,5},{8,10},{9,11},{10,... | collective-permute-start | bytes 12296 | tf_op jit(solution)/shard_map/ppermute | solution.py:703
  18.9 0.0 collective-permute-start.5
  19.0 0.0 copy-start.10
  19.0 2.3 %shard_map.227 = (f32[10,2,80,512]{3,2,1,0:T(8,128)S(1)}, bf16[12,80,2048]{2,1,0:T(8,128)(2,1)S(1)}) custom-call(s32[2]{0:T(128)S(1)} %pad_add_fusion.meta, f32[8,128]{1,0:T(8,128)S(1)} %get-tuple-element.28.s0, f32[8,128]{1,0:T(8,128)S(1)} %collective-permute-done.s1, ...), custom_call_target="tpu_custom_call", output_to_operand_aliasing={{0}: (12, {}), {1}: (13, {})} | custom-call | flops 10000000000 | tf_op jit(solution)/shard_map/pallas_call | solution.py:270
  21.2 0.0 collective-permute-done.7.s3
  21.3 0.0 collective-permute-done.6.s2
  21.3 0.0 collective-permute-done.5.s1
  21.3 0.0 copy-start.3
  21.4 0.0 copy-start.11
  21.4 0.0 copy-start.12
  21.4 0.0 copy-start.13
  21.4 0.0 copy-start.14
  21.4 0.0 copy-start.15
  21.4 7.3 %conv2.1 = (f32[8,2,80,512]{3,2,1,0:T(8,128)S(1)}, f32[8,128]{1,0:T(8,128)S(1)}) custom-call(s32[2]{0:T(128)S(1)} %pad_add_fusion.meta, f32[8,128]{1,0:T(8,128)S(1)} %get-tuple-element.35.s0, f32[8,128]{1,0:T(8,128)S(1)} %collective-permute-done.5.s1, f32[8,128]{1,0:T(8,128)S(1)} %collective-permute-done.6.s2, f32[8,128]{1,0:T(8,128)S(1)} %collective-permute-done.7.s3, ...), custom_call_target="tpu_custom_call" | custom-call | flops 30000001024 | tf_op jit(solution)/shard_map/conv2/pallas_call | solution.py:324
  28.7 0.8 %collective-permute-start.10 = (f32[8,128]{1,0:T(8,128)S(1)}, f32[8,128]{1,0:T(8,128)S(1)}, u32[]{:S(2)}, u32[]{:S(2)}) collective-permute-start(f32[8,128]{1,0:T(8,128)S(1)} %get-tuple-element.40.s0), channel_id=1, source_target_pairs={{0,3},{1,2},{2,1},{3,0},{4,7},{5,6},{6,5},{7,4},{8,11},{9,10},{10,... | collective-permute-start | bytes 12296 | tf_op jit(solution)/shard_map/ppermute | solution.py:703
  29.5 1.3 %collective-permute-start.9 = (f32[8,128]{1,0:T(8,128)S(1)}, f32[8,128]{1,0:T(8,128)S(1)}, u32[]{:S(2)}, u32[]{:S(2)}) collective-permute-start(f32[8,128]{1,0:T(8,128)S(1)} %get-tuple-element.40.s0), channel_id=1, source_target_pairs={{0,2},{1,3},{2,0},{3,1},{4,6},{5,7},{6,4},{7,5},{8,10},{9,11},{10,... | collective-permute-start | bytes 12296 | tf_op jit(solution)/shard_map/ppermute | solution.py:703
  30.9 0.0 collective-permute-start.8
  30.9 0.9 %collective-permute-done.10.s3 = f32[8,128]{1,0:T(8,128)S(1)} collective-permute-done((f32[8,128]{1,0:T(8,128)S(1)}, f32[8,128]{1,0:T(8,128)S(1)}, u32[]{:S(2)}, u32[]{:S(2)}) %collective-permute-start.10) | collective-permute-done | bytes 4128 | tf_op jit(solution)/shard_map/ppermute | solution.py:703
  31.8 1.3 %collective-permute-done.9.s2 = f32[8,128]{1,0:T(8,128)S(1)} collective-permute-done((f32[8,128]{1,0:T(8,128)S(1)}, f32[8,128]{1,0:T(8,128)S(1)}, u32[]{:S(2)}, u32[]{:S(2)}) %collective-permute-start.9) | collective-permute-done | bytes 4128 | tf_op jit(solution)/shard_map/ppermute | solution.py:703
  33.1 0.0 collective-permute-done.8.s1
  33.2 0.0 copy-start.4
  33.2 0.0 copy-start.16
  33.2 2.3 %head.1 = (f32[4,1664]{1,0:T(4,128)S(1)}, f32[4,640]{1,0:T(4,128)S(1)}, f32[4,640]{1,0:T(4,128)S(1)}) custom-call(s32[2]{0:T(128)S(1)} %pad_add_fusion.meta, f32[8,128]{1,0:T(8,128)S(1)} %get-tuple-element.40.s0, f32[8,128]{1,0:T(8,128)S(1)} %collective-permute-done.8.s1, f32[8,128]{1,0:T(8,128)S(1)} %collective-permute-done.9.s2, ...), custom_call_target="tpu_custom_call" | custom-call | flops 10000000000 | tf_op jit(solution)/shard_map/head/pallas_call | solution.py:407
  35.5 0.1 collective-permute-start.11
  35.6 1.7 %collective-permute-start.12 = (f32[4,640]{1,0:T(4,128)S(1)}, f32[4,640]{1,0:T(4,128)S(1)}, u32[]{:S(2)}, u32[]{:S(2)}) collective-permute-start(f32[4,640]{1,0:T(4,128)S(1)} %get-tuple-element.44), channel_id=1, source_target_pairs={{0,3},{1,0},{2,1},{3,2},{4,7},{5,4},{6,5},{7,6},{8,11},{9,8},{10,9... | collective-permute-start | bytes 30728 | tf_op jit(solution)/shard_map/ppermute | solution.py:687
  37.3 1.4 %collective-permute-done.11 = f32[4,640]{1,0:T(4,128)S(1)} collective-permute-done((f32[4,640]{1,0:T(4,128)S(1)}, f32[4,640]{1,0:T(4,128)S(1)}, u32[]{:S(2)}, u32[]{:S(2)}) %collective-permute-start.11) | collective-permute-done | bytes 10272 | tf_op jit(solution)/shard_map/ppermute | solution.py:687
  38.7 0.0 collective-permute-done.12
  38.7 0.1 fusion.2
  38.8 13.9 %all_to_all.5.latents = bf16[8,4,2304]{2,1,0:T(4,128)(2,1)S(1)} all-to-all(bf16[8,4,2304]{2,1,0:T(4,128)(2,1)S(1)} %broadcast_in_dim.12), channel_id=1, replica_groups=mesh['frames'=8,'rows'=4] {'frames'}, dimensions={0} | all-to-all | bytes 294912 | tf_op jit(solution)/shard_map/all_to_all | solution.py:744
  52.7 0.0 copy-start.18
  52.7 2.2 %lift.1 = (f32[1920,640]{1,0:T(8,128)S(1)}, f32[16,128]{1,0:T(8,128)S(1)}) custom-call(s32[2]{0:T(128)S(1)} %pad_add_fusion.meta, bf16[27,4,128]{2,1,0:T(4,128)(2,1)S(1)} %bitcast.36, f32[1,128]{1,0:T(1,128)S(1)} %bitcast.52, bf16[8,4,2304]{2,1,0:T(4,128)(2,1)S(1)} %all_to_all.5.latents), custom_call_target="tpu_custom_call" | custom-call | flops 8000000000 | tf_op jit(solution)/shard_map/lift/pallas_call | solution.py:466
  55.0 0.1 collective-permute-start.15
  55.0 1.8 %collective-permute-start.14 = (f32[16,128]{1,0:T(8,128)S(1)}, f32[16,128]{1,0:T(8,128)S(1)}, u32[]{:S(2)}, u32[]{:S(2)}) collective-permute-start(f32[16,128]{1,0:T(8,128)S(1)} %get-tuple-element.45.s0), channel_id=1, source_target_pairs={{0,2},{1,3},{2,0},{3,1},{4,6},{5,7},{6,4},{7,5},{8,10},{9,11},{10,... | collective-permute-start | bytes 24584 | tf_op jit(solution)/shard_map/ppermute | solution.py:703
  56.8 0.1 collective-permute-start.13
  56.9 1.2 %collective-permute-done.15.s3 = f32[16,128]{1,0:T(8,128)S(1)} collective-permute-done((f32[16,128]{1,0:T(8,128)S(1)}, f32[16,128]{1,0:T(8,128)S(1)}, u32[]{:S(2)}, u32[]{:S(2)}) %collective-permute-start.15) | collective-permute-done | bytes 8224 | tf_op jit(solution)/shard_map/ppermute | solution.py:703
  58.1 0.7 collective-permute-done.14.s2
  58.8 0.0 collective-permute-done.13.s1
  58.8 5.7 %time1.1 = (f32[3,10,80,256]{3,2,1,0:T(8,128)S(1)}, bf16[5,12,80,512]{3,2,1,0:T(8,128)(2,1)S(1)}, f32[8,128]{1,0:T(8,128)S(1)}) custom-call(s32[2]{0:T(128)S(1)} %pad_add_fusion.meta, f32[16,128]{1,0:T(8,128)S(1)} %get-tuple-element.45.s0, f32[16,128]{1,0:T(8,128)S(1)} %collective-permute-done.13.s1, f32[16,128]{1,0:T(8,128)S(1)} %collective-permute-done.14.s2, ...), custom_call_target="tpu_custom_call" | custom-call | flops 30000001024 | tf_op jit(solution)/shard_map/time1/pallas_call | solution.py:605
  64.5 0.6 collective-permute-start.18
  65.1 1.3 %collective-permute-start.17 = (f32[8,128]{1,0:T(8,128)S(1)}, f32[8,128]{1,0:T(8,128)S(1)}, u32[]{:S(2)}, u32[]{:S(2)}) collective-permute-start(f32[8,128]{1,0:T(8,128)S(1)} %get-tuple-element.47.s0), channel_id=1, source_target_pairs={{0,2},{1,3},{2,0},{3,1},{4,6},{5,7},{6,4},{7,5},{8,10},{9,11},{10,... | collective-permute-start | bytes 12296 | tf_op jit(solution)/shard_map/ppermute | solution.py:703
  66.4 0.1 collective-permute-start.16
  66.5 1.9 %time1_edge.1 = (f32[3,10,80,256]{3,2,1,0:T(8,128)S(1)}, bf16[5,12,80,512]{3,2,1,0:T(8,128)(2,1)S(1)}) custom-call(s32[2]{0:T(128)S(1)} %pad_add_fusion.meta, f32[16,128]{1,0:T(8,128)S(1)} %get-tuple-element.45.s0, f32[16,128]{1,0:T(8,128)S(1)} %collective-permute-done.13.s1, ...), custom_call_target="tpu_custom_call", output_to_operand_aliasing={{0}: (9, {}), {1}: (10, {})} | custom-call | flops 8000000000 | tf_op jit(solution)/shard_map/time1_edge/pallas_call | solution.py:616
  68.4 0.0 collective-permute-done.18.s3
  68.4 0.3 collective-permute-done.17.s2
  68.7 0.0 collective-permute-done.16.s1
  68.8 3.3 %time2.1 = bf16[1,8,160,128]{3,2,1,0:T(8,128)(2,1)} custom-call(s32[2]{0:T(128)S(1)} %pad_add_fusion.meta, f32[8,128]{1,0:T(8,128)S(1)} %get-tuple-element.47.s0, f32[8,128]{1,0:T(8,128)S(1)} %collective-permute-done.16.s1, f32[8,128]{1,0:T(8,128)S(1)} %collective-permute-done.17.s2, f32[8,128]{1,0:T(8,128)S(1)} %collective-permute-done.18.s3, ...), custom_call_target="tpu_custom_call" | custom-call | flops 12000000000 | tf_op jit(solution)/shard_map/time2/pallas_call | solution.py:669
  (39 shorter events, 0.1 us)
Async XLA Ops:
  0.1 8.5 %copy-start = (bf16[3,3,512,512]{3,2,1,0:T(8,128)(2,1)S(1)}, bf16[3,3,512,512]{3,2,1,0:T(8,128)(2,1)}, u32[]{:S(2)}) copy-start(bf16[3,3,512,512]{3,2,1,0:T(8,128)(2,1)} %param.27) | copy-start | bytes 14155780
  0.1 8.5 %copy-start.5 = (f32[512]{0:T(512)S(1)}, f32[512]{0:T(512)}, u32[]{:S(2)}) copy-start(f32[512]{0:T(512)} %param.25) | copy-start | bytes 6148
  0.1 8.5 %copy-start.6 = (f32[512]{0:T(512)S(1)}, f32[512]{0:T(512)}, u32[]{:S(2)}) copy-start(f32[512]{0:T(512)} %param.26) | copy-start | bytes 6148
  0.1 8.5 %copy-start.7 = (f32[512]{0:T(512)S(1)}, f32[512]{0:T(512)}, u32[]{:S(2)}) copy-start(f32[512]{0:T(512)} %param.28) | copy-start | bytes 6148
  2.5 4.3 %collective-permute-start.2 = (f32[8,128]{1,0:T(8,128)S(1)}, f32[8,128]{1,0:T(8,128)S(1)}, u32[]{:S(2)}, u32[]{:S(2)}) collective-permute-start(f32[8,128]{1,0:T(8,128)S(1)} %get-tuple-element.28.s0), channel_id=1, source_target_pairs={{0,3},{1,2},{2,1},{3,0},{4,7},{5,6},{6,5},{7,4},{8,11},{9,10},{10,... | collective-permute-start | bytes 12296 | tf_op jit(solution)/shard_map/ppermute | solution.py:703
  5.0 3.6 %collective-permute-start.1 = (f32[8,128]{1,0:T(8,128)S(1)}, f32[8,128]{1,0:T(8,128)S(1)}, u32[]{:S(2)}, u32[]{:S(2)}) collective-permute-start(f32[8,128]{1,0:T(8,128)S(1)} %get-tuple-element.28.s0), channel_id=1, source_target_pairs={{0,2},{1,3},{2,0},{3,1},{4,6},{5,7},{6,4},{7,5},{8,10},{9,11},{10,... | collective-permute-start | bytes 12296 | tf_op jit(solution)/shard_map/ppermute | solution.py:703
  5.6 3.0 %collective-permute-start = (f32[8,128]{1,0:T(8,128)S(1)}, f32[8,128]{1,0:T(8,128)S(1)}, u32[]{:S(2)}, u32[]{:S(2)}) collective-permute-start(f32[8,128]{1,0:T(8,128)S(1)} %get-tuple-element.28.s0), channel_id=1, source_target_pairs={{0,1},{1,0},{2,3},{3,2},{4,5},{5,4},{6,7},{7,6},{8,9},{9,8},{10,11... | collective-permute-start | bytes 12296 | tf_op jit(solution)/shard_map/ppermute | solution.py:703
  5.7 8.3 %collective-permute-start.3 = (bf16[2,160,512]{2,1,0:T(8,128)(2,1)S(1)}, bf16[2,160,512]{2,1,0:T(8,128)(2,1)S(1)}, u32[]{:S(2)}, u32[]{:S(2)}) collective-permute-start(bf16[2,160,512]{2,1,0:T(8,128)(2,1)S(1)} %get-tuple-element.29), channel_id=1, source_target_pairs={{0,1},{1,0},{2,3},{3,2},{4,5},{5,4},{6,7},{7,6},{8,9},{9,8},{10,11... | collective-permute-start | bytes 983048 | tf_op jit(solution)/shard_map/ppermute | solution.py:695
  6.1 7.8 %collective-permute-start.4 = (bf16[2,160,512]{2,1,0:T(8,128)(2,1)S(1)}, bf16[2,160,512]{2,1,0:T(8,128)(2,1)S(1)}, u32[]{:S(2)}, u32[]{:S(2)}) collective-permute-start(bf16[2,160,512]{2,1,0:T(8,128)(2,1)S(1)} %get-tuple-element.30), channel_id=1, source_target_pairs={{0,0},{1,2},{2,1},{3,3},{4,4},{5,6},{6,5},{7,7},{8,8},{9,10},{10,9... | collective-permute-start | bytes 983048 | tf_op jit(solution)/shard_map/ppermute | solution.py:695
  13.9 7.3 %slice-start = ((s8[4718592]{0:T(1024)(128)(4,1)}), s8[4194304]{0:T(1024)(128)(4,1)S(1)}, s32[]{:S(2)}) async-start(s8[4718592]{0:T(1024)(128)(4,1)} %bitcast.29), calls=%async_computation.1 | async-start | bytes 8388608
  16.3 5.0 %collective-permute-start.7 = (f32[8,128]{1,0:T(8,128)S(1)}, f32[8,128]{1,0:T(8,128)S(1)}, u32[]{:S(2)}, u32[]{:S(2)}) collective-permute-start(f32[8,128]{1,0:T(8,128)S(1)} %get-tuple-element.35.s0), channel_id=1, source_target_pairs={{0,3},{1,2},{2,1},{3,0},{4,7},{5,6},{6,5},{7,4},{8,11},{9,10},{10,... | collective-permute-start | bytes 12296 | tf_op jit(solution)/shard_map/ppermute | solution.py:703
  16.3 4.9 %collective-permute-start.6 = (f32[8,128]{1,0:T(8,128)S(1)}, f32[8,128]{1,0:T(8,128)S(1)}, u32[]{:S(2)}, u32[]{:S(2)}) collective-permute-start(f32[8,128]{1,0:T(8,128)S(1)} %get-tuple-element.35.s0), channel_id=1, source_target_pairs={{0,2},{1,3},{2,0},{3,1},{4,6},{5,7},{6,4},{7,5},{8,10},{9,11},{10,... | collective-permute-start | bytes 12296 | tf_op jit(solution)/shard_map/ppermute | solution.py:703
  18.9 2.3 %collective-permute-start.5 = (f32[8,128]{1,0:T(8,128)S(1)}, f32[8,128]{1,0:T(8,128)S(1)}, u32[]{:S(2)}, u32[]{:S(2)}) collective-permute-start(f32[8,128]{1,0:T(8,128)S(1)} %get-tuple-element.35.s0), channel_id=1, source_target_pairs={{0,1},{1,0},{2,3},{3,2},{4,5},{5,4},{6,7},{7,6},{8,9},{9,8},{10,11... | collective-permute-start | bytes 12296 | tf_op jit(solution)/shard_map/ppermute | solution.py:703
  18.9 2.3 %slice-start.1 = ((s8[4718592]{0:T(1024)(128)(4,1)}), s8[524288]{0:T(1024)(128)(4,1)S(1)}, s32[]{:S(2)}) async-start(s8[4718592]{0:T(1024)(128)(4,1)} %bitcast.29), calls=%async_computation.2 | async-start | bytes 1048576
  18.9 2.4 %copy-start.8 = (f32[512]{0:T(512)S(1)}, f32[512]{0:T(512)}, u32[]{:S(2)}) copy-start(f32[512]{0:T(512)} %param.29) | copy-start | bytes 6148
  19.0 2.4 %copy-start.9 = (f32[512]{0:T(512)S(1)}, f32[512]{0:T(512)}, u32[]{:S(2)}) copy-start(f32[512]{0:T(512)} %param.30) | copy-start | bytes 6148
  19.0 2.4 %copy-start.10 = (f32[512]{0:T(512)S(1)}, f32[512]{0:T(512)}, u32[]{:S(2)}) copy-start(f32[512]{0:T(512)} %param.32) | copy-start | bytes 6148
  21.3 11.8 %copy-start.3 = (bf16[3,3,512,8]{2,3,1,0:T(8,128)(2,1)S(1)}, bf16[3,3,512,8]{2,3,1,0:T(8,128)(2,1)}, u32[]{:S(2)}) copy-start(bf16[3,3,512,8]{2,3,1,0:T(8,128)(2,1)} %param.35) | copy-start | bytes 221188
  21.4 11.8 %copy-start.11 = (f32[512]{0:T(512)S(1)}, f32[512]{0:T(512)}, u32[]{:S(2)}) copy-start(f32[512]{0:T(512)} %param.33) | copy-start | bytes 6148
  21.4 11.8 %copy-start.12 = (f32[512]{0:T(512)S(1)}, f32[512]{0:T(512)}, u32[]{:S(2)}) copy-start(f32[512]{0:T(512)} %param.34) | copy-start | bytes 6148
  21.4 11.8 %copy-start.13 = (f32[8,4]{0,1:T(4,128)S(1)}, f32[8,4]{0,1:T(4,128)}, u32[]{:S(2)}) copy-start(f32[8,4]{0,1:T(4,128)} %param.37) | copy-start | bytes 388
  21.4 11.8 %copy-start.14 = (f32[8]{0:T(128)S(1)}, f32[8]{0:T(128)}, u32[]{:S(2)}) copy-start(f32[8]{0:T(128)} %b_ref.1) | copy-start | bytes 100
  21.4 11.8 %copy-start.15 = (f32[4]{0:T(128)S(1)}, f32[4]{0:T(128)}, u32[]{:S(2)}) copy-start(f32[4]{0:T(128)} %qb_ref.1) | copy-start | bytes 52
  28.7 3.1 %collective-permute-start.10 = (f32[8,128]{1,0:T(8,128)S(1)}, f32[8,128]{1,0:T(8,128)S(1)}, u32[]{:S(2)}, u32[]{:S(2)}) collective-permute-start(f32[8,128]{1,0:T(8,128)S(1)} %get-tuple-element.40.s0), channel_id=1, source_target_pairs={{0,3},{1,2},{2,1},{3,0},{4,7},{5,6},{6,5},{7,4},{8,11},{9,10},{10,... | collective-permute-start | bytes 12296 | tf_op jit(solution)/shard_map/ppermute | solution.py:703
  29.5 3.6 %collective-permute-start.9 = (f32[8,128]{1,0:T(8,128)S(1)}, f32[8,128]{1,0:T(8,128)S(1)}, u32[]{:S(2)}, u32[]{:S(2)}) collective-permute-start(f32[8,128]{1,0:T(8,128)S(1)} %get-tuple-element.40.s0), channel_id=1, source_target_pairs={{0,2},{1,3},{2,0},{3,1},{4,6},{5,7},{6,4},{7,5},{8,10},{9,11},{10,... | collective-permute-start | bytes 12296 | tf_op jit(solution)/shard_map/ppermute | solution.py:703
  30.9 2.3 %collective-permute-start.8 = (f32[8,128]{1,0:T(8,128)S(1)}, f32[8,128]{1,0:T(8,128)S(1)}, u32[]{:S(2)}, u32[]{:S(2)}) collective-permute-start(f32[8,128]{1,0:T(8,128)S(1)} %get-tuple-element.40.s0), channel_id=1, source_target_pairs={{0,1},{1,0},{2,3},{3,2},{4,5},{5,4},{6,7},{7,6},{8,9},{9,8},{10,11... | collective-permute-start | bytes 12296 | tf_op jit(solution)/shard_map/ppermute | solution.py:703
  33.2 19.5 %copy-start.4 = (bf16[3,3,3,4,128]{4,3,2,1,0:T(4,128)(2,1)S(1)}, bf16[3,3,3,4,128]{4,3,2,1,0:T(4,128)(2,1)}, u32[]{:S(2)}) copy-start(bf16[3,3,3,4,128]{4,3,2,1,0:T(4,128)(2,1)} %param.39) | copy-start | bytes 82948
  33.2 19.5 %copy-start.16 = (f32[128]{0:T(128)S(1)}, f32[128]{0:T(128)}, u32[]{:S(2)}) copy-start(f32[128]{0:T(128)} %param.40) | copy-start | bytes 1540
  35.5 3.2 %collective-permute-start.11 = (f32[4,640]{1,0:T(4,128)S(1)}, f32[4,640]{1,0:T(4,128)S(1)}, u32[]{:S(2)}, u32[]{:S(2)}) collective-permute-start(f32[4,640]{1,0:T(4,128)S(1)} %get-tuple-element.43), channel_id=1, source_target_pairs={{0,1},{1,2},{2,3},{3,0},{4,5},{5,6},{6,7},{7,4},{8,9},{9,10},{10,1... | collective-permute-start | bytes 30728 | tf_op jit(solution)/shard_map/ppermute | solution.py:687
  35.6 3.1 %collective-permute-start.12 = (f32[4,640]{1,0:T(4,128)S(1)}, f32[4,640]{1,0:T(4,128)S(1)}, u32[]{:S(2)}, u32[]{:S(2)}) collective-permute-start(f32[4,640]{1,0:T(4,128)S(1)} %get-tuple-element.44), channel_id=1, source_target_pairs={{0,3},{1,0},{2,1},{3,2},{4,7},{5,4},{6,5},{7,6},{8,11},{9,8},{10,9... | collective-permute-start | bytes 30728 | tf_op jit(solution)/shard_map/ppermute | solution.py:687
  52.7 6.0 %copy-start.1 = (bf16[3,3,3,128,128]{4,3,2,1,0:T(8,128)(2,1)S(1)}, bf16[3,3,3,128,128]{4,3,2,1,0:T(8,128)(2,1)}, u32[]{:S(2)}) copy-start(bf16[3,3,3,128,128]{4,3,2,1,0:T(8,128)(2,1)} %param.43) | copy-start | bytes 2654212
  52.7 6.0 %copy-start.17 = (f32[128]{0:T(128)S(1)}, f32[128]{0:T(128)}, u32[]{:S(2)}) copy-start(f32[128]{0:T(128)} %param.41) | copy-start | bytes 1540
  52.7 6.0 %copy-start.18 = (f32[128]{0:T(128)S(1)}, f32[128]{0:T(128)}, u32[]{:S(2)}) copy-start(f32[128]{0:T(128)} %param.42) | copy-start | bytes 1540
  55.0 3.1 %collective-permute-start.15 = (f32[16,128]{1,0:T(8,128)S(1)}, f32[16,128]{1,0:T(8,128)S(1)}, u32[]{:S(2)}, u32[]{:S(2)}) collective-permute-start(f32[16,128]{1,0:T(8,128)S(1)} %get-tuple-element.45.s0), channel_id=1, source_target_pairs={{0,3},{1,2},{2,1},{3,0},{4,7},{5,6},{6,5},{7,4},{8,11},{9,10},{10,... | collective-permute-start | bytes 24584 | tf_op jit(solution)/shard_map/ppermute | solution.py:703
  55.0 3.7 %collective-permute-start.14 = (f32[16,128]{1,0:T(8,128)S(1)}, f32[16,128]{1,0:T(8,128)S(1)}, u32[]{:S(2)}, u32[]{:S(2)}) collective-permute-start(f32[16,128]{1,0:T(8,128)S(1)} %get-tuple-element.45.s0), channel_id=1, source_target_pairs={{0,2},{1,3},{2,0},{3,1},{4,6},{5,7},{6,4},{7,5},{8,10},{9,11},{10,... | collective-permute-start | bytes 24584 | tf_op jit(solution)/shard_map/ppermute | solution.py:703
  56.8 1.9 %collective-permute-start.13 = (f32[16,128]{1,0:T(8,128)S(1)}, f32[16,128]{1,0:T(8,128)S(1)}, u32[]{:S(2)}, u32[]{:S(2)}) collective-permute-start(f32[16,128]{1,0:T(8,128)S(1)} %get-tuple-element.45.s0), channel_id=1, source_target_pairs={{0,1},{1,0},{2,3},{3,2},{4,5},{5,4},{6,7},{7,6},{8,9},{9,8},{10,11... | collective-permute-start | bytes 24584 | tf_op jit(solution)/shard_map/ppermute | solution.py:703
  64.5 3.9 %collective-permute-start.18 = (f32[8,128]{1,0:T(8,128)S(1)}, f32[8,128]{1,0:T(8,128)S(1)}, u32[]{:S(2)}, u32[]{:S(2)}) collective-permute-start(f32[8,128]{1,0:T(8,128)S(1)} %get-tuple-element.47.s0), channel_id=1, source_target_pairs={{0,3},{1,2},{2,1},{3,0},{4,7},{5,6},{6,5},{7,4},{8,11},{9,10},{10,... | collective-permute-start | bytes 12296 | tf_op jit(solution)/shard_map/ppermute | solution.py:703
  65.1 3.6 %collective-permute-start.17 = (f32[8,128]{1,0:T(8,128)S(1)}, f32[8,128]{1,0:T(8,128)S(1)}, u32[]{:S(2)}, u32[]{:S(2)}) collective-permute-start(f32[8,128]{1,0:T(8,128)S(1)} %get-tuple-element.47.s0), channel_id=1, source_target_pairs={{0,2},{1,3},{2,0},{3,1},{4,6},{5,7},{6,4},{7,5},{8,10},{9,11},{10,... | collective-permute-start | bytes 12296 | tf_op jit(solution)/shard_map/ppermute | solution.py:703
  66.4 2.3 %collective-permute-start.16 = (f32[8,128]{1,0:T(8,128)S(1)}, f32[8,128]{1,0:T(8,128)S(1)}, u32[]{:S(2)}, u32[]{:S(2)}) collective-permute-start(f32[8,128]{1,0:T(8,128)S(1)} %get-tuple-element.47.s0), channel_id=1, source_target_pairs={{0,1},{1,0},{2,3},{3,2},{4,5},{5,4},{6,7},{7,6},{8,9},{9,8},{10,11... | collective-permute-start | bytes 12296 | tf_op jit(solution)/shard_map/ppermute | solution.py:703
  66.5 2.3 %copy-start.2 = (bf16[3,3,3,128,128]{4,3,2,1,0:T(8,128)(2,1)S(1)}, bf16[3,3,3,128,128]{4,3,2,1,0:T(8,128)(2,1)}, u32[]{:S(2)}) copy-start(bf16[3,3,3,128,128]{4,3,2,1,0:T(8,128)(2,1)} %param.46) | copy-start | bytes 2654212
  66.5 2.3 %copy-start.19 = (f32[128]{0:T(128)S(1)}, f32[128]{0:T(128)}, u32[]{:S(2)}) copy-start(f32[128]{0:T(128)} %param.44) | copy-start | bytes 1540
  66.5 2.3 %copy-start.20 = (f32[128]{0:T(128)S(1)}, f32[128]{0:T(128)}, u32[]{:S(2)}) copy-start(f32[128]{0:T(128)} %param.45) | copy-start | bytes 1540
  66.5 2.3 %copy-start.21 = (f32[128]{0:T(128)S(1)}, f32[128]{0:T(128)}, u32[]{:S(2)}) copy-start(f32[128]{0:T(128)} %param.47) | copy-start | bytes 1540
